TPU v7x, 512 devices: a whole 4x8x8 slice. The times are simulated.
512 devices in a mesh: dp: 8 (over y_hi, x), expert: 64 (over z, y_lo, core).
Axes of the slice: x: 4, y: 8 (y_hi: 2, y_lo: 4; y = y_hi * 4 + y_lo), z: 8, core: 2. Of those that a mesh axis runs over, the one named last changes fastest.
Arguments:
- tokens: bfloat16 [65536, 1024], P(('dp', 'expert')), may hold values from -6 to 6
- out_grad: bfloat16 [65536, 1024], P(('dp', 'expert')), may hold values from -6 to 6
- expert_ids: int32 [65536, 3], P(('dp', 'expert')), may hold values from 0 to 63, all different within a row; in each aligned block of 128 rows (0 to 127, 128 to 255, ...) at most 7 rows name the same one
- gate_probs: float32 [65536, 3], P(('dp', 'expert')), may hold values from 0.1 to 0.6
- saved_pre: bfloat16 [8, 64, 448, 1536], P('dp', 'expert'), may hold values from -6 to 6
- gate_weight: bfloat16 [64, 1024, 768], P('expert', 'dp'), may hold values from -0.1875 to 0.1875
- up_weight: bfloat16 [64, 1024, 768], P('expert', 'dp'), may hold values from -0.1875 to 0.1875
- down_weight: bfloat16 [64, 1024, 768], P('expert', 'dp'), may hold values from -0.21875 to 0.21875
- basis: bfloat16 [64, 1024, 256], P('expert', 'dp'), may hold values from -0.1875 to 0.1875
Outputs:
- in_grad: bfloat16 [65536, 1024], P(('dp', 'expert'))
- proj_grads: float32 [64, 3, 256, 768], P('expert', None, 'dp')
Inputs may be any that keep to these rules, and one draw needn't show every extreme that they name: `expert_ids`: each token names 3 different experts. The rows of one device name one expert at most 7 times, and on some devices some expert exactly 7 times.
All inputs are finite; a program needn't handle non-finite values.
Results may differ from a plain program's by a relative error of at most 0.0091.
Values may be sent and summed in bfloat16 or wider, within the bound.
No kernel may reach another device: no remote copies, remote signals or barrier semaphores. Data moves between devices by JAX's collectives and lax.ppermute only.
A program may use at most 64 MiB of HBM per device.

v0:
```python
import jax
import jax.numpy as jnp
from jax import lax
from jax.sharding import Mesh
from jax.sharding import PartitionSpec as P

DP = ("dp_0", "dp_1")
DP_EXPERT = ("dp_0", "dp_1", "expert")


def side_by_side(arrays, axis, split_dim, concat_dim, along):
    widths = [a.shape[along] for a in arrays]
    both = jnp.concatenate(arrays, axis=along)
    filled = lax.all_to_all(both, axis, split_axis=split_dim, concat_axis=concat_dim, tiled=True)
    return tuple(jnp.split(filled, [sum(widths[:k]) for k in range(1, len(widths))], axis=along))


def side_by_side_2(arrays, axis, dim, along):
    both = jnp.concatenate(arrays, axis=along)
    filled, at, outs = (lax.all_gather(both, axis, axis=dim, tiled=True), 0, [])
    for a in arrays:
        outs.append(lax.slice_in_dim(filled, at, at + a.shape[along], axis=along))
        at += a.shape[along]
    return tuple(outs)


def sum_in_order(tiles, axes, sequence):
    dims = [lax.axis_size(a) for a in axes]
    tiles = tiles.reshape(*dims, *tiles.shape[1:])
    tiles = tiles.transpose(*sequence, *range(len(axes), tiles.ndim))
    tiles = tiles.reshape(-1, *tiles.shape[len(axes) :])
    for k in sequence:
        tiles = lax.psum_scatter(tiles, axes[k], scatter_dimension=0, tiled=True)
    return tiles[0]


def cut_along(value, dim, peers):
    dims = value.shape
    tiles = value.reshape(*dims[:dim], peers, dims[dim] // peers, *dims[dim + 1 :])
    return jnp.moveaxis(tiles, dim, 0)


def scatter_axes(value, axes, sequence, dim):
    peers = lax.axis_size(axes)
    return sum_in_order(cut_along(value, dim, peers), axes, sequence)


def contract_rows(left, right):
    return lax.dot_general(
        left, right, (((0,), (0,)), ((), ())), preferred_element_type=jnp.float32
    )


def contract_cols(left, right):
    return lax.dot_general(
        left, right, (((1,), (1,)), ((), ())), preferred_element_type=jnp.float32
    )


def body(
    tokens, out_grad, expert_ids, gate_probs, saved_pre, gate_weight, up_weight, down_weight, basis
):
    n_owner = lax.axis_size("expert")
    tok_rows, width = tokens.shape
    topk = expert_ids.shape[1]
    slots = saved_pre.shape[2]
    cap = slots // n_owner
    hidden = gate_weight.shape[2]
    onehot = (expert_ids[:, :, None] == jnp.arange(n_owner, dtype=jnp.int32)[None, None, :]).astype(
        jnp.int32
    )
    per_token = jnp.sum(onehot, axis=1)
    before = jnp.cumsum(per_token, axis=0) - per_token
    position = jnp.sum(onehot * before[:, None, :], axis=2)
    target = expert_ids * cap + position
    token_index = jnp.broadcast_to(jnp.arange(tok_rows, dtype=jnp.int32)[:, None], target.shape)
    choice_index = jnp.broadcast_to(jnp.arange(topk, dtype=jnp.int32)[None, :], target.shape)
    fill_token = (
        jnp.full((n_owner * cap,), -1, jnp.int32)
        .at[target.reshape(-1)]
        .set(token_index.reshape(-1))
    )
    fill_choice = (
        jnp.zeros((n_owner * cap,), jnp.int32).at[target.reshape(-1)].set(choice_index.reshape(-1))
    )
    filled = fill_token >= 0
    picked = jnp.maximum(fill_token, 0)
    send_rows = jnp.where(filled[:, None], tokens[picked], jnp.zeros((), jnp.bfloat16))
    weight_pick = gate_probs[picked, fill_choice]
    scaled = (out_grad[picked].astype(jnp.float32) * weight_pick[:, None]).astype(jnp.bfloat16)
    send_grad = jnp.where(filled[:, None], scaled, jnp.zeros((), jnp.bfloat16))
    arrived_rows, arrived_grad = side_by_side(
        (send_rows.reshape(n_owner, cap, width), send_grad.reshape(n_owner, cap, width)),
        "expert",
        0,
        0,
        1,
    )
    rows_in = arrived_rows.reshape(slots, width)
    grad_in = arrived_grad.reshape(slots, width)
    full_down, full_basis, full_gate, full_up = side_by_side_2(
        (down_weight, basis, gate_weight, up_weight), DP, 1, 2
    )
    pieces = (full_down, full_basis)
    down_piece = pieces[0][0]
    basis_piece = pieces[1][0]
    hidden_grad = jnp.dot(grad_in, down_piece, preferred_element_type=jnp.float32)
    x_acc = jnp.dot(rows_in, basis_piece, preferred_element_type=jnp.float32)
    dy_acc = jnp.dot(grad_in, basis_piece, preferred_element_type=jnp.float32)
    hidden_grad, x_acc, dy_acc = (hidden_grad, x_acc, dy_acc)
    pre = saved_pre[0, 0].astype(jnp.float32)
    gate_pre = pre[:, :hidden]
    up_pre = pre[:, hidden:]
    sig = jax.nn.sigmoid(gate_pre)
    hid = (gate_pre * sig * up_pre).astype(jnp.bfloat16)
    up_grad = (hidden_grad * gate_pre * sig).astype(jnp.bfloat16)
    gate_grad = (hidden_grad * up_pre * sig * (1.0 + gate_pre * (1.0 - sig))).astype(jnp.bfloat16)
    x_proj = x_acc.astype(jnp.bfloat16)
    dy_proj = dy_acc.astype(jnp.bfloat16)
    pieces = (full_gate, full_up)
    row_grad = contract_cols(gate_grad, pieces[0][0]) + contract_cols(up_grad, pieces[1][0])
    terms = jnp.stack(
        [
            contract_rows(x_proj, gate_grad),
            contract_rows(x_proj, up_grad),
            contract_rows(dy_proj, hid),
        ]
    )
    proj_grads = scatter_axes(terms[None].astype(jnp.bfloat16), DP, (1, 0), 2).astype(jnp.float32)
    returned = lax.all_to_all(
        row_grad.astype(jnp.bfloat16).reshape(n_owner, cap, width),
        "expert",
        split_axis=0,
        concat_axis=0,
        tiled=True,
    )
    returned = returned.reshape(n_owner * cap, width)
    in_grad = jnp.sum(returned[target].astype(jnp.float32), axis=1).astype(jnp.bfloat16)
    return (in_grad, proj_grads)


def solution(mesh):
    finer = Mesh(mesh.devices.reshape(2, 4, mesh.shape["expert"]), ("dp_0", "dp_1", "expert"))
    placed = (
        P(DP_EXPERT, None),
        P(DP_EXPERT, None),
        P(DP_EXPERT, None),
        P(DP_EXPERT, None),
        P(DP, "expert", None, None),
        P("expert", DP, None),
        P("expert", DP, None),
        P("expert", DP, None),
        P("expert", DP, None),
    )
    return jax.shard_map(
        body,
        mesh=finer,
        in_specs=placed,
        out_specs=(P(DP_EXPERT, None), P("expert", None, DP, None)),
        check_vma=False,
    )
```

profile of v0, /device:TPU:9, one launch (start us, length us, event | category | flops | bytes accessed | tf_op | source)
XLA Modules:
  0.0 236.9 jit_solution(16643770522436022008)
XLA Ops:
  7.2 2.1 pad_maximum_fusion.2
  10.6 2.9 %scatter_custom_fusion.1 = s32[448]{0:T(512)S(1)} fusion(s32[384]{0:T(512)S(1)} %fusion.7, s32[384]{0:T(512)S(1)} %reshape.218, s32[]{:T(128)} %constant.9.clone.1), kind=kCustom, calls=%fused_computation.44 | custom fusion | bytes 1796 | tf_op jit(solution)/shard_map/scatter | solution.py:84
  13.5 2.9 %scatter_custom_fusion = s32[448]{0:T(512)S(1)} fusion(s32[384]{0:T(512)S(1)} %fusion.7, s32[384]{0:T(512)S(1)} %reshape.210, s32[]{:T(128)} %constant.7.clone.1), kind=kCustom, calls=%fused_computation.48 | custom fusion | bytes 1796 | tf_op jit(solution)/shard_map/scatter | solution.py:81
  16.6 4.0 %gather_fusion.2 = f32[448]{0:T(512)S(1)} fusion(f32[128,3]{0,1:T(4,128)S(1)} %copy-done.1, s32[448]{0:T(512)S(1)} %get-tuple-element.10), kind=kCustom, calls=%fused_computation.2 | custom fusion | bytes 7168 | tf_op jit(solution)/shard_map/gather | solution.py:89
  20.8 2.7 %gather_fusion.1 = bf16[448,1024]{1,0:T(8,128)(2,1)} fusion(bf16[128,1024]{1,0:T(8,128)(2,1)S(1)} %copy-done, s32[1024]{0:T(1024)S(1)} %pad_clamp_fusion.1), kind=kCustom, calls=%fused_computation.1 | custom fusion | bytes 1836800 | tf_op jit(solution)/shard_map/gather | solution.py:90
  23.5 2.1 gather_fusion
  27.6 2.2 pad_maximum_fusion
  29.8 14.7 %all-to-all-start = ((bf16[64,14,1024]{2,1,0:T(8,128)(2,1)}), bf16[64,14,1024]{2,1,0:T(8,128)(2,1)S(1)}, u32[]{:S(2)}, u32[]{:S(2)}) async-start(bf16[64,14,1024]{2,1,0:T(8,128)(2,1)} %pad_maximum_fusion), calls=%async_computation | async-start | bytes 4194304 | tf_op jit(solution)/shard_map/all_to_all | solution.py:14
  44.7 3.2 %bitcast_convert_fusion = f32[448,1536]{1,0:T(8,128)} fusion(bf16[1,1,448,1536]{3,2,1,0:T(8,128)(2,1)} %param.13), kind=kLoop, calls=%fused_computation.15 | loop fusion | flops 688128 | bytes 4128768 | tf_op jit(solution)/shard_map/convert_element_type | solution.py:111
  47.9 107.0 %all-to-all-done = bf16[64,14,1024]{2,1,0:T(8,128)(2,1)S(1)} async-done(((bf16[64,14,1024]{2,1,0:T(8,128)(2,1)}), bf16[64,14,1024]{2,1,0:T(8,128)(2,1)S(1)}, u32[]{:S(2)}, u32[]{:S(2)}) %all-to-all-start) | async-done | bytes 1835040 | tf_op jit(solution)/shard_map/all_to_all | solution.py:14
  154.9 1.6 fusion.13
  156.5 1.4 reshape.170
  159.3 1.5 convolution_convert_fusion.4
  160.9 3.5 %multiply_convert_fusion.3 = (bf16[448,768]{1,0:T(8,128)(2,1)S(1)}, bf16[448,768]{1,0:T(8,128)(2,1)S(1)}) fusion(f32[448,1536]{1,0:T(8,128)} %bitcast_convert_fusion, bf16[448,1024]{1,0:T(8,128)(2,1)S(1)} %copy-done.4, bf16[1,1024,2560]{2,1,0:T(8,128)(2,1)} %all-gather.2.cloned.1.call-done), kind=kOutput, calls=%fused_computation.18 | convolution fusion | flops 709115904 | bytes 6619136 | tf_op jit(solution)/shard_map/dot_general | solution.py:107
  166.9 3.2 %convolution_convert_fusion = bf16[256,768]{1,0:T(8,128)(2,1)} fusion(bf16[448,1024]{1,0:T(8,128)(2,1)} %reshape.167, f32[448,1536]{1,0:T(8,128)S(1)} %copy-done.3, bf16[1,1024,2560]{2,1,0:T(8,128)(2,1)} %all-gather.2.cloned.1.call-done), kind=kOutput, calls=%fused_computation.20 | convolution fusion | flops 413417472 | bytes 4587520 | tf_op jit(solution)/shard_map/dot_general | solution.py:49
  172.7 2.4 %fusion = f32[448,1024]{1,0:T(8,128)S(1)} fusion(bf16[448,768]{1,0:T(8,128)(2,1)S(1)} %copy-done.8, bf16[1,1024,2560]{2,1,0:T(8,128)(2,1)} %all-gather.2.cloned.1.call-done), kind=kOutput, calls=%fused_computation.10 | convolution fusion | flops 704643072 | bytes 4096000 | tf_op jit(solution)/shard_map/dot_general | solution.py:55
  175.0 2.3 add_convert_fusion
  178.6 6.5 %all-to-all-start.1 = ((bf16[64,7,1024]{2,1,0:T(8,128)(2,1)}), bf16[64,7,1024]{2,1,0:T(8,128)(2,1)S(1)}, u32[]{:S(2)}, u32[]{:S(2)}) async-start(bf16[64,7,1024]{2,1,0:T(8,128)(2,1)} %reshape.168), calls=%async_computation.1 | async-start | bytes 2097152 | tf_op jit(solution)/shard_map/all_to_all | solution.py:130
  185.2 13.1 %reduce-scatter.3.cloned.1.call-done = bf16[2,1,3,32,768]{4,3,2,1,0:T(8,128)(2,1)} async-done(((bf16[8,1,3,32,768]{4,3,2,1,0:T(8,128)(2,1)}), bf16[2,1,3,32,768]{4,3,2,1,0:T(8,128)(2,1)}) %reduce-scatter.3.cloned.1.call-update) | async-done | bytes 294928 | tf_op jit(solution)/shard_map/reduce_scatter | solution.py:33
  198.6 15.8 %all-to-all-done.1 = bf16[64,7,1024]{2,1,0:T(8,128)(2,1)S(1)} async-done(((bf16[64,7,1024]{2,1,0:T(8,128)(2,1)}), bf16[64,7,1024]{2,1,0:T(8,128)(2,1)S(1)}, u32[]{:S(2)}, u32[]{:S(2)}) %all-to-all-start.1) | async-done | bytes 917536 | tf_op jit(solution)/shard_map/all_to_all | solution.py:130
  214.7 2.1 gather_fusion.3
  217.3 2.1 reduce_sum.32
  219.4 9.3 %reduce-scatter.5.cloned.1.call-done = bf16[1,1,3,32,768]{4,3,2,1,0:T(8,128)(2,1)} async-done(((bf16[2,1,3,32,768]{4,3,2,1,0:T(8,128)(2,1)}), bf16[1,1,3,32,768]{4,3,2,1,0:T(8,128)(2,1)}) %reduce-scatter.5.cloned.1.call-update) | async-done | bytes 147472 | tf_op jit(solution)/shard_map/reduce_scatter | solution.py:33
  228.7 1.6 bitcast_convert_fusion.1
  (60 shorter events, 12.5 us)
Async XLA Ops:
  7.2 13.6 %copy-start = (bf16[128,1024]{1,0:T(8,128)(2,1)S(1)}, bf16[128,1024]{1,0:T(8,128)(2,1)}, u32[]{:S(2)}) copy-start(bf16[128,1024]{1,0:T(8,128)(2,1)} %param.10) | copy-start | bytes 786436
  7.2 2.2 copy-start.9
  7.2 9.4 %copy-start.1 = (f32[128,3]{0,1:T(4,128)S(1)}, f32[128,3]{0,1:T(4,128)}, u32[]{:S(2)}) copy-start(f32[128,3]{0,1:T(4,128)} %param.12) | copy-start | bytes 4612
  7.2 152.1 %all-gather.2.cloned.1.call-start = ((), (), s32[]{:S(2)}) async-start(), calls=%async_computation.4 | async-start | bytes 5898240 | tf_op jit(solution)/shard_map/all_gather | solution.py:20
  20.8 2.7 %copy-start.2 = (bf16[128,1024]{1,0:T(8,128)(2,1)S(1)}, bf16[128,1024]{1,0:T(8,128)(2,1)}, u32[]{:S(2)}) copy-start(bf16[128,1024]{1,0:T(8,128)(2,1)} %param.9) | copy-start | bytes 786436
  29.8 125.1 %all-to-all-start = ((bf16[64,14,1024]{2,1,0:T(8,128)(2,1)}), bf16[64,14,1024]{2,1,0:T(8,128)(2,1)S(1)}, u32[]{:S(2)}, u32[]{:S(2)}) async-start(bf16[64,14,1024]{2,1,0:T(8,128)(2,1)} %pad_maximum_fusion), calls=%async_computation | async-start | bytes 4194304 | tf_op jit(solution)/shard_map/all_to_all | solution.py:14
  44.5 153.8 %reduce-scatter.3.cloned.1.call-start = ((), (), s32[]{:S(2)}) async-start(), calls=%async_computation.5 | async-start | bytes 1474560 | tf_op jit(solution)/shard_map/reduce_scatter | solution.py:33
  159.3 1.5 copy-start.4
  160.9 6.0 %copy-start.3 = (f32[448,1536]{1,0:T(8,128)S(1)}, f32[448,1536]{1,0:T(8,128)}, u32[]{:S(2)}) copy-start(f32[448,1536]{1,0:T(8,128)} %bitcast_convert_fusion) | copy-start | bytes 8257540
  164.4 0.9 copy-start.5
  164.4 1.3 copy-start.7
  171.3 1.3 copy-start.8
  172.7 2.4 %copy-start.6 = (bf16[448,768]{1,0:T(8,128)(2,1)S(1)}, bf16[448,768]{1,0:T(8,128)(2,1)}, u32[]{:S(2)}) copy-start(bf16[448,768]{1,0:T(8,128)(2,1)} %copy-done.5) | copy-start | bytes 2064388
  178.6 35.7 %all-to-all-start.1 = ((bf16[64,7,1024]{2,1,0:T(8,128)(2,1)}), bf16[64,7,1024]{2,1,0:T(8,128)(2,1)S(1)}, u32[]{:S(2)}, u32[]{:S(2)}) async-start(bf16[64,7,1024]{2,1,0:T(8,128)(2,1)} %reshape.168), calls=%async_computation.1 | async-start | bytes 2097152 | tf_op jit(solution)/shard_map/all_to_all | solution.py:130
  185.1 43.6 %reduce-scatter.5.cloned.1.call-start = ((), (), s32[]{:S(2)}) async-start(), calls=%async_computation.6 | async-start | bytes 442368 | tf_op jit(solution)/shard_map/reduce_scatter | solution.py:33
Sparse Core Ops, SparseCore 0:
  11.2 113.0 all-gather.1
  172.6 25.6 reduce-scatter.2
  201.0 27.6 reduce-scatter.4
where the time goes:
time: 238 us; the launch traced here: 237 us
  waiting for transfers between devices  145 us (61%)
  local copies, waits for them, and re-layouts  28.6 us (12%)
  starting transfers between devices  21.5 us (9%)
  matrix products  14.5 us (6%)
  between operations  14.1 us (6%)
  other arithmetic  13 us (5%)
    all_to_all x1, waiting for transfers between devices, side_by_side(): lax.all_to_all(both, axis, split_axis=split_dim, concat_axis=concat_dim,...  107 us
    reduce_scatter x2, waiting for transfers between devices, sum_in_order(): tiles = lax.psum_scatter(tiles, axes[k], scatter_dimension=0, tiled=True)  22.4 us
    all_to_all x1, waiting for transfers between devices, body(): lax.all_to_all(row_grad.astype(jnp.bfloat16).reshape(n_owner, cap, width)...  15.8 us
    all_to_all x1, starting transfers between devices, side_by_side(): lax.all_to_all(both, axis, split_axis=split_dim, concat_axis=concat_dim,...  14.7 us
    all_to_all x1, starting transfers between devices, body(): lax.all_to_all(row_grad.astype(jnp.bfloat16).reshape(n_owner, cap, width)...  6.49 us
  transfers between devices with their start and end apart: 5, of which 4 were waited for; matrix products, arithmetic and copies ran while one was open for 17% of the time, Pallas kernels for 0%

commit v1 on v0

v1 whole, which is shorter than its diff:
```python
import functools

import jax
import jax.numpy as jnp
from jax import lax
from jax.experimental import pallas as pl
from jax.experimental.pallas import tpu as pltpu
from jax.sharding import Mesh
from jax.sharding import PartitionSpec as P


DP = ("dp_0", "dp_1")
DP_EXPERT = ("dp_0", "dp_1", "expert")
F32 = jnp.float32
BF16 = jnp.bfloat16
LANES = 128


def chunk_rows(start, slots, step):
    return pl.ds(start, slots, stride=step)


def pack_kernel(cap, ids_ref, probs_ref, tok_ref, grad_ref, out_ref, match_ref, wide_ref):
    slots, n_tok = match_ref.shape
    topk = ids_ref.shape[0]
    n_owner = slots // cap
    ids = ids_ref[...]
    probs = probs_ref[...]
    owner = lax.broadcasted_iota(jnp.int32, (n_owner, n_tok), 0)
    named = [owner == ids[k : k + 1, :] for k in range(topk)]
    per_owner = sum(n.astype(F32) for n in named)
    earlier = (
        lax.broadcasted_iota(jnp.int32, (n_tok, n_tok), 0)
        < lax.broadcasted_iota(jnp.int32, (n_tok, n_tok), 1)
    ).astype(F32)
    before = jnp.dot(per_owner.astype(BF16), earlier.astype(BF16), preferred_element_type=F32)
    slot = lax.broadcasted_iota(jnp.int32, (slots, n_tok), 0)
    match = jnp.zeros((slots, n_tok), F32)
    weight = jnp.zeros((slots, n_tok), F32)
    for k in range(topk):
        position = jnp.sum(jnp.where(named[k], before, 0.0), axis=0, keepdims=True)
        here = slot == ids[k : k + 1, :] * cap + position.astype(jnp.int32)
        match = match + here.astype(F32)
        weight = weight + jnp.where(here, probs[k : k + 1, :], 0.0)
    weight = jnp.sum(weight, axis=1, keepdims=True)
    match = match.astype(BF16)
    match_ref[...] = match
    n_chunk = tok_ref.shape[1] // LANES
    for half, src in enumerate((tok_ref, grad_ref)):
        for c in range(0, n_chunk, 2):
            rows = jnp.dot(
                match, src[:, c * LANES : (c + 2) * LANES], preferred_element_type=F32
            )
            if half:
                rows = rows * weight
            for i in range(2):
                wide_ref[chunk_rows(half * n_chunk + c + i, slots, 2 * n_chunk), :] = rows[
                    :, i * LANES : (i + 1) * LANES
                ]
    out_ref[...] = wide_ref[...].astype(BF16)


def pack(ids, probs, tokens, out_grad, n_owner, cap):
    n_tok, width = tokens.shape
    slots = n_owner * cap
    rows = slots * 2 * width // LANES
    return pl.pallas_call(
        functools.partial(pack_kernel, cap),
        out_shape=(
            jax.ShapeDtypeStruct((rows, LANES), BF16),
            jax.ShapeDtypeStruct((slots, n_tok), BF16),
        ),
        scratch_shapes=[pltpu.VMEM((rows, LANES), F32)],
        name="pack",
    )(ids, probs, tokens, out_grad)


def take_pair(wide_ref, first, second, slots, step):
    return jnp.concatenate(
        [
            wide_ref[chunk_rows(first, slots, step), :],
            wide_ref[chunk_rows(second, slots, step), :],
        ],
        axis=1,
    ).astype(BF16)


def piece_index(where_ref, k):
    high, low, n_low = where_ref[0], where_ref[1], 4
    column = lax.rem(low - k + n_low, n_low)
    return high * n_low + column, (1 - high) * n_low + column


def grads_kernel(n_piece, hidden, *refs):
    where_ref, got_ref, pre_ref = refs[:3]
    mine1, other1 = refs[3 : 3 + n_piece], refs[3 + n_piece : 3 + 2 * n_piece]
    at = 3 + 2 * n_piece
    mine2, other2 = refs[at : at + n_piece], refs[at + n_piece : at + 2 * n_piece]
    row_ref, both_ref, hid_ref, proj_ref, wide_ref, narrow_ref = refs[at + 2 * n_piece :]
    slots = pre_ref.shape[0]
    n_chunk = 2 * n_piece
    wide_ref[...] = got_ref[...].astype(F32)
    total = None
    for k in range(n_piece):
        first, second = piece_index(where_ref, k)
        left = take_pair(wide_ref, n_chunk + first, n_chunk + second, slots, 2 * n_chunk)
        right = jnp.concatenate([mine1[k][...], other1[k][...]], axis=0)
        part = jnp.dot(left, right, preferred_element_type=F32)
        total = part if total is None else total + part
    proj_ref[...] = total[:, hidden:].astype(BF16)
    grad = total[:, :hidden]
    gate = pre_ref[:, :hidden].astype(F32)
    up = pre_ref[:, hidden:].astype(F32)
    sig = jax.nn.sigmoid(gate)
    act = gate * sig
    hid_ref[...] = (act * up).astype(BF16)
    both_ref[:, hidden:] = (grad * act).astype(BF16)
    both_ref[:, :hidden] = (grad * up * sig * (1.0 + gate * (1.0 - sig))).astype(BF16)
    for k in range(n_piece):
        first, second = piece_index(where_ref, k)
        right = jnp.concatenate([mine2[k][...], other2[k][...]], axis=0)
        rows = lax.dot_general(
            both_ref[...], right, (((1,), (1,)), ((), ())), preferred_element_type=F32
        )
        narrow_ref[chunk_rows(first, slots, n_chunk), :] = rows[:, :LANES]
        narrow_ref[chunk_rows(second, slots, n_chunk), :] = rows[:, LANES:]
    row_ref[...] = narrow_ref[...].astype(BF16)


def vmem():
    return pl.BlockSpec(memory_space=pltpu.VMEM)


def grads(where, got, pre, mine1, other1, mine2, other2, hidden, width):
    slots = pre.shape[0]
    n_piece = len(mine1)
    rank = mine1[0].shape[1] - hidden
    n_in = 2 + 4 * n_piece
    return pl.pallas_call(
        functools.partial(grads_kernel, n_piece, hidden),
        in_specs=[pl.BlockSpec(memory_space=pltpu.SMEM)] + [vmem()] * n_in,
        out_shape=(
            jax.ShapeDtypeStruct((slots * width // LANES, LANES), BF16),
            jax.ShapeDtypeStruct((slots, 2 * hidden), BF16),
            jax.ShapeDtypeStruct((slots, hidden), BF16),
            jax.ShapeDtypeStruct((slots, rank), BF16),
        ),
        scratch_shapes=[
            pltpu.VMEM((2 * slots * width // LANES, LANES), F32),
            pltpu.VMEM((slots * width // LANES, LANES), F32),
        ],
        name="grads",
    )(where, got, pre, *mine1, *other1, *mine2, *other2)


def terms_kernel(n_piece, hidden, *refs):
    where_ref, got_ref, both_ref, hid_ref, proj_ref = refs[:5]
    mine1, other1 = refs[5 : 5 + n_piece], refs[5 + n_piece : 5 + 2 * n_piece]
    out_ref, wide_ref = refs[5 + 2 * n_piece :]
    slots = hid_ref.shape[0]
    n_chunk = 2 * n_piece
    wide_ref[...] = got_ref[...].astype(F32)
    total = None
    for k in range(n_piece):
        first, second = piece_index(where_ref, k)
        left = take_pair(wide_ref, first, second, slots, 2 * n_chunk)
        right = jnp.concatenate([mine1[k][:, hidden:], other1[k][:, hidden:]], axis=0)
        part = jnp.dot(left, right, preferred_element_type=F32)
        total = part if total is None else total + part
    x_proj = total.astype(BF16)
    by_rows = (((0,), (0,)), ((), ()))
    first_two = lax.dot_general(x_proj, both_ref[...], by_rows, preferred_element_type=F32)
    last = lax.dot_general(proj_ref[...], hid_ref[...], by_rows, preferred_element_type=F32)
    part = x_proj.shape[1] // n_chunk
    for n, term in enumerate((first_two[:, :hidden], first_two[:, hidden:], last)):
        term = term.astype(BF16)
        for d in range(n_chunk):
            out_ref[d % n_piece, d // n_piece, n] = term[d * part : (d + 1) * part]


def terms(where, got, both, hid, proj, mine1, other1):
    hidden = hid.shape[1]
    n_piece = len(mine1)
    part = proj.shape[1] // (2 * n_piece)
    return pl.pallas_call(
        functools.partial(terms_kernel, n_piece, hidden),
        in_specs=[pl.BlockSpec(memory_space=pltpu.SMEM)] + [vmem()] * (4 + 2 * n_piece),
        out_shape=jax.ShapeDtypeStruct((n_piece, 2, 3, part, hidden), BF16),
        scratch_shapes=[pltpu.VMEM(got.shape, F32)],
        name="terms",
    )(where, got, both, hid, proj, *mine1, *other1)


def combine_kernel(match_ref, got_ref, out_ref, wide_ref):
    slots = match_ref.shape[0]
    n_chunk = out_ref.shape[1] // LANES
    wide_ref[...] = got_ref[...].astype(F32)
    for c in range(0, n_chunk, 2):
        rows = take_pair(wide_ref, c, c + 1, slots, n_chunk)
        total = lax.dot_general(
            match_ref[...], rows, (((0,), (0,)), ((), ())), preferred_element_type=F32
        )
        out_ref[:, c * LANES : (c + 2) * LANES] = total.astype(BF16)


def combine(match, got, width):
    n_tok = match.shape[1]
    return pl.pallas_call(
        combine_kernel,
        out_shape=jax.ShapeDtypeStruct((n_tok, width), BF16),
        scratch_shapes=[pltpu.VMEM(got.shape, F32)],
        name="combine",
    )(match, got)


def swap(value):
    return lax.ppermute(value, "dp_0", [(0, 1), (1, 0)])


def shifted(value):
    size = lax.axis_size("dp_1")
    return [
        lax.ppermute(value, "dp_1", [(i, (i + k) % size) for i in range(size)])
        for k in range(1, size)
    ]


def exchange(value, n_owner):
    rows, lanes = value.shape
    out = lax.all_to_all(
        value.reshape(n_owner, rows // n_owner, lanes), "expert", 0, 0, tiled=True
    )
    return out.reshape(rows, lanes)


def body(
    tokens, out_grad, expert_ids, gate_probs, saved_pre, gate_weight, up_weight, down_weight, basis
):
    n_owner = lax.axis_size("expert")
    width = tokens.shape[1]
    slots = saved_pre.shape[2]
    cap = slots // n_owner
    hidden = gate_weight.shape[2]
    where = jnp.stack([lax.axis_index("dp_0"), lax.axis_index("dp_1")]).astype(jnp.int32)

    w1 = jnp.concatenate([down_weight[0], basis[0]], axis=1)
    far1 = swap(w1)
    sent, match = pack(expert_ids.T, gate_probs.T, tokens, out_grad, n_owner, cap)
    got = exchange(sent, n_owner)
    w2 = jnp.concatenate([gate_weight[0], up_weight[0]], axis=1)
    far2 = swap(w2)
    mine1 = [w1] + shifted(w1)
    mine2 = [w2] + shifted(w2)
    other1 = [far1] + shifted(far1)
    other2 = [far2] + shifted(far2)
    row_grad, both, hid, proj = grads(
        where, got, saved_pre[0, 0], mine1, other1, mine2, other2, hidden, width
    )
    back = exchange(row_grad, n_owner)
    parts = terms(where, got, both, hid, proj, mine1, other1)
    n_low, n_high, n_term, part, _ = parts.shape
    parts = parts.reshape(n_low, n_high * n_term * part, hidden)
    low = lax.axis_index("dp_1")
    summed = lax.dynamic_index_in_dim(parts, low, 0, keepdims=False).astype(F32)
    for k in range(1, n_low):
        out = lax.dynamic_index_in_dim(parts, lax.rem(low + k, n_low), 0, keepdims=False)
        out = lax.ppermute(out, "dp_1", [(i, (i + k) % n_low) for i in range(n_low)])
        summed = summed + out.astype(F32)
    summed = summed.reshape(n_high, n_term * part, hidden)
    high = lax.axis_index("dp_0")
    mine = jnp.where(high == 0, summed[0], summed[1])
    other = jnp.where(high == 0, summed[1], summed[0]).astype(BF16)
    other = swap(other)
    proj_grads = (mine + other.astype(F32)).reshape(1, n_term, part, hidden)
    in_grad = combine(match, back, width)
    return in_grad, proj_grads


def solution(mesh):
    finer = Mesh(mesh.devices.reshape(2, 4, mesh.shape["expert"]), DP_EXPERT)
    placed = (
        P(DP_EXPERT, None),
        P(DP_EXPERT, None),
        P(DP_EXPERT, None),
        P(DP_EXPERT, None),
        P(DP, "expert", None, None),
        P("expert", DP, None),
        P("expert", DP, None),
        P("expert", DP, None),
        P("expert", DP, None),
    )
    return jax.shard_map(
        body,
        mesh=finer,
        in_specs=placed,
        out_specs=(P(DP_EXPERT, None), P("expert", None, DP, None)),
        check_vma=False,
    )
```

time: 238 us -> 189 us (0.79)
  the two profiles are of different devices: /device:TPU:9 before, /device:TPU:17 now
where the time goes in v1:
time: 189 us; the launch traced here: 188 us
  starting transfers between devices  107 us (57%)
  waiting for transfers between devices  50.8 us (27%)
  Pallas kernels  21 us (11%)
  local copies, waits for them, and re-layouts  4.06 us (2%)
  other arithmetic  3.57 us (2%)
    all_to_all x2, starting transfers between devices, exchange(): lax.all_to_all(value.reshape(n_owner, rows // n_owner, lanes), 'expert',...  44.8 us
    ppermute x12, starting transfers between devices, shifted(): lax.ppermute(value, 'dp_1', [(i, (i + k) % size) for i in range(size)])  39.1 us
    ppermute x3, waiting for transfers between devices, swap(): return lax.ppermute(value, 'dp_0', [(0, 1), (1, 0)])  20.5 us
    ppermute x12, waiting for transfers between devices, shifted(): lax.ppermute(value, 'dp_1', [(i, (i + k) % size) for i in range(size)])  17 us
    ppermute x3, starting transfers between devices, swap(): return lax.ppermute(value, 'dp_0', [(0, 1), (1, 0)])  13.6 us
    ppermute x3, waiting for transfers between devices, body(): lax.ppermute(out, 'dp_1', [(i, (i + k) % n_low) for i in range(n_low)])  13.3 us
    ppermute x3, starting transfers between devices, body(): lax.ppermute(out, 'dp_1', [(i, (i + k) % n_low) for i in range(n_low)])  9.57 us
    pallas_call x1, Pallas kernels, grads(): pl.pallas_call(functools.partial(grads_kernel, n_piece, hidden), in_specs...  8.51 us
  transfers between devices with their start and end apart: 20, of which 8 were waited for; matrix products, arithmetic and copies ran while one was open for 3% of the time, Pallas kernels for 3%

profile of v1, /device:TPU:17, one launch (start us, length us, event | category | flops | bytes accessed | tf_op | source)
XLA Modules:
  0.0 187.6 jit_solution(5925885714042974788)
XLA Ops:
  0.6 3.9 %pack.1 = (bf16[7168,128]{1,0:T(8,128)(2,1)}, bf16[448,128]{1,0:T(8,128)(2,1)}) custom-call(s32[3,128]{1,0:T(4,128)} %bitcast.37, f32[3,128]{1,0:T(4,128)} %bitcast.38, bf16[128,1024]{1,0:T(8,128)(2,1)} %tok_ref.1, bf16[128,1024]{1,0:T(8,128)(2,1)} %grad_ref.1), custom_call_target="tpu_custom_call" | custom-call | tf_op jit(solution)/shard_map/pack/pallas_call | solution.py:67
  4.6 14.7 %all-to-all-start = ((bf16[64,112,128]{2,1,0:T(8,128)(2,1)}), bf16[64,112,128]{2,1,0:T(8,128)(2,1)S(1)}, u32[]{:S(2)}, u32[]{:S(2)}) async-start(bf16[64,112,128]{2,1,0:T(8,128)(2,1)} %bitcast.29), calls=%async_computation | async-start | bytes 3670016 | tf_op jit(solution)/shard_map/all_to_all | solution.py:230
  19.3 3.1 %collective-permute-start = (bf16[128,1024]{1,0:T(8,128)(2,1)S(1)}, bf16[128,1024]{1,0:T(8,128)(2,1)S(1)}, u32[]{:S(2)}, u32[]{:S(2)}) collective-permute-start(bf16[128,1024]{1,0:T(8,128)(2,1)S(1)} %pad_maximum_fusion.1.refs_3_.refs_5_), channel_id=1, source_target_pairs={{0,64},{64,128},{128,192},{192,0},{1,65},{65,129},{129,193},{193,1... | collective-permute-start | bytes 786440 | tf_op jit(solution)/shard_map/ppermute | solution.py:223
  22.4 4.4 %collective-permute-start.1 = (bf16[128,1024]{1,0:T(8,128)(2,1)S(1)}, bf16[128,1024]{1,0:T(8,128)(2,1)S(1)}, u32[]{:S(2)}, u32[]{:S(2)}) collective-permute-start(bf16[128,1024]{1,0:T(8,128)(2,1)S(1)} %pad_maximum_fusion.1.refs_3_.refs_5_), channel_id=1, source_target_pairs={{0,128},{64,192},{128,0},{192,64},{1,129},{65,193},{129,1},{193,65... | collective-permute-start | bytes 786440 | tf_op jit(solution)/shard_map/ppermute | solution.py:223
  29.9 4.8 %collective-permute-start.3 = (bf16[128,1024]{1,0:T(8,128)(2,1)S(1)}, bf16[128,1024]{1,0:T(8,128)(2,1)S(1)}, u32[]{:S(2)}, u32[]{:S(2)}) collective-permute-start(bf16[128,1024]{1,0:T(8,128)(2,1)S(1)} %pad_maximum_fusion.1.refs_3_.refs_5_), channel_id=1, source_target_pairs={{0,256},{256,0},{1,257},{257,1},{2,258},{258,2},{3,259},{259,3},{4... | collective-permute-start | bytes 786440 | tf_op jit(solution)/shard_map/ppermute | solution.py:217
  35.7 4.4 %collective-permute-start.10 = (bf16[128,1536]{1,0:T(8,128)(2,1)S(1)}, bf16[128,1536]{1,0:T(8,128)(2,1)}, u32[]{:S(2)}, u32[]{:S(2)}) collective-permute-start(bf16[128,1536]{1,0:T(8,128)(2,1)S(1)} %pad_maximum_fusion.refs_11_), channel_id=1, source_target_pairs={{0,256},{256,0},{1,257},{257,1},{2,258},{258,2},{3,259},{259,3},{4... | collective-permute-start | bytes 1179656 | tf_op jit(solution)/shard_map/ppermute | solution.py:217
  45.2 3.4 %collective-permute-start.9 = (bf16[128,1536]{1,0:T(8,128)(2,1)S(1)}, bf16[128,1536]{1,0:T(8,128)(2,1)S(1)}, u32[]{:S(2)}, u32[]{:S(2)}) collective-permute-start(bf16[128,1536]{1,0:T(8,128)(2,1)S(1)} %pad_maximum_fusion.refs_11_), channel_id=1, source_target_pairs={{0,192},{64,0},{128,64},{192,128},{1,193},{65,1},{129,65},{193,129... | collective-permute-start | bytes 1179656 | tf_op jit(solution)/shard_map/ppermute | solution.py:223
  48.6 4.6 %collective-permute-done.3.refs_7_.refs_9_ = bf16[128,1024]{1,0:T(8,128)(2,1)S(1)} collective-permute-done((bf16[128,1024]{1,0:T(8,128)(2,1)S(1)}, bf16[128,1024]{1,0:T(8,128)(2,1)S(1)}, u32[]{:S(2)}, u32[]{:S(2)}) %collective-permute-start.3) | collective-permute-done | bytes 262176 | tf_op jit(solution)/shard_map/ppermute | solution.py:217
  53.2 3.1 %collective-permute-start.4 = (bf16[128,1024]{1,0:T(8,128)(2,1)S(1)}, bf16[128,1024]{1,0:T(8,128)(2,1)S(1)}, u32[]{:S(2)}, u32[]{:S(2)}) collective-permute-start(bf16[128,1024]{1,0:T(8,128)(2,1)S(1)} %collective-permute-done.3.refs_7_.refs_9_), channel_id=1, source_target_pairs={{0,64},{64,128},{128,192},{192,0},{1,65},{65,129},{129,193},{193,1... | collective-permute-start | bytes 786440 | tf_op jit(solution)/shard_map/ppermute | solution.py:223
  56.3 5.8 %collective-permute-done.10.refs_15_ = bf16[128,1536]{1,0:T(8,128)(2,1)} collective-permute-done((bf16[128,1536]{1,0:T(8,128)(2,1)S(1)}, bf16[128,1536]{1,0:T(8,128)(2,1)}, u32[]{:S(2)}, u32[]{:S(2)}) %collective-permute-start.10) | collective-permute-done | bytes 393248 | tf_op jit(solution)/shard_map/ppermute | solution.py:217
  62.2 3.1 %collective-permute-start.11 = (bf16[128,1536]{1,0:T(8,128)(2,1)}, bf16[128,1536]{1,0:T(8,128)(2,1)}, u32[]{:S(2)}, u32[]{:S(2)}) collective-permute-start(bf16[128,1536]{1,0:T(8,128)(2,1)} %collective-permute-done.10.refs_15_), channel_id=1, source_target_pairs={{0,64},{64,128},{128,192},{192,0},{1,65},{65,129},{129,193},{193,1... | collective-permute-start | bytes 1179656 | tf_op jit(solution)/shard_map/ppermute | solution.py:223
  65.3 4.4 %collective-permute-start.12 = (bf16[128,1536]{1,0:T(8,128)(2,1)}, bf16[128,1536]{1,0:T(8,128)(2,1)}, u32[]{:S(2)}, u32[]{:S(2)}) collective-permute-start(bf16[128,1536]{1,0:T(8,128)(2,1)} %collective-permute-done.10.refs_15_), channel_id=1, source_target_pairs={{0,128},{64,192},{128,0},{192,64},{1,129},{65,193},{129,1},{193,65... | collective-permute-start | bytes 1179656 | tf_op jit(solution)/shard_map/ppermute | solution.py:223
  75.7 4.4 %collective-permute-start.6 = (bf16[128,1024]{1,0:T(8,128)(2,1)S(1)}, bf16[128,1024]{1,0:T(8,128)(2,1)}, u32[]{:S(2)}, u32[]{:S(2)}) collective-permute-start(bf16[128,1024]{1,0:T(8,128)(2,1)S(1)} %collective-permute-done.3.refs_7_.refs_9_), channel_id=1, source_target_pairs={{0,192},{64,0},{128,64},{192,128},{1,193},{65,1},{129,65},{193,129... | collective-permute-start | bytes 786440 | tf_op jit(solution)/shard_map/ppermute | solution.py:223
  80.7 9.9 %collective-permute-done.5.refs_9_.refs_11_ = bf16[128,1024]{1,0:T(8,128)(2,1)} collective-permute-done((bf16[128,1024]{1,0:T(8,128)(2,1)S(1)}, bf16[128,1024]{1,0:T(8,128)(2,1)}, u32[]{:S(2)}, u32[]{:S(2)}) %collective-permute-start.5) | collective-permute-done | bytes 262176 | tf_op jit(solution)/shard_map/ppermute | solution.py:223
  90.6 7.1 %collective-permute-done.6.refs_10_.refs_12_ = bf16[128,1024]{1,0:T(8,128)(2,1)} collective-permute-done((bf16[128,1024]{1,0:T(8,128)(2,1)S(1)}, bf16[128,1024]{1,0:T(8,128)(2,1)}, u32[]{:S(2)}, u32[]{:S(2)}) %collective-permute-start.6) | collective-permute-done | bytes 262176 | tf_op jit(solution)/shard_map/ppermute | solution.py:223
  98.9 8.5 %grads.1 = (bf16[3584,128]{1,0:T(8,128)(2,1)}, bf16[448,1536]{1,0:T(8,128)(2,1)}, bf16[448,768]{1,0:T(8,128)(2,1)}, bf16[448,256]{1,0:T(8,128)(2,1)}) custom-call(s32[2]{0:T(128)} %pad_add_fusion.refs_0_, bf16[7168,128]{1,0:T(8,128)(2,1)} %bitcast.24, bf16[448,1536]{1,0:T(8,128)(2,1)} %bitcast.30, bf16[128,1024]{1,0:T(8,128)(2,1)} %copy-done.2, ...), custom_call_target="tpu_custom_call" | custom-call | tf_op jit(solution)/shard_map/grads/pallas_call | solution.py:139
  107.4 30.1 %all-to-all-start.1 = ((bf16[64,56,128]{2,1,0:T(8,128)(2,1)}), bf16[64,56,128]{2,1,0:T(8,128)(2,1)S(1)}, u32[]{:S(2)}, u32[]{:S(2)}) async-start(bf16[64,56,128]{2,1,0:T(8,128)(2,1)} %bitcast.31), calls=%async_computation.1 | async-start | bytes 1835008 | tf_op jit(solution)/shard_map/all_to_all | solution.py:230
  137.6 6.1 %terms.1 = bf16[4,2,3,32,768]{4,3,2,1,0:T(8,128)(2,1)} custom-call(s32[2]{0:T(128)} %pad_add_fusion.refs_0_, bf16[7168,128]{1,0:T(8,128)(2,1)} %bitcast.25, bf16[448,1536]{1,0:T(8,128)(2,1)} %get-tuple-element.11.refs_2_, bf16[448,768]{1,0:T(8,128)(2,1)} %get-tuple-element.12.refs_3_, bf16[448,256]{1,0:T(8,128)(2,1)} %get-tuple-element.13.refs_4_, ...), custom_call_target="tpu_custom_call" | custom-call | tf_op jit(solution)/shard_map/terms/pallas_call | solution.py:185
  144.8 4.2 %collective-permute-start.16 = (bf16[192,768]{1,0:T(8,128)(2,1)S(1)}, bf16[192,768]{1,0:T(8,128)(2,1)S(1)}, u32[]{:S(2)}, u32[]{:S(2)}) collective-permute-start(bf16[192,768]{1,0:T(8,128)(2,1)S(1)} %get-tuple-element.15), channel_id=1, source_target_pairs={{0,192},{64,0},{128,64},{192,128},{1,193},{65,1},{129,65},{193,129... | collective-permute-start | bytes 884744 | tf_op jit(solution)/shard_map/ppermute | solution.py:267
  149.0 3.4 %collective-permute-start.15 = (bf16[192,768]{1,0:T(8,128)(2,1)S(1)}, bf16[192,768]{1,0:T(8,128)(2,1)S(1)}, u32[]{:S(2)}, u32[]{:S(2)}) collective-permute-start(bf16[192,768]{1,0:T(8,128)(2,1)S(1)} %get-tuple-element.16), channel_id=1, source_target_pairs={{0,128},{64,192},{128,0},{192,64},{1,129},{65,193},{129,1},{193,65... | collective-permute-start | bytes 884744 | tf_op jit(solution)/shard_map/ppermute | solution.py:267
  155.8 4.6 %collective-permute-done.15 = bf16[192,768]{1,0:T(8,128)(2,1)S(1)} collective-permute-done((bf16[192,768]{1,0:T(8,128)(2,1)S(1)}, bf16[192,768]{1,0:T(8,128)(2,1)S(1)}, u32[]{:S(2)}, u32[]{:S(2)}) %collective-permute-start.15) | collective-permute-done | bytes 294944 | tf_op jit(solution)/shard_map/ppermute | solution.py:267
  160.4 7.3 %collective-permute-done.14 = bf16[192,768]{1,0:T(8,128)(2,1)S(1)} collective-permute-done((bf16[192,768]{1,0:T(8,128)(2,1)S(1)}, bf16[192,768]{1,0:T(8,128)(2,1)S(1)}, u32[]{:S(2)}, u32[]{:S(2)}) %collective-permute-start.14) | collective-permute-done | bytes 294944 | tf_op jit(solution)/shard_map/ppermute | solution.py:267
  168.8 4.4 %collective-permute-start.17 = (bf16[96,768]{1,0:T(8,128)(2,1)S(1)}, bf16[96,768]{1,0:T(8,128)(2,1)S(1)}, u32[]{:S(2)}, u32[]{:S(2)}) collective-permute-start(bf16[96,768]{1,0:T(8,128)(2,1)S(1)} %select_convert_fusion), channel_id=1, source_target_pairs={{0,256},{256,0},{1,257},{257,1},{2,258},{258,2},{3,259},{259,3},{4... | collective-permute-start | bytes 442376 | tf_op jit(solution)/shard_map/ppermute | solution.py:217
  173.3 10.1 %collective-permute-done.17 = bf16[96,768]{1,0:T(8,128)(2,1)S(1)} collective-permute-done((bf16[96,768]{1,0:T(8,128)(2,1)S(1)}, bf16[96,768]{1,0:T(8,128)(2,1)S(1)}, u32[]{:S(2)}, u32[]{:S(2)}) %collective-permute-start.17) | collective-permute-done | bytes 147488 | tf_op jit(solution)/shard_map/ppermute | solution.py:217
  (55 shorter events, 26.7 us)
Async XLA Ops:
  4.6 93.1 %all-to-all-start = ((bf16[64,112,128]{2,1,0:T(8,128)(2,1)}), bf16[64,112,128]{2,1,0:T(8,128)(2,1)S(1)}, u32[]{:S(2)}, u32[]{:S(2)}) async-start(bf16[64,112,128]{2,1,0:T(8,128)(2,1)} %bitcast.29), calls=%async_computation | async-start | bytes 3670016 | tf_op jit(solution)/shard_map/all_to_all | solution.py:230
  19.3 78.4 %copy-start.2 = (bf16[128,1024]{1,0:T(8,128)(2,1)}, bf16[128,1024]{1,0:T(8,128)(2,1)S(1)}, u32[]{:S(2)}) copy-start(bf16[128,1024]{1,0:T(8,128)(2,1)S(1)} %pad_maximum_fusion.1.refs_3_.refs_5_) | copy-start | bytes 786436
  19.3 20.8 %collective-permute-start = (bf16[128,1024]{1,0:T(8,128)(2,1)S(1)}, bf16[128,1024]{1,0:T(8,128)(2,1)S(1)}, u32[]{:S(2)}, u32[]{:S(2)}) collective-permute-start(bf16[128,1024]{1,0:T(8,128)(2,1)S(1)} %pad_maximum_fusion.1.refs_3_.refs_5_), channel_id=1, source_target_pairs={{0,64},{64,128},{128,192},{192,0},{1,65},{65,129},{129,193},{193,1... | collective-permute-start | bytes 786440 | tf_op jit(solution)/shard_map/ppermute | solution.py:223
  22.4 20.0 %collective-permute-start.1 = (bf16[128,1024]{1,0:T(8,128)(2,1)S(1)}, bf16[128,1024]{1,0:T(8,128)(2,1)S(1)}, u32[]{:S(2)}, u32[]{:S(2)}) collective-permute-start(bf16[128,1024]{1,0:T(8,128)(2,1)S(1)} %pad_maximum_fusion.1.refs_3_.refs_5_), channel_id=1, source_target_pairs={{0,128},{64,192},{128,0},{192,64},{1,129},{65,193},{129,1},{193,65... | collective-permute-start | bytes 786440 | tf_op jit(solution)/shard_map/ppermute | solution.py:223
  26.8 18.4 %collective-permute-start.2 = (bf16[128,1024]{1,0:T(8,128)(2,1)S(1)}, bf16[128,1024]{1,0:T(8,128)(2,1)S(1)}, u32[]{:S(2)}, u32[]{:S(2)}) collective-permute-start(bf16[128,1024]{1,0:T(8,128)(2,1)S(1)} %pad_maximum_fusion.1.refs_3_.refs_5_), channel_id=1, source_target_pairs={{0,192},{64,0},{128,64},{192,128},{1,193},{65,1},{129,65},{193,129... | collective-permute-start | bytes 786440 | tf_op jit(solution)/shard_map/ppermute | solution.py:223
  29.9 23.3 %collective-permute-start.3 = (bf16[128,1024]{1,0:T(8,128)(2,1)S(1)}, bf16[128,1024]{1,0:T(8,128)(2,1)S(1)}, u32[]{:S(2)}, u32[]{:S(2)}) collective-permute-start(bf16[128,1024]{1,0:T(8,128)(2,1)S(1)} %pad_maximum_fusion.1.refs_3_.refs_5_), channel_id=1, source_target_pairs={{0,256},{256,0},{1,257},{257,1},{2,258},{258,2},{3,259},{259,3},{4... | collective-permute-start | bytes 786440 | tf_op jit(solution)/shard_map/ppermute | solution.py:217
  35.7 62.0 %copy-start.3 = (bf16[128,1536]{1,0:T(8,128)(2,1)}, bf16[128,1536]{1,0:T(8,128)(2,1)S(1)}, u32[]{:S(2)}) copy-start(bf16[128,1536]{1,0:T(8,128)(2,1)S(1)} %pad_maximum_fusion.refs_11_) | copy-start | bytes 1179652
  35.7 26.5 %collective-permute-start.10 = (bf16[128,1536]{1,0:T(8,128)(2,1)S(1)}, bf16[128,1536]{1,0:T(8,128)(2,1)}, u32[]{:S(2)}, u32[]{:S(2)}) collective-permute-start(bf16[128,1536]{1,0:T(8,128)(2,1)S(1)} %pad_maximum_fusion.refs_11_), channel_id=1, source_target_pairs={{0,256},{256,0},{1,257},{257,1},{2,258},{258,2},{3,259},{259,3},{4... | collective-permute-start | bytes 1179656 | tf_op jit(solution)/shard_map/ppermute | solution.py:217
  40.1 57.6 %copy-start.4 = (bf16[128,1024]{1,0:T(8,128)(2,1)}, bf16[128,1024]{1,0:T(8,128)(2,1)S(1)}, u32[]{:S(2)}) copy-start(bf16[128,1024]{1,0:T(8,128)(2,1)S(1)} %collective-permute-done.refs_4_.refs_6_) | copy-start | bytes 786436
  40.1 25.1 %collective-permute-start.7 = (bf16[128,1536]{1,0:T(8,128)(2,1)S(1)}, bf16[128,1536]{1,0:T(8,128)(2,1)S(1)}, u32[]{:S(2)}, u32[]{:S(2)}) collective-permute-start(bf16[128,1536]{1,0:T(8,128)(2,1)S(1)} %pad_maximum_fusion.refs_11_), channel_id=1, source_target_pairs={{0,64},{64,128},{128,192},{192,0},{1,65},{65,129},{129,193},{193,1... | collective-permute-start | bytes 1179656 | tf_op jit(solution)/shard_map/ppermute | solution.py:223
  42.4 55.3 %copy-start.5 = (bf16[128,1024]{1,0:T(8,128)(2,1)}, bf16[128,1024]{1,0:T(8,128)(2,1)S(1)}, u32[]{:S(2)}) copy-start(bf16[128,1024]{1,0:T(8,128)(2,1)S(1)} %collective-permute-done.1.refs_5_.refs_7_) | copy-start | bytes 786436
  42.4 27.3 %collective-permute-start.8 = (bf16[128,1536]{1,0:T(8,128)(2,1)S(1)}, bf16[128,1536]{1,0:T(8,128)(2,1)S(1)}, u32[]{:S(2)}, u32[]{:S(2)}) collective-permute-start(bf16[128,1536]{1,0:T(8,128)(2,1)S(1)} %pad_maximum_fusion.refs_11_), channel_id=1, source_target_pairs={{0,128},{64,192},{128,0},{192,64},{1,129},{65,193},{129,1},{193,65... | collective-permute-start | bytes 1179656 | tf_op jit(solution)/shard_map/ppermute | solution.py:223
  45.2 27.5 %collective-permute-start.9 = (bf16[128,1536]{1,0:T(8,128)(2,1)S(1)}, bf16[128,1536]{1,0:T(8,128)(2,1)S(1)}, u32[]{:S(2)}, u32[]{:S(2)}) collective-permute-start(bf16[128,1536]{1,0:T(8,128)(2,1)S(1)} %pad_maximum_fusion.refs_11_), channel_id=1, source_target_pairs={{0,192},{64,0},{128,64},{192,128},{1,193},{65,1},{129,65},{193,129... | collective-permute-start | bytes 1179656 | tf_op jit(solution)/shard_map/ppermute | solution.py:223
  53.2 21.7 %collective-permute-start.4 = (bf16[128,1024]{1,0:T(8,128)(2,1)S(1)}, bf16[128,1024]{1,0:T(8,128)(2,1)S(1)}, u32[]{:S(2)}, u32[]{:S(2)}) collective-permute-start(bf16[128,1024]{1,0:T(8,128)(2,1)S(1)} %collective-permute-done.3.refs_7_.refs_9_), channel_id=1, source_target_pairs={{0,64},{64,128},{128,192},{192,0},{1,65},{65,129},{129,193},{193,1... | collective-permute-start | bytes 786440 | tf_op jit(solution)/shard_map/ppermute | solution.py:223
  62.2 35.5 %collective-permute-start.11 = (bf16[128,1536]{1,0:T(8,128)(2,1)}, bf16[128,1536]{1,0:T(8,128)(2,1)}, u32[]{:S(2)}, u32[]{:S(2)}) collective-permute-start(bf16[128,1536]{1,0:T(8,128)(2,1)} %collective-permute-done.10.refs_15_), channel_id=1, source_target_pairs={{0,64},{64,128},{128,192},{192,0},{1,65},{65,129},{129,193},{193,1... | collective-permute-start | bytes 1179656 | tf_op jit(solution)/shard_map/ppermute | solution.py:223
  65.3 32.4 %collective-permute-start.12 = (bf16[128,1536]{1,0:T(8,128)(2,1)}, bf16[128,1536]{1,0:T(8,128)(2,1)}, u32[]{:S(2)}, u32[]{:S(2)}) collective-permute-start(bf16[128,1536]{1,0:T(8,128)(2,1)} %collective-permute-done.10.refs_15_), channel_id=1, source_target_pairs={{0,128},{64,192},{128,0},{192,64},{1,129},{65,193},{129,1},{193,65... | collective-permute-start | bytes 1179656 | tf_op jit(solution)/shard_map/ppermute | solution.py:223
  69.7 28.0 %collective-permute-start.13 = (bf16[128,1536]{1,0:T(8,128)(2,1)}, bf16[128,1536]{1,0:T(8,128)(2,1)}, u32[]{:S(2)}, u32[]{:S(2)}) collective-permute-start(bf16[128,1536]{1,0:T(8,128)(2,1)} %collective-permute-done.10.refs_15_), channel_id=1, source_target_pairs={{0,192},{64,0},{128,64},{192,128},{1,193},{65,1},{129,65},{193,129... | collective-permute-start | bytes 1179656 | tf_op jit(solution)/shard_map/ppermute | solution.py:223
  72.8 17.8 %collective-permute-start.5 = (bf16[128,1024]{1,0:T(8,128)(2,1)S(1)}, bf16[128,1024]{1,0:T(8,128)(2,1)}, u32[]{:S(2)}, u32[]{:S(2)}) collective-permute-start(bf16[128,1024]{1,0:T(8,128)(2,1)S(1)} %collective-permute-done.3.refs_7_.refs_9_), channel_id=1, source_target_pairs={{0,128},{64,192},{128,0},{192,64},{1,129},{65,193},{129,1},{193,65... | collective-permute-start | bytes 786440 | tf_op jit(solution)/shard_map/ppermute | solution.py:223
  75.7 22.0 %collective-permute-start.6 = (bf16[128,1024]{1,0:T(8,128)(2,1)S(1)}, bf16[128,1024]{1,0:T(8,128)(2,1)}, u32[]{:S(2)}, u32[]{:S(2)}) collective-permute-start(bf16[128,1024]{1,0:T(8,128)(2,1)S(1)} %collective-permute-done.3.refs_7_.refs_9_), channel_id=1, source_target_pairs={{0,192},{64,0},{128,64},{192,128},{1,193},{65,1},{129,65},{193,129... | collective-permute-start | bytes 786440 | tf_op jit(solution)/shard_map/ppermute | solution.py:223
  107.4 76.7 %all-to-all-start.1 = ((bf16[64,56,128]{2,1,0:T(8,128)(2,1)}), bf16[64,56,128]{2,1,0:T(8,128)(2,1)S(1)}, u32[]{:S(2)}, u32[]{:S(2)}) async-start(bf16[64,56,128]{2,1,0:T(8,128)(2,1)} %bitcast.31), calls=%async_computation.1 | async-start | bytes 1835008 | tf_op jit(solution)/shard_map/all_to_all | solution.py:230
  144.8 10.9 %collective-permute-start.16 = (bf16[192,768]{1,0:T(8,128)(2,1)S(1)}, bf16[192,768]{1,0:T(8,128)(2,1)S(1)}, u32[]{:S(2)}, u32[]{:S(2)}) collective-permute-start(bf16[192,768]{1,0:T(8,128)(2,1)S(1)} %get-tuple-element.15), channel_id=1, source_target_pairs={{0,192},{64,0},{128,64},{192,128},{1,193},{65,1},{129,65},{193,129... | collective-permute-start | bytes 884744 | tf_op jit(solution)/shard_map/ppermute | solution.py:267
  149.0 11.3 %collective-permute-start.15 = (bf16[192,768]{1,0:T(8,128)(2,1)S(1)}, bf16[192,768]{1,0:T(8,128)(2,1)S(1)}, u32[]{:S(2)}, u32[]{:S(2)}) collective-permute-start(bf16[192,768]{1,0:T(8,128)(2,1)S(1)} %get-tuple-element.16), channel_id=1, source_target_pairs={{0,128},{64,192},{128,0},{192,64},{1,129},{65,193},{129,1},{193,65... | collective-permute-start | bytes 884744 | tf_op jit(solution)/shard_map/ppermute | solution.py:267
  152.5 15.2 %collective-permute-start.14 = (bf16[192,768]{1,0:T(8,128)(2,1)S(1)}, bf16[192,768]{1,0:T(8,128)(2,1)S(1)}, u32[]{:S(2)}, u32[]{:S(2)}) collective-permute-start(bf16[192,768]{1,0:T(8,128)(2,1)S(1)} %get-tuple-element.14), channel_id=1, source_target_pairs={{0,64},{64,128},{128,192},{192,0},{1,65},{65,129},{129,193},{193,1... | collective-permute-start | bytes 884744 | tf_op jit(solution)/shard_map/ppermute | solution.py:267
  168.8 14.6 %collective-permute-start.17 = (bf16[96,768]{1,0:T(8,128)(2,1)S(1)}, bf16[96,768]{1,0:T(8,128)(2,1)S(1)}, u32[]{:S(2)}, u32[]{:S(2)}) collective-permute-start(bf16[96,768]{1,0:T(8,128)(2,1)S(1)} %select_convert_fusion), channel_id=1, source_target_pairs={{0,256},{256,0},{1,257},{257,1},{2,258},{258,2},{3,259},{259,3},{4... | collective-permute-start | bytes 442376 | tf_op jit(solution)/shard_map/ppermute | solution.py:217
  (10 other events, 161.7 us)

commit v2 on v1

v2 whole, which is shorter than its diff:
```python
import functools

import jax
import jax.numpy as jnp
from jax import lax
from jax.experimental import pallas as pl
from jax.experimental.pallas import tpu as pltpu
from jax.sharding import Mesh
from jax.sharding import PartitionSpec as P


DP = ("dp_0", "dp_1")
DP_EXPERT = ("dp_0", "dp_1", "expert")
F32 = jnp.float32
BF16 = jnp.bfloat16
LANES = 128


def chunk_rows(start, slots, step):
    return pl.ds(start, slots, stride=step)


def pack_kernel(cap, ids_ref, probs_ref, tok_ref, grad_ref, out_ref, match_ref, wide_ref):
    slots, n_tok = match_ref.shape
    topk = ids_ref.shape[0]
    n_owner = slots // cap
    ids = ids_ref[...]
    probs = probs_ref[...]
    owner = lax.broadcasted_iota(jnp.int32, (n_owner, n_tok), 0)
    named = [owner == ids[k : k + 1, :] for k in range(topk)]
    per_owner = sum(n.astype(F32) for n in named)
    earlier = (
        lax.broadcasted_iota(jnp.int32, (n_tok, n_tok), 0)
        < lax.broadcasted_iota(jnp.int32, (n_tok, n_tok), 1)
    ).astype(F32)
    before = jnp.dot(per_owner.astype(BF16), earlier.astype(BF16), preferred_element_type=F32)
    slot = lax.broadcasted_iota(jnp.int32, (slots, n_tok), 0)
    match = jnp.zeros((slots, n_tok), F32)
    weight = jnp.zeros((slots, n_tok), F32)
    for k in range(topk):
        position = jnp.sum(jnp.where(named[k], before, 0.0), axis=0, keepdims=True)
        here = slot == ids[k : k + 1, :] * cap + position.astype(jnp.int32)
        match = match + here.astype(F32)
        weight = weight + jnp.where(here, probs[k : k + 1, :], 0.0)
    weight = jnp.sum(weight, axis=1, keepdims=True)
    match = match.astype(BF16)
    match_ref[...] = match
    n_chunk = tok_ref.shape[1] // LANES
    for half, src in enumerate((tok_ref, grad_ref)):
        for c in range(0, n_chunk, 2):
            rows = jnp.dot(
                match, src[:, c * LANES : (c + 2) * LANES], preferred_element_type=F32
            )
            if half:
                rows = rows * weight
            for i in range(2):
                wide_ref[chunk_rows(half * n_chunk + c + i, slots, 2 * n_chunk), :] = rows[
                    :, i * LANES : (i + 1) * LANES
                ]
    out_ref[...] = wide_ref[...].astype(BF16)


def pack(ids, probs, tokens, out_grad, n_owner, cap):
    n_tok, width = tokens.shape
    slots = n_owner * cap
    rows = slots * 2 * width // LANES
    return pl.pallas_call(
        functools.partial(pack_kernel, cap),
        out_shape=(
            jax.ShapeDtypeStruct((rows, LANES), BF16),
            jax.ShapeDtypeStruct((slots, n_tok), BF16),
        ),
        scratch_shapes=[pltpu.VMEM((rows, LANES), F32)],
        name="pack",
    )(ids, probs, tokens, out_grad)


def piece_rows(where_ref, k, other):
    high, low = where_ref[0], where_ref[1]
    row = jnp.bitwise_and(high + other, 1) * 4 + jnp.bitwise_and(low + 4 - k, 3)
    return pl.ds(pl.multiple_of(row * LANES, LANES), LANES)


def fetch_pieces(where_ref, pieces, columns, into, sems):
    copies = []
    for i, piece in enumerate(pieces):
        rows = piece_rows(where_ref, i // 2, i % 2)
        copy = pltpu.make_async_copy(piece.at[:, columns], into.at[rows, :], sems.at[i])
        copy.start()
        copies.append(copy)
    return copies


def spread(wide_ref, first, step, into):
    slots, width = into.shape
    for c in range(width // LANES):
        into[:, c * LANES : (c + 1) * LANES] = wide_ref[
            chunk_rows(first + c, slots, step), :
        ].astype(BF16)


def core_kernel(n_piece, hidden, *refs):
    where_ref, got_ref, pre_ref = refs[:3]
    pieces = refs[3 : 3 + n_piece]
    outs = refs[3 + n_piece : 3 + n_piece + 5]
    both_ref, part_refs = outs[0], outs[1:]
    got, pre, weights, wide, x_rows, dy_rows, term_ref, sems = refs[3 + n_piece + 5 :]
    width = weights.shape[0]
    n_chunk = width // LANES
    fetch_got = pltpu.make_async_copy(got_ref, got, sems.at[n_piece])
    fetch_got.start()
    copies = fetch_pieces(where_ref, pieces, pl.ds(0, weights.shape[1]), weights, sems)
    fetch_pre = pltpu.make_async_copy(pre_ref, pre, sems.at[n_piece + 1])
    fetch_pre.start()
    fetch_got.wait()
    wide[...] = got[...].astype(F32)
    spread(wide, n_chunk, 2 * n_chunk, dy_rows)
    spread(wide, 0, 2 * n_chunk, x_rows)
    for copy in copies:
        copy.wait()
    grad = jnp.dot(dy_rows[...], weights[:, :hidden], preferred_element_type=F32)
    dy_proj = jnp.dot(dy_rows[...], weights[:, hidden:], preferred_element_type=F32).astype(BF16)
    x_proj = jnp.dot(x_rows[...], weights[:, hidden:], preferred_element_type=F32).astype(BF16)
    fetch_pre.wait()
    gate = pre[:, :hidden].astype(F32)
    up = pre[:, hidden:].astype(F32)
    sig = jax.nn.sigmoid(gate)
    act = gate * sig
    hid = (act * up).astype(BF16)
    both_ref[:, hidden:] = (grad * act).astype(BF16)
    both_ref[:, :hidden] = (grad * up * sig * (1.0 + gate * (1.0 - sig))).astype(BF16)
    by_rows = (((0,), (0,)), ((), ()))
    term_ref[2] = lax.dot_general(dy_proj, hid, by_rows, preferred_element_type=F32)
    term_ref[0] = lax.dot_general(
        x_proj, both_ref[:, :hidden], by_rows, preferred_element_type=F32
    )
    term_ref[1] = lax.dot_general(
        x_proj, both_ref[:, hidden:], by_rows, preferred_element_type=F32
    )
    high, low = where_ref[0], where_ref[1]
    n_term, rank, _ = term_ref.shape
    part = rank // n_piece
    for k, out in enumerate(part_refs):
        column = jnp.bitwise_and(low + k, 3)
        for h in range(2):
            first = (jnp.bitwise_and(high + h, 1) * 4 + column) * part
            for n in range(n_term):
                out[h, n] = term_ref[n, pl.ds(pl.multiple_of(first, part), part), :].astype(
                    out.dtype
                )


def core(where, got, pre, pieces, hidden, rank):
    slots = pre.shape[0]
    n_piece = len(pieces)
    width = n_piece * LANES
    part = rank // n_piece
    return pl.pallas_call(
        functools.partial(core_kernel, n_piece, hidden),
        in_specs=[pl.BlockSpec(memory_space=pltpu.SMEM)]
        + [pl.BlockSpec(memory_space=pl.ANY)] * (2 + n_piece),
        out_shape=(
            jax.ShapeDtypeStruct((slots, 2 * hidden), BF16),
            *(
                jax.ShapeDtypeStruct((2, 3, part, hidden), F32 if k == 0 else BF16)
                for k in range(4)
            ),
        ),
        scratch_shapes=[
            pltpu.VMEM(got.shape, BF16),
            pltpu.VMEM(pre.shape, BF16),
            pltpu.VMEM((width, hidden + rank), BF16),
            pltpu.VMEM(got.shape, F32),
            pltpu.VMEM((slots, width), BF16),
            pltpu.VMEM((slots, width), BF16),
            pltpu.VMEM((3, rank, hidden), F32),
            pltpu.SemaphoreType.DMA((n_piece + 2,)),
        ],
        name="core",
    )(where, got, pre, *pieces)


def rows_kernel(n_piece, first, *refs):
    where_ref, both_ref = refs[:2]
    pieces = refs[2 : 2 + n_piece]
    row_ref, weights, wide, sems = refs[2 + n_piece :]
    slots = both_ref.shape[0]
    copies = fetch_pieces(where_ref, pieces, pl.ds(first, weights.shape[1]), weights, sems)
    for copy in copies:
        copy.wait()
    for c in range(0, n_piece, 2):
        rows = lax.dot_general(
            both_ref[...],
            weights[c * LANES : (c + 2) * LANES, :],
            (((1,), (1,)), ((), ())),
            preferred_element_type=F32,
        )
        wide[chunk_rows(c, slots, n_piece), :] = rows[:, :LANES]
        wide[chunk_rows(c + 1, slots, n_piece), :] = rows[:, LANES:]
    row_ref[...] = wide[...].astype(BF16)


def row_grads(where, both, pieces, first):
    slots, inner = both.shape
    n_piece = len(pieces)
    rows = slots * n_piece
    return pl.pallas_call(
        functools.partial(rows_kernel, n_piece, first),
        in_specs=[pl.BlockSpec(memory_space=pltpu.SMEM), pl.BlockSpec(memory_space=pltpu.VMEM)]
        + [pl.BlockSpec(memory_space=pl.ANY)] * n_piece,
        out_shape=jax.ShapeDtypeStruct((rows, LANES), BF16),
        scratch_shapes=[
            pltpu.VMEM((n_piece * LANES, inner), BF16),
            pltpu.VMEM((rows, LANES), F32),
            pltpu.SemaphoreType.DMA((n_piece,)),
        ],
        name="row_grads",
    )(where, both, *pieces)


def take_pair(wide_ref, first, second, slots, step):
    return jnp.concatenate(
        [
            wide_ref[chunk_rows(first, slots, step), :],
            wide_ref[chunk_rows(second, slots, step), :],
        ],
        axis=1,
    ).astype(BF16)


def combine_kernel(match_ref, got_ref, out_ref, wide_ref):
    slots = match_ref.shape[0]
    n_chunk = out_ref.shape[1] // LANES
    wide_ref[...] = got_ref[...].astype(F32)
    for c in range(0, n_chunk, 2):
        rows = take_pair(wide_ref, c, c + 1, slots, n_chunk)
        total = lax.dot_general(
            match_ref[...], rows, (((0,), (0,)), ((), ())), preferred_element_type=F32
        )
        out_ref[:, c * LANES : (c + 2) * LANES] = total.astype(BF16)


def combine(match, got, width):
    n_tok = match.shape[1]
    return pl.pallas_call(
        combine_kernel,
        out_shape=jax.ShapeDtypeStruct((n_tok, width), BF16),
        scratch_shapes=[pltpu.VMEM(got.shape, F32)],
        name="combine",
    )(match, got)


def swap(value):
    return lax.ppermute(value, "dp_0", [(0, 1), (1, 0)])


def shifted(value):
    size = lax.axis_size("dp_1")
    return [
        lax.ppermute(value, "dp_1", [(i, (i + k) % size) for i in range(size)])
        for k in range(1, size)
    ]


def exchange(value, n_owner):
    rows, lanes = value.shape
    out = lax.all_to_all(
        value.reshape(n_owner, rows // n_owner, lanes), "expert", 0, 0, tiled=True
    )
    return out.reshape(rows, lanes)


def body(
    tokens, out_grad, expert_ids, gate_probs, saved_pre, gate_weight, up_weight, down_weight, basis
):
    n_owner = lax.axis_size("expert")
    width = tokens.shape[1]
    slots = saved_pre.shape[2]
    cap = slots // n_owner
    hidden = gate_weight.shape[2]
    where = jnp.stack([lax.axis_index("dp_0"), lax.axis_index("dp_1")]).astype(jnp.int32)

    own = jnp.concatenate([down_weight[0], basis[0], gate_weight[0], up_weight[0]], axis=1)
    far = swap(own)
    sent, match = pack(expert_ids.T, gate_probs.T, tokens, out_grad, n_owner, cap)
    got = exchange(sent, n_owner)
    owns = [own] + shifted(own)
    fars = [far] + shifted(far)
    pieces = [piece for pair in zip(owns, fars) for piece in pair]
    rank = basis.shape[2]
    both, *parts = core(where, got, saved_pre[0, 0], pieces, hidden, rank)
    size = lax.axis_size("dp_1")
    summed = parts[0]
    for k in range(1, size):
        part = lax.ppermute(parts[k], "dp_1", [(i, (i + k) % size) for i in range(size)])
        summed = summed + part.astype(F32)
    row_grad = row_grads(where, both, pieces, hidden + rank)
    back = exchange(row_grad, n_owner)
    other = swap(summed[1].astype(BF16))
    proj_grads = (summed[0] + other.astype(F32))[None]
    in_grad = combine(match, back, width)
    return in_grad, proj_grads


def solution(mesh):
    finer = Mesh(mesh.devices.reshape(2, 4, mesh.shape["expert"]), DP_EXPERT)
    placed = (
        P(DP_EXPERT, None),
        P(DP_EXPERT, None),
        P(DP_EXPERT, None),
        P(DP_EXPERT, None),
        P(DP, "expert", None, None),
        P("expert", DP, None),
        P("expert", DP, None),
        P("expert", DP, None),
        P("expert", DP, None),
    )
    return jax.shard_map(
        body,
        mesh=finer,
        in_specs=placed,
        out_specs=(P(DP_EXPERT, None), P("expert", None, DP, None)),
        check_vma=False,
    )
```

time: 189 us -> 186 us (0.984)
  the two profiles are of different devices: /device:TPU:17 before, /device:TPU:23 now
where the time goes in v2:
time: 186 us; the launch traced here: 185 us
  starting transfers between devices  80.5 us (43%)
  waiting for transfers between devices  78.2 us (42%)
  Pallas kernels  20.8 us (11%)
  local copies, waits for them, and re-layouts  3.07 us (2%)
    all_to_all x2, starting transfers between devices, exchange(): lax.all_to_all(value.reshape(n_owner, rows // n_owner, lanes), 'expert',...  44.8 us
    ppermute x2, waiting for transfers between devices, swap(): return lax.ppermute(value, 'dp_0', [(0, 1), (1, 0)])  39.1 us
    ppermute x6, waiting for transfers between devices, shifted(): lax.ppermute(value, 'dp_1', [(i, (i + k) % size) for i in range(size)])  24.9 us
    ppermute x6, starting transfers between devices, shifted(): lax.ppermute(value, 'dp_1', [(i, (i + k) % size) for i in range(size)])  17.8 us
    ppermute x3, waiting for transfers between devices, body(): lax.ppermute(parts[k], 'dp_1', [(i, (i + k) % size) for i in range(size)])  14.2 us
    ppermute x2, starting transfers between devices, swap(): return lax.ppermute(value, 'dp_0', [(0, 1), (1, 0)])  9.19 us
    ppermute x3, starting transfers between devices, body(): lax.ppermute(parts[k], 'dp_1', [(i, (i + k) % size) for i in range(size)])  8.67 us
    pallas_call x1, Pallas kernels, core(): pl.pallas_call(functools.partial(core_kernel, n_piece, hidden), in_specs=...  8.39 us
  transfers between devices with their start and end apart: 13, of which 7 were waited for; matrix products, arithmetic and copies ran while one was open for 1% of the time, Pallas kernels for 0%

profile of v2, /device:TPU:23, one launch (start us, length us, event | category | flops | bytes accessed | tf_op | source)
XLA Modules:
  0.0 185.1 jit_solution(5046959146241803751)
XLA Ops:
  0.6 3.9 %pack.1 = (bf16[7168,128]{1,0:T(8,128)(2,1)}, bf16[448,128]{1,0:T(8,128)(2,1)}) custom-call(s32[3,128]{1,0:T(4,128)} %bitcast.32, f32[3,128]{1,0:T(4,128)} %bitcast.33, bf16[128,1024]{1,0:T(8,128)(2,1)} %tok_ref.1, bf16[128,1024]{1,0:T(8,128)(2,1)} %grad_ref.1), custom_call_target="tpu_custom_call" | custom-call | tf_op jit(solution)/shard_map/pack/pallas_call | solution.py:67
  4.6 14.7 %all-to-all-start = ((bf16[64,112,128]{2,1,0:T(8,128)(2,1)}), bf16[64,112,128]{2,1,0:T(8,128)(2,1)S(1)}, u32[]{:S(2)}, u32[]{:S(2)}) async-start(bf16[64,112,128]{2,1,0:T(8,128)(2,1)} %bitcast.26), calls=%async_computation | async-start | bytes 3670016 | tf_op jit(solution)/shard_map/all_to_all | solution.py:267
  19.4 4.8 %collective-permute-start = (bf16[128,2560]{1,0:T(8,128)(2,1)S(1)}, bf16[128,2560]{1,0:T(8,128)(2,1)S(1)}, u32[]{:S(2)}, u32[]{:S(2)}) collective-permute-start(bf16[128,2560]{1,0:T(8,128)(2,1)S(1)} %pad_maximum_fusion.refs_3_.refs_2_), channel_id=1, source_target_pairs={{0,256},{256,0},{1,257},{257,1},{2,258},{258,2},{3,259},{259,3},{4... | collective-permute-start | bytes 1966088 | tf_op jit(solution)/shard_map/ppermute | solution.py:254
  24.1 2.5 %collective-permute-start.5 = (bf16[128,2560]{1,0:T(8,128)(2,1)S(1)}, bf16[128,2560]{1,0:T(8,128)(2,1)S(1)}, u32[]{:S(2)}, u32[]{:S(2)}) collective-permute-start(bf16[128,2560]{1,0:T(8,128)(2,1)S(1)} %pad_maximum_fusion.refs_3_.refs_2_), channel_id=1, source_target_pairs={{0,192},{64,0},{128,64},{192,128},{1,193},{65,1},{129,65},{193,129... | collective-permute-start | bytes 1966088 | tf_op jit(solution)/shard_map/ppermute | solution.py:260
  26.6 2.7 %collective-permute-start.3 = (bf16[128,2560]{1,0:T(8,128)(2,1)S(1)}, bf16[128,2560]{1,0:T(8,128)(2,1)}, u32[]{:S(2)}, u32[]{:S(2)}) collective-permute-start(bf16[128,2560]{1,0:T(8,128)(2,1)S(1)} %pad_maximum_fusion.refs_3_.refs_2_), channel_id=1, source_target_pairs={{0,128},{64,192},{128,0},{192,64},{1,129},{65,193},{129,1},{193,65... | collective-permute-start | bytes 1966088 | tf_op jit(solution)/shard_map/ppermute | solution.py:260
  29.4 3.7 %collective-permute-start.1 = (bf16[128,2560]{1,0:T(8,128)(2,1)S(1)}, bf16[128,2560]{1,0:T(8,128)(2,1)}, u32[]{:S(2)}, u32[]{:S(2)}) collective-permute-start(bf16[128,2560]{1,0:T(8,128)(2,1)S(1)} %pad_maximum_fusion.refs_3_.refs_2_), channel_id=1, source_target_pairs={{0,64},{64,128},{128,192},{192,0},{1,65},{65,129},{129,193},{193,1... | collective-permute-start | bytes 1966088 | tf_op jit(solution)/shard_map/ppermute | solution.py:260
  33.1 29.0 %collective-permute-done.refs_4_.refs_3_ = bf16[128,2560]{1,0:T(8,128)(2,1)S(1)} collective-permute-done((bf16[128,2560]{1,0:T(8,128)(2,1)S(1)}, bf16[128,2560]{1,0:T(8,128)(2,1)S(1)}, u32[]{:S(2)}, u32[]{:S(2)}) %collective-permute-start) | collective-permute-done | bytes 655392 | tf_op jit(solution)/shard_map/ppermute | solution.py:254
  62.1 2.4 %collective-permute-start.6 = (bf16[128,2560]{1,0:T(8,128)(2,1)S(1)}, bf16[128,2560]{1,0:T(8,128)(2,1)}, u32[]{:S(2)}, u32[]{:S(2)}) collective-permute-start(bf16[128,2560]{1,0:T(8,128)(2,1)S(1)} %collective-permute-done.refs_4_.refs_3_), channel_id=1, source_target_pairs={{0,192},{64,0},{128,64},{192,128},{1,193},{65,1},{129,65},{193,129... | collective-permute-start | bytes 1966088 | tf_op jit(solution)/shard_map/ppermute | solution.py:260
  64.6 2.7 %collective-permute-start.4 = (bf16[128,2560]{1,0:T(8,128)(2,1)S(1)}, bf16[128,2560]{1,0:T(8,128)(2,1)}, u32[]{:S(2)}, u32[]{:S(2)}) collective-permute-start(bf16[128,2560]{1,0:T(8,128)(2,1)S(1)} %collective-permute-done.refs_4_.refs_3_), channel_id=1, source_target_pairs={{0,128},{64,192},{128,0},{192,64},{1,129},{65,193},{129,1},{193,65... | collective-permute-start | bytes 1966088 | tf_op jit(solution)/shard_map/ppermute | solution.py:260
  68.2 3.7 %collective-permute-start.2 = (bf16[128,2560]{1,0:T(8,128)(2,1)S(1)}, bf16[128,2560]{1,0:T(8,128)(2,1)}, u32[]{:S(2)}, u32[]{:S(2)}) collective-permute-start(bf16[128,2560]{1,0:T(8,128)(2,1)S(1)} %collective-permute-done.refs_4_.refs_3_), channel_id=1, source_target_pairs={{0,64},{64,128},{128,192},{192,0},{1,65},{65,129},{129,193},{193,1... | collective-permute-start | bytes 1966088 | tf_op jit(solution)/shard_map/ppermute | solution.py:260
  72.5 22.4 %collective-permute-done.6.refs_10_.refs_9_ = bf16[128,2560]{1,0:T(8,128)(2,1)} collective-permute-done((bf16[128,2560]{1,0:T(8,128)(2,1)S(1)}, bf16[128,2560]{1,0:T(8,128)(2,1)}, u32[]{:S(2)}, u32[]{:S(2)}) %collective-permute-start.6) | collective-permute-done | bytes 655392 | tf_op jit(solution)/shard_map/ppermute | solution.py:260
  94.9 2.4 %collective-permute-done.2.refs_6_.refs_5_ = bf16[128,2560]{1,0:T(8,128)(2,1)} collective-permute-done((bf16[128,2560]{1,0:T(8,128)(2,1)S(1)}, bf16[128,2560]{1,0:T(8,128)(2,1)}, u32[]{:S(2)}, u32[]{:S(2)}) %collective-permute-start.2) | collective-permute-done | bytes 655392 | tf_op jit(solution)/shard_map/ppermute | solution.py:260
  98.6 8.4 %core.1 = (bf16[448,1536]{1,0:T(8,128)(2,1)}, f32[2,3,32,768]{3,2,1,0:T(8,128)}, bf16[2,3,32,768]{3,2,1,0:T(8,128)(2,1)}, bf16[2,3,32,768]{3,2,1,0:T(8,128)(2,1)}, bf16[2,3,32,768]{3,2,1,0:T(8,128)(2,1)}) custom-call(s32[2]{0:T(128)} %pad_add_fusion.refs_0_, bf16[7168,128]{1,0:T(8,128)(2,1)} %bitcast.23, bf16[448,1536]{1,0:T(8,128)(2,1)} %bitcast.27, ...), custom_call_target="tpu_custom_call" | custom-call | tf_op jit(solution)/shard_map/core/pallas_call | solution.py:158
  107.0 5.9 %row_grads.1 = bf16[3584,128]{1,0:T(8,128)(2,1)} custom-call(s32[2]{0:T(128)} %pad_add_fusion.refs_0_, bf16[448,1536]{1,0:T(8,128)(2,1)} %get-tuple-element.11.refs_1_, bf16[128,2560]{1,0:T(8,128)(2,1)} %copy-done.1, bf16[128,2560]{1,0:T(8,128)(2,1)} %copy-done.3, bf16[128,2560]{1,0:T(8,128)(2,1)} %collective-permute-done.1.refs_5_.refs_4_, ...), custom_call_target="tpu_custom_call" | custom-call | tf_op jit(solution)/shard_map/row_grads/pallas_call | solution.py:207
  113.0 30.2 %all-to-all-start.1 = ((bf16[64,56,128]{2,1,0:T(8,128)(2,1)}), bf16[64,56,128]{2,1,0:T(8,128)(2,1)S(1)}, u32[]{:S(2)}, u32[]{:S(2)}) async-start(bf16[64,56,128]{2,1,0:T(8,128)(2,1)} %bitcast.25), calls=%async_computation.1 | async-start | bytes 1835008 | tf_op jit(solution)/shard_map/all_to_all | solution.py:267
  143.2 4.3 %collective-permute-start.7 = (bf16[2,3,32,768]{3,2,1,0:T(8,128)(2,1)S(1)}, bf16[2,3,32,768]{3,2,1,0:T(8,128)(2,1)S(1)}, u32[]{:S(2)}, u32[]{:S(2)}) collective-permute-start(bf16[2,3,32,768]{3,2,1,0:T(8,128)(2,1)S(1)} %copy-done.12), channel_id=1, source_target_pairs={{0,64},{64,128},{128,192},{192,0},{1,65},{65,129},{129,193},{193,1... | collective-permute-start | bytes 884744 | tf_op jit(solution)/shard_map/ppermute | solution.py:295
  147.5 1.9 %collective-permute-start.8 = (bf16[2,3,32,768]{3,2,1,0:T(8,128)(2,1)S(1)}, bf16[2,3,32,768]{3,2,1,0:T(8,128)(2,1)S(1)}, u32[]{:S(2)}, u32[]{:S(2)}) collective-permute-start(bf16[2,3,32,768]{3,2,1,0:T(8,128)(2,1)S(1)} %copy-done.11), channel_id=1, source_target_pairs={{0,128},{64,192},{128,0},{192,64},{1,129},{65,193},{129,1},{193,65... | collective-permute-start | bytes 884744 | tf_op jit(solution)/shard_map/ppermute | solution.py:295
  149.4 2.5 %collective-permute-start.9 = (bf16[2,3,32,768]{3,2,1,0:T(8,128)(2,1)S(1)}, bf16[2,3,32,768]{3,2,1,0:T(8,128)(2,1)S(1)}, u32[]{:S(2)}, u32[]{:S(2)}) collective-permute-start(bf16[2,3,32,768]{3,2,1,0:T(8,128)(2,1)S(1)} %copy-done.10), channel_id=1, source_target_pairs={{0,192},{64,0},{128,64},{192,128},{1,193},{65,1},{129,65},{193,129... | collective-permute-start | bytes 884744 | tf_op jit(solution)/shard_map/ppermute | solution.py:295
  151.9 2.2 %collective-permute-done.7 = bf16[2,3,32,768]{3,2,1,0:T(8,128)(2,1)S(1)} collective-permute-done((bf16[2,3,32,768]{3,2,1,0:T(8,128)(2,1)S(1)}, bf16[2,3,32,768]{3,2,1,0:T(8,128)(2,1)S(1)}, u32[]{:S(2)}, u32[]{:S(2)}) %collective-permute-start.7) | collective-permute-done | bytes 294944 | tf_op jit(solution)/shard_map/ppermute | solution.py:295
  154.1 4.7 %collective-permute-done.8 = bf16[2,3,32,768]{3,2,1,0:T(8,128)(2,1)S(1)} collective-permute-done((bf16[2,3,32,768]{3,2,1,0:T(8,128)(2,1)S(1)}, bf16[2,3,32,768]{3,2,1,0:T(8,128)(2,1)S(1)}, u32[]{:S(2)}, u32[]{:S(2)}) %collective-permute-start.8) | collective-permute-done | bytes 294944 | tf_op jit(solution)/shard_map/ppermute | solution.py:295
  158.8 7.3 %collective-permute-done.9 = bf16[2,3,32,768]{3,2,1,0:T(8,128)(2,1)S(1)} collective-permute-done((bf16[2,3,32,768]{3,2,1,0:T(8,128)(2,1)S(1)}, bf16[2,3,32,768]{3,2,1,0:T(8,128)(2,1)S(1)}, u32[]{:S(2)}, u32[]{:S(2)}) %collective-permute-start.9) | collective-permute-done | bytes 294944 | tf_op jit(solution)/shard_map/ppermute | solution.py:295
  166.3 4.4 %collective-permute-start.10 = (bf16[3,32,768]{2,1,0:T(8,128)(2,1)S(1)}, bf16[3,32,768]{2,1,0:T(8,128)(2,1)S(1)}, u32[]{:S(2)}, u32[]{:S(2)}) collective-permute-start(bf16[3,32,768]{2,1,0:T(8,128)(2,1)S(1)} %fusion.2), channel_id=1, source_target_pairs={{0,256},{256,0},{1,257},{257,1},{2,258},{258,2},{3,259},{259,3},{4... | collective-permute-start | bytes 442376 | tf_op jit(solution)/shard_map/ppermute | solution.py:254
  170.7 10.1 %collective-permute-done.10 = bf16[3,32,768]{2,1,0:T(8,128)(2,1)S(1)} collective-permute-done((bf16[3,32,768]{2,1,0:T(8,128)(2,1)S(1)}, bf16[3,32,768]{2,1,0:T(8,128)(2,1)S(1)}, u32[]{:S(2)}, u32[]{:S(2)}) %collective-permute-start.10) | collective-permute-done | bytes 147488 | tf_op jit(solution)/shard_map/ppermute | solution.py:254
  182.5 2.5 %combine.1 = bf16[128,1024]{1,0:T(8,128)(2,1)} custom-call(bf16[448,128]{1,0:T(8,128)(2,1)} %get-tuple-element.9.match_ref, bf16[3584,128]{1,0:T(8,128)(2,1)} %bitcast.24), custom_call_target="tpu_custom_call" | custom-call | tf_op jit(solution)/shard_map/combine/pallas_call | solution.py:245
  (37 shorter events, 4.6 us)
Async XLA Ops:
  4.6 14.7 %copy-start.6 = (bf16[1,128,768]{2,1,0:T(8,128)(2,1)S(1)}, bf16[1,128,768]{2,1,0:T(8,128)(2,1)}, u32[]{:S(2)}) copy-start(bf16[1,128,768]{2,1,0:T(8,128)(2,1)} %param.15) | copy-start | bytes 589828
  4.6 14.7 %copy-start.7 = (bf16[1,128,768]{2,1,0:T(8,128)(2,1)S(1)}, bf16[1,128,768]{2,1,0:T(8,128)(2,1)}, u32[]{:S(2)}) copy-start(bf16[1,128,768]{2,1,0:T(8,128)(2,1)} %param.14) | copy-start | bytes 589828
  4.6 14.7 %copy-start.8 = (bf16[1,128,768]{2,1,0:T(8,128)(2,1)S(1)}, bf16[1,128,768]{2,1,0:T(8,128)(2,1)}, u32[]{:S(2)}) copy-start(bf16[1,128,768]{2,1,0:T(8,128)(2,1)} %param.16) | copy-start | bytes 589828
  4.6 14.7 %copy-start.9 = (bf16[1,128,256]{2,1,0:T(8,128)(2,1)S(1)}, bf16[1,128,256]{2,1,0:T(8,128)(2,1)}, u32[]{:S(2)}) copy-start(bf16[1,128,256]{2,1,0:T(8,128)(2,1)} %param.17) | copy-start | bytes 196612
  4.6 92.8 %all-to-all-start = ((bf16[64,112,128]{2,1,0:T(8,128)(2,1)}), bf16[64,112,128]{2,1,0:T(8,128)(2,1)S(1)}, u32[]{:S(2)}, u32[]{:S(2)}) async-start(bf16[64,112,128]{2,1,0:T(8,128)(2,1)} %bitcast.26), calls=%async_computation | async-start | bytes 3670016 | tf_op jit(solution)/shard_map/all_to_all | solution.py:267
  19.4 78.0 %copy-start.1 = (bf16[128,2560]{1,0:T(8,128)(2,1)}, bf16[128,2560]{1,0:T(8,128)(2,1)S(1)}, u32[]{:S(2)}) copy-start(bf16[128,2560]{1,0:T(8,128)(2,1)S(1)} %pad_maximum_fusion.refs_3_.refs_2_) | copy-start | bytes 1966084
  19.4 42.7 %collective-permute-start = (bf16[128,2560]{1,0:T(8,128)(2,1)S(1)}, bf16[128,2560]{1,0:T(8,128)(2,1)S(1)}, u32[]{:S(2)}, u32[]{:S(2)}) collective-permute-start(bf16[128,2560]{1,0:T(8,128)(2,1)S(1)} %pad_maximum_fusion.refs_3_.refs_2_), channel_id=1, source_target_pairs={{0,256},{256,0},{1,257},{257,1},{2,258},{258,2},{3,259},{259,3},{4... | collective-permute-start | bytes 1966088 | tf_op jit(solution)/shard_map/ppermute | solution.py:254
  24.1 43.2 %collective-permute-start.5 = (bf16[128,2560]{1,0:T(8,128)(2,1)S(1)}, bf16[128,2560]{1,0:T(8,128)(2,1)S(1)}, u32[]{:S(2)}, u32[]{:S(2)}) collective-permute-start(bf16[128,2560]{1,0:T(8,128)(2,1)S(1)} %pad_maximum_fusion.refs_3_.refs_2_), channel_id=1, source_target_pairs={{0,192},{64,0},{128,64},{192,128},{1,193},{65,1},{129,65},{193,129... | collective-permute-start | bytes 1966088 | tf_op jit(solution)/shard_map/ppermute | solution.py:260
  26.6 45.9 %collective-permute-start.3 = (bf16[128,2560]{1,0:T(8,128)(2,1)S(1)}, bf16[128,2560]{1,0:T(8,128)(2,1)}, u32[]{:S(2)}, u32[]{:S(2)}) collective-permute-start(bf16[128,2560]{1,0:T(8,128)(2,1)S(1)} %pad_maximum_fusion.refs_3_.refs_2_), channel_id=1, source_target_pairs={{0,128},{64,192},{128,0},{192,64},{1,129},{65,193},{129,1},{193,65... | collective-permute-start | bytes 1966088 | tf_op jit(solution)/shard_map/ppermute | solution.py:260
  29.4 43.1 %collective-permute-start.1 = (bf16[128,2560]{1,0:T(8,128)(2,1)S(1)}, bf16[128,2560]{1,0:T(8,128)(2,1)}, u32[]{:S(2)}, u32[]{:S(2)}) collective-permute-start(bf16[128,2560]{1,0:T(8,128)(2,1)S(1)} %pad_maximum_fusion.refs_3_.refs_2_), channel_id=1, source_target_pairs={{0,64},{64,128},{128,192},{192,0},{1,65},{65,129},{129,193},{193,1... | collective-permute-start | bytes 1966088 | tf_op jit(solution)/shard_map/ppermute | solution.py:260
  62.1 35.3 %copy-start.3 = (bf16[128,2560]{1,0:T(8,128)(2,1)}, bf16[128,2560]{1,0:T(8,128)(2,1)S(1)}, u32[]{:S(2)}) copy-start(bf16[128,2560]{1,0:T(8,128)(2,1)S(1)} %collective-permute-done.refs_4_.refs_3_) | copy-start | bytes 1966084
  62.1 32.8 %collective-permute-start.6 = (bf16[128,2560]{1,0:T(8,128)(2,1)S(1)}, bf16[128,2560]{1,0:T(8,128)(2,1)}, u32[]{:S(2)}, u32[]{:S(2)}) collective-permute-start(bf16[128,2560]{1,0:T(8,128)(2,1)S(1)} %collective-permute-done.refs_4_.refs_3_), channel_id=1, source_target_pairs={{0,192},{64,0},{128,64},{192,128},{1,193},{65,1},{129,65},{193,129... | collective-permute-start | bytes 1966088 | tf_op jit(solution)/shard_map/ppermute | solution.py:260
  64.6 30.4 %collective-permute-start.4 = (bf16[128,2560]{1,0:T(8,128)(2,1)S(1)}, bf16[128,2560]{1,0:T(8,128)(2,1)}, u32[]{:S(2)}, u32[]{:S(2)}) collective-permute-start(bf16[128,2560]{1,0:T(8,128)(2,1)S(1)} %collective-permute-done.refs_4_.refs_3_), channel_id=1, source_target_pairs={{0,128},{64,192},{128,0},{192,64},{1,129},{65,193},{129,1},{193,65... | collective-permute-start | bytes 1966088 | tf_op jit(solution)/shard_map/ppermute | solution.py:260
  68.2 29.2 %collective-permute-start.2 = (bf16[128,2560]{1,0:T(8,128)(2,1)S(1)}, bf16[128,2560]{1,0:T(8,128)(2,1)}, u32[]{:S(2)}, u32[]{:S(2)}) collective-permute-start(bf16[128,2560]{1,0:T(8,128)(2,1)S(1)} %collective-permute-done.refs_4_.refs_3_), channel_id=1, source_target_pairs={{0,64},{64,128},{128,192},{192,0},{1,65},{65,129},{129,193},{193,1... | collective-permute-start | bytes 1966088 | tf_op jit(solution)/shard_map/ppermute | solution.py:260
  97.4 1.2 copy-start
  113.0 30.2 %copy-start.12 = (bf16[2,3,32,768]{3,2,1,0:T(8,128)(2,1)S(1)}, bf16[2,3,32,768]{3,2,1,0:T(8,128)(2,1)}, u32[]{:S(2)}) copy-start(bf16[2,3,32,768]{3,2,1,0:T(8,128)(2,1)} %get-tuple-element.13) | copy-start | bytes 884740
  113.0 34.5 %copy-start.11 = (bf16[2,3,32,768]{3,2,1,0:T(8,128)(2,1)S(1)}, bf16[2,3,32,768]{3,2,1,0:T(8,128)(2,1)}, u32[]{:S(2)}) copy-start(bf16[2,3,32,768]{3,2,1,0:T(8,128)(2,1)} %get-tuple-element.14) | copy-start | bytes 884740
  113.0 36.4 %copy-start.10 = (bf16[2,3,32,768]{3,2,1,0:T(8,128)(2,1)S(1)}, bf16[2,3,32,768]{3,2,1,0:T(8,128)(2,1)}, u32[]{:S(2)}) copy-start(bf16[2,3,32,768]{3,2,1,0:T(8,128)(2,1)} %get-tuple-element.15) | copy-start | bytes 884740
  113.0 53.1 %copy-start.5 = (f32[2,3,32,768]{3,2,1,0:T(8,128)S(1)}, f32[2,3,32,768]{3,2,1,0:T(8,128)}, u32[]{:S(2)}) copy-start(f32[2,3,32,768]{3,2,1,0:T(8,128)} %get-tuple-element.12) | copy-start | bytes 1769476
  113.0 68.6 %all-to-all-start.1 = ((bf16[64,56,128]{2,1,0:T(8,128)(2,1)}), bf16[64,56,128]{2,1,0:T(8,128)(2,1)S(1)}, u32[]{:S(2)}, u32[]{:S(2)}) async-start(bf16[64,56,128]{2,1,0:T(8,128)(2,1)} %bitcast.25), calls=%async_computation.1 | async-start | bytes 1835008 | tf_op jit(solution)/shard_map/all_to_all | solution.py:267
  143.2 10.9 %collective-permute-start.7 = (bf16[2,3,32,768]{3,2,1,0:T(8,128)(2,1)S(1)}, bf16[2,3,32,768]{3,2,1,0:T(8,128)(2,1)S(1)}, u32[]{:S(2)}, u32[]{:S(2)}) collective-permute-start(bf16[2,3,32,768]{3,2,1,0:T(8,128)(2,1)S(1)} %copy-done.12), channel_id=1, source_target_pairs={{0,64},{64,128},{128,192},{192,0},{1,65},{65,129},{129,193},{193,1... | collective-permute-start | bytes 884744 | tf_op jit(solution)/shard_map/ppermute | solution.py:295
  147.5 11.3 %collective-permute-start.8 = (bf16[2,3,32,768]{3,2,1,0:T(8,128)(2,1)S(1)}, bf16[2,3,32,768]{3,2,1,0:T(8,128)(2,1)S(1)}, u32[]{:S(2)}, u32[]{:S(2)}) collective-permute-start(bf16[2,3,32,768]{3,2,1,0:T(8,128)(2,1)S(1)} %copy-done.11), channel_id=1, source_target_pairs={{0,128},{64,192},{128,0},{192,64},{1,129},{65,193},{129,1},{193,65... | collective-permute-start | bytes 884744 | tf_op jit(solution)/shard_map/ppermute | solution.py:295
  149.4 16.7 %collective-permute-start.9 = (bf16[2,3,32,768]{3,2,1,0:T(8,128)(2,1)S(1)}, bf16[2,3,32,768]{3,2,1,0:T(8,128)(2,1)S(1)}, u32[]{:S(2)}, u32[]{:S(2)}) collective-permute-start(bf16[2,3,32,768]{3,2,1,0:T(8,128)(2,1)S(1)} %copy-done.10), channel_id=1, source_target_pairs={{0,192},{64,0},{128,64},{192,128},{1,193},{65,1},{129,65},{193,129... | collective-permute-start | bytes 884744 | tf_op jit(solution)/shard_map/ppermute | solution.py:295
  166.3 14.6 %collective-permute-start.10 = (bf16[3,32,768]{2,1,0:T(8,128)(2,1)S(1)}, bf16[3,32,768]{2,1,0:T(8,128)(2,1)S(1)}, u32[]{:S(2)}, u32[]{:S(2)}) collective-permute-start(bf16[3,32,768]{2,1,0:T(8,128)(2,1)S(1)} %fusion.2), channel_id=1, source_target_pairs={{0,256},{256,0},{1,257},{257,1},{2,258},{258,2},{3,259},{259,3},{4... | collective-permute-start | bytes 442376 | tf_op jit(solution)/shard_map/ppermute | solution.py:254
  (2 other events, 1.8 us)

commit v3 on v2

v3 whole, which is shorter than its diff:
```python
import functools

import jax
import jax.numpy as jnp
from jax import lax
from jax.experimental import pallas as pl
from jax.experimental.pallas import tpu as pltpu
from jax.sharding import Mesh
from jax.sharding import PartitionSpec as P


DP = ("dp_0", "dp_1")
DP_EXPERT = ("dp_0", "dp_1", "expert")
F32 = jnp.float32
BF16 = jnp.bfloat16
LANES = 128


def chunk_rows(start, slots, step):
    return pl.ds(start, slots, stride=step)


def pack_kernel(cap, ids_ref, probs_ref, tok_ref, grad_ref, out_ref, match_ref, wide_ref):
    slots, n_tok = match_ref.shape
    topk = ids_ref.shape[0]
    n_owner = slots // cap
    ids = ids_ref[...]
    probs = probs_ref[...]
    owner = lax.broadcasted_iota(jnp.int32, (n_owner, n_tok), 0)
    named = [owner == ids[k : k + 1, :] for k in range(topk)]
    per_owner = sum(n.astype(F32) for n in named)
    earlier = (
        lax.broadcasted_iota(jnp.int32, (n_tok, n_tok), 0)
        < lax.broadcasted_iota(jnp.int32, (n_tok, n_tok), 1)
    ).astype(F32)
    before = jnp.dot(per_owner.astype(BF16), earlier.astype(BF16), preferred_element_type=F32)
    slot = lax.broadcasted_iota(jnp.int32, (slots, n_tok), 0)
    match = jnp.zeros((slots, n_tok), F32)
    weight = jnp.zeros((slots, n_tok), F32)
    for k in range(topk):
        position = jnp.sum(jnp.where(named[k], before, 0.0), axis=0, keepdims=True)
        here = slot == ids[k : k + 1, :] * cap + position.astype(jnp.int32)
        match = match + here.astype(F32)
        weight = weight + jnp.where(here, probs[k : k + 1, :], 0.0)
    weight = jnp.sum(weight, axis=1, keepdims=True)
    match = match.astype(BF16)
    match_ref[...] = match
    n_chunk = tok_ref.shape[1] // LANES
    for half, src in enumerate((tok_ref, grad_ref)):
        for c in range(0, n_chunk, 2):
            rows = jnp.dot(
                match, src[:, c * LANES : (c + 2) * LANES], preferred_element_type=F32
            )
            if half:
                rows = rows * weight
            for i in range(2):
                wide_ref[chunk_rows(half * n_chunk + c + i, slots, 2 * n_chunk), :] = rows[
                    :, i * LANES : (i + 1) * LANES
                ]
    out_ref[...] = wide_ref[...].astype(BF16)


def pack(ids, probs, tokens, out_grad, n_owner, cap):
    n_tok, width = tokens.shape
    slots = n_owner * cap
    rows = slots * 2 * width // LANES
    return pl.pallas_call(
        functools.partial(pack_kernel, cap),
        out_shape=(
            jax.ShapeDtypeStruct((rows, LANES), BF16),
            jax.ShapeDtypeStruct((slots, n_tok), BF16),
        ),
        scratch_shapes=[pltpu.VMEM((rows, LANES), F32)],
        name="pack",
    )(ids, probs, tokens, out_grad)


def near(value):
    return pltpu.with_memory_space_constraint(value, pltpu.VMEM)


def in_vmem():
    return pl.BlockSpec(memory_space=pltpu.VMEM)


def in_place():
    return pl.BlockSpec(memory_space=pl.ANY)


def fetch(where_ref, pieces, places, columns, into, sems, at):
    high, low = where_ref[0], where_ref[1]
    copies = []
    for i, (piece, (other, k, first)) in enumerate(zip(pieces, places)):
        block = jnp.bitwise_and(high + other, 1) * 4 + jnp.bitwise_and(low + 4 - k, 3)
        rows = pl.ds(pl.multiple_of(block * LANES + first, LANES // 2), piece.shape[0])
        copy = pltpu.make_async_copy(piece.at[:, columns], into.at[rows, :], sems.at[at + i])
        copy.start()
        copies.append(copy)
    return copies


def fetch_all(sources, targets, sems, at):
    copies = []
    for i, (source, target) in enumerate(zip(sources, targets)):
        copy = pltpu.make_async_copy(source, target, sems.at[at + i])
        copy.start()
        copies.append(copy)
    return copies


def slopes_kernel(pre_ref, act_ref, slope_ref, hid_ref):
    hidden = act_ref.shape[1]
    gate = pre_ref[:, :hidden].astype(F32)
    up = pre_ref[:, hidden:].astype(F32)
    sig = jax.nn.sigmoid(gate)
    act = gate * sig
    act_ref[...] = act
    slope_ref[...] = up * sig * (1.0 + gate * (1.0 - sig))
    hid_ref[...] = (act * up).astype(BF16)


def slopes(pre):
    slots, both = pre.shape
    hidden = both // 2
    return pl.pallas_call(
        slopes_kernel,
        out_shape=(
            jax.ShapeDtypeStruct((slots, hidden), F32),
            jax.ShapeDtypeStruct((slots, hidden), F32),
            jax.ShapeDtypeStruct((slots, hidden), BF16),
        ),
        name="slopes",
    )(pre)


def spread(wide_ref, first, step, into):
    slots, width = into.shape
    for c in range(width // LANES):
        into[:, c * LANES : (c + 1) * LANES] = wide_ref[
            chunk_rows(first + c, slots, step), :
        ].astype(BF16)


def grads_kernel(places, *refs):
    n = len(places)
    where_ref, got_ref, act_hbm, slope_hbm = refs[:4]
    pieces = refs[4 : 4 + n]
    row_ref, both_ref, proj_ref = refs[4 + n : 7 + n]
    wide, dy_rows, rows_wide, w1, w2, act, slope, sems = refs[7 + n :]
    hidden = act.shape[1]
    slots, width = dy_rows.shape
    n_chunk = width // LANES
    first = fetch(where_ref, pieces, places, pl.ds(0, w1.shape[1]), w1, sems, 0)
    middle = fetch_all((slope_hbm, act_hbm), (slope, act), sems, 2 * n)
    last = fetch(where_ref, pieces, places, pl.ds(w1.shape[1], w2.shape[1]), w2, sems, n)
    wide[...] = got_ref[...].astype(F32)
    spread(wide, n_chunk, 2 * n_chunk, dy_rows)
    for copy in first:
        copy.wait()
    grad = jnp.dot(dy_rows[...], w1[:, :hidden], preferred_element_type=F32)
    for copy in middle:
        copy.wait()
    both_ref[:, :hidden] = (grad * slope[...]).astype(BF16)
    both_ref[:, hidden:] = (grad * act[...]).astype(BF16)
    for copy in last:
        copy.wait()
    for c in range(0, n_chunk, 2):
        rows = lax.dot_general(
            both_ref[...],
            w2[c * LANES : (c + 2) * LANES, :],
            (((1,), (1,)), ((), ())),
            preferred_element_type=F32,
        )
        rows_wide[chunk_rows(c, slots, n_chunk), :] = rows[:, :LANES]
        rows_wide[chunk_rows(c + 1, slots, n_chunk), :] = rows[:, LANES:]
    row_ref[...] = rows_wide[...].astype(BF16)
    proj_ref[...] = jnp.dot(dy_rows[...], w1[:, hidden:], preferred_element_type=F32).astype(BF16)


def grads(where, got, act, slope, pieces, places, rank):
    slots, hidden = act.shape
    width = got.shape[0] * LANES // slots // 2
    rows = slots * width // LANES
    n = len(pieces)
    return pl.pallas_call(
        functools.partial(grads_kernel, places),
        in_specs=[pl.BlockSpec(memory_space=pltpu.SMEM), in_vmem()] + [in_place()] * (2 + n),
        out_shape=(
            jax.ShapeDtypeStruct((rows, LANES), BF16),
            jax.ShapeDtypeStruct((slots, 2 * hidden), BF16),
            jax.ShapeDtypeStruct((slots, rank), BF16),
        ),
        scratch_shapes=[
            pltpu.VMEM(got.shape, F32),
            pltpu.VMEM((slots, width), BF16),
            pltpu.VMEM((rows, LANES), F32),
            pltpu.VMEM((width, hidden + rank), BF16),
            pltpu.VMEM((width, 2 * hidden), BF16),
            pltpu.VMEM((slots, hidden), F32),
            pltpu.VMEM((slots, hidden), F32),
            pltpu.SemaphoreType.DMA((2 * n + 2,)),
        ],
        name="grads",
    )(where, near(got), act, slope, *pieces)


def terms_kernel(places, first_column, *refs):
    n = len(places)
    where_ref, got_hbm, both_hbm, proj_hbm, hid_hbm = refs[:5]
    pieces = refs[5 : 5 + n]
    part_refs = refs[5 + n : 9 + n]
    got, both, proj, hid, basis, wide, x_rows, term_ref, sems = refs[9 + n :]
    hidden = hid.shape[1]
    n_chunk = x_rows.shape[1] // LANES
    (first,) = fetch_all((got_hbm,), (got,), sems, n)
    middle = fetch(
        where_ref, pieces, places, pl.ds(first_column, basis.shape[1]), basis, sems, 0
    )
    last = fetch_all((both_hbm, proj_hbm, hid_hbm), (both, proj, hid), sems, n + 1)
    first.wait()
    wide[...] = got[...].astype(F32)
    spread(wide, 0, 2 * n_chunk, x_rows)
    for copy in middle:
        copy.wait()
    x_proj = jnp.dot(x_rows[...], basis[...], preferred_element_type=F32).astype(BF16)
    for copy in last:
        copy.wait()
    by_rows = (((0,), (0,)), ((), ()))
    term_ref[0] = lax.dot_general(x_proj, both[:, :hidden], by_rows, preferred_element_type=F32)
    term_ref[1] = lax.dot_general(x_proj, both[:, hidden:], by_rows, preferred_element_type=F32)
    term_ref[2] = lax.dot_general(proj[...], hid[...], by_rows, preferred_element_type=F32)
    high, low = where_ref[0], where_ref[1]
    n_term, rank, _ = term_ref.shape
    part = rank // n_chunk
    for k, out in enumerate(part_refs):
        column = jnp.bitwise_and(low + k, 3)
        for h in range(2):
            begin = (jnp.bitwise_and(high + h, 1) * 4 + column) * part
            for t in range(n_term):
                out[h, t] = term_ref[t, pl.ds(pl.multiple_of(begin, part), part), :].astype(
                    out.dtype
                )


def terms(where, got, both, proj, hid, pieces, places):
    slots, hidden = hid.shape
    rank = proj.shape[1]
    width = got.shape[0] * LANES // slots // 2
    part = rank * LANES // width
    n = len(pieces)
    return pl.pallas_call(
        functools.partial(terms_kernel, places, hidden),
        in_specs=[pl.BlockSpec(memory_space=pltpu.SMEM)] + [in_place()] * (4 + n),
        out_shape=tuple(
            jax.ShapeDtypeStruct((2, 3, part, hidden), F32 if k == 0 else BF16) for k in range(4)
        ),
        scratch_shapes=[
            pltpu.VMEM(got.shape, BF16),
            pltpu.VMEM(both.shape, BF16),
            pltpu.VMEM(proj.shape, BF16),
            pltpu.VMEM(hid.shape, BF16),
            pltpu.VMEM((width, rank), BF16),
            pltpu.VMEM(got.shape, F32),
            pltpu.VMEM((slots, width), BF16),
            pltpu.VMEM((3, rank, hidden), F32),
            pltpu.SemaphoreType.DMA((n + 4,)),
        ],
        name="terms",
    )(where, got, both, proj, hid, *pieces)


def take_pair(wide_ref, first, second, slots, step):
    return jnp.concatenate(
        [
            wide_ref[chunk_rows(first, slots, step), :],
            wide_ref[chunk_rows(second, slots, step), :],
        ],
        axis=1,
    ).astype(BF16)


def combine_kernel(match_ref, got_ref, out_ref, wide_ref):
    slots = match_ref.shape[0]
    n_chunk = out_ref.shape[1] // LANES
    wide_ref[...] = got_ref[...].astype(F32)
    for c in range(0, n_chunk, 2):
        rows = take_pair(wide_ref, c, c + 1, slots, n_chunk)
        total = lax.dot_general(
            match_ref[...], rows, (((0,), (0,)), ((), ())), preferred_element_type=F32
        )
        out_ref[:, c * LANES : (c + 2) * LANES] = total.astype(BF16)


def combine(match, got, width):
    n_tok = match.shape[1]
    return pl.pallas_call(
        combine_kernel,
        out_shape=jax.ShapeDtypeStruct((n_tok, width), BF16),
        scratch_shapes=[pltpu.VMEM(got.shape, F32)],
        name="combine",
    )(match, near(got))


def swap(value):
    return lax.ppermute(value, "dp_0", [(0, 1), (1, 0)])


def shifted(value, k):
    size = lax.axis_size("dp_1")
    return lax.ppermute(value, "dp_1", [(i, (i + k) % size) for i in range(size)])


def exchange(value, n_owner):
    rows, lanes = value.shape
    out = lax.all_to_all(
        value.reshape(n_owner, rows // n_owner, lanes), "expert", 0, 0, tiled=True
    )
    return out.reshape(rows, lanes)


def body(
    tokens, out_grad, expert_ids, gate_probs, saved_pre, gate_weight, up_weight, down_weight, basis
):
    n_owner = lax.axis_size("expert")
    width = tokens.shape[1]
    slots = saved_pre.shape[2]
    cap = slots // n_owner
    where = jnp.stack([lax.axis_index("dp_0"), lax.axis_index("dp_1")]).astype(jnp.int32)

    own = jnp.concatenate([down_weight[0], basis[0], gate_weight[0], up_weight[0]], axis=1)
    far = swap(own)
    sent, match = pack(expert_ids.T, gate_probs.T, tokens, out_grad, n_owner, cap)
    got = exchange(sent, n_owner)
    pieces, places = [], []
    half = own.shape[0] // 2
    for other, block in enumerate((own, far)):
        left, right = shifted(block, 1), shifted(block, -1)
        top, bottom = shifted(left[:half], 1), shifted(right[half:], -1)
        pieces += [block, left, right, top, bottom]
        places += [(other, 0, 0), (other, 1, 0), (other, 3, 0), (other, 2, 0), (other, 2, half)]
    rank = basis.shape[2]
    act, slope, hid = slopes(saved_pre[0, 0])
    places = tuple(places)
    row_grad, both, proj = grads(where, got, act, slope, pieces, places, rank)
    back = exchange(row_grad, n_owner)
    parts = terms(where, got, both, proj, hid, pieces, places)
    size = lax.axis_size("dp_1")
    summed = parts[0]
    for k in range(1, size):
        summed = summed + shifted(parts[k], k).astype(F32)
    other = swap(summed[1].astype(BF16))
    proj_grads = (summed[0] + other.astype(F32))[None]
    in_grad = combine(match, back, width)
    return in_grad, proj_grads


def solution(mesh):
    finer = Mesh(mesh.devices.reshape(2, 4, mesh.shape["expert"]), DP_EXPERT)
    placed = (
        P(DP_EXPERT, None),
        P(DP_EXPERT, None),
        P(DP_EXPERT, None),
        P(DP_EXPERT, None),
        P(DP, "expert", None, None),
        P("expert", DP, None),
        P("expert", DP, None),
        P("expert", DP, None),
        P("expert", DP, None),
    )
    return jax.shard_map(
        body,
        mesh=finer,
        in_specs=placed,
        out_specs=(P(DP_EXPERT, None), P("expert", None, DP, None)),
        check_vma=False,
    )
```

time: 186 us -> 184 us (0.989)
  waiting for transfers between devices: 78.2 us -> 63 us
  starting transfers between devices: 80.5 us -> 90.2 us
  Pallas kernels: 20.8 us -> 23 us
    ppermute x6 -> x11, starting transfers between devices: 17.8 us -> 35.5 us  [shifted(): lax.ppermute(value, 'dp_1', [(i, (i + k) % size) for i in range(size)])]
    ppermute x3 -> x0, waiting for transfers between devices: 14.2 us -> none  [body(): lax.ppermute(parts[k], 'dp_1', [(i, (i + k) % size) for i in range(size)])]
    ppermute x3 -> x0, starting transfers between devices: 8.67 us -> none  [body(): lax.ppermute(parts[k], 'dp_1', [(i, (i + k) % size) for i in range(size)])]
    ppermute x6 -> x11, waiting for transfers between devices: 24.9 us -> 21.4 us  [shifted(): lax.ppermute(value, 'dp_1', [(i, (i + k) % size) for i in range(size)])]
    pallas_call x2 -> x3, Pallas kernels: 14.3 us -> 16.8 us  [the longest x1 7.02 us: grads(): pl.pallas_call(functools.partial(grads_kernel, places), in_specs=[pl.Bloc...]
    ppermute x2, waiting for transfers between devices: 39.1 us -> 41.6 us  [swap(): return lax.ppermute(value, 'dp_0', [(0, 1), (1, 0)])]
    slice x0 -> x4, local copies, waits for them, and re-layouts: none -> 2.4 us  [body(): top, bottom = (shifted(left[:half], 1), shifted(right[half:], -1))]
    unnamed x26 -> x30, local copies, waits for them, and re-layouts: 3.05 us -> 0.78 us
  transfers between devices with their start and end apart: 13 -> 15, of which waited for: 7 -> 7; matrix products, arithmetic and copies ran while one was open for 1% -> 3% of each run, Pallas kernels for 0% -> 5%
where the time goes in v3:
time: 184 us; the launch traced here: 183 us
  starting transfers between devices  90.2 us (49%)
  waiting for transfers between devices  63 us (34%)
  Pallas kernels  23 us (12%)
  local copies, waits for them, and re-layouts  3.2 us (2%)
  other arithmetic  2.57 us (1%)
    all_to_all x2, starting transfers between devices, exchange(): lax.all_to_all(value.reshape(n_owner, rows // n_owner, lanes), 'expert',...  45.5 us
    ppermute x2, waiting for transfers between devices, swap(): return lax.ppermute(value, 'dp_0', [(0, 1), (1, 0)])  41.6 us
    ppermute x11, starting transfers between devices, shifted(): lax.ppermute(value, 'dp_1', [(i, (i + k) % size) for i in range(size)])  35.5 us
    ppermute x11, waiting for transfers between devices, shifted(): lax.ppermute(value, 'dp_1', [(i, (i + k) % size) for i in range(size)])  21.4 us
    ppermute x2, starting transfers between devices, swap(): return lax.ppermute(value, 'dp_0', [(0, 1), (1, 0)])  9.19 us
    pallas_call x1, Pallas kernels, grads(): pl.pallas_call(functools.partial(grads_kernel, places), in_specs=[pl.Bloc...  7.02 us
    pallas_call x1, Pallas kernels, terms(): pl.pallas_call(functools.partial(terms_kernel, places, hidden), in_specs=...  6.26 us
    pallas_call x1, Pallas kernels, pack(): pl.pallas_call(functools.partial(pack_kernel, cap), out_shape=(jax.ShapeD...  3.95 us
  transfers between devices with their start and end apart: 15, of which 7 were waited for; matrix products, arithmetic and copies ran while one was open for 3% of the time, Pallas kernels for 5%

profile of v3, /device:TPU:23, one launch (start us, length us, event | category | flops | bytes accessed | tf_op | source)
XLA Modules:
  0.0 182.9 jit_solution(10593346860672837159)
XLA Ops:
  0.6 4.0 %pack.1 = (bf16[7168,128]{1,0:T(8,128)(2,1)}, bf16[448,128]{1,0:T(8,128)(2,1)}) custom-call(s32[3,128]{1,0:T(4,128)} %bitcast.33, f32[3,128]{1,0:T(4,128)} %bitcast.34, bf16[128,1024]{1,0:T(8,128)(2,1)} %tok_ref.1, bf16[128,1024]{1,0:T(8,128)(2,1)} %grad_ref.1), custom_call_target="tpu_custom_call" | custom-call | tf_op jit(solution)/shard_map/pack/pallas_call | solution.py:67
  4.6 14.7 %all-to-all-start = ((bf16[64,112,128]{2,1,0:T(8,128)(2,1)}), bf16[64,112,128]{2,1,0:T(8,128)(2,1)S(1)}, u32[]{:S(2)}, u32[]{:S(2)}) async-start(bf16[64,112,128]{2,1,0:T(8,128)(2,1)} %bitcast.26), calls=%async_computation | async-start | bytes 3670016 | tf_op jit(solution)/shard_map/all_to_all | solution.py:315
  19.4 4.8 %collective-permute-start.4 = (bf16[128,2560]{1,0:T(8,128)(2,1)S(1)}, bf16[128,2560]{1,0:T(8,128)(2,1)S(1)}, u32[]{:S(2)}, u32[]{:S(2)}) collective-permute-start(bf16[128,2560]{1,0:T(8,128)(2,1)S(1)} %pad_maximum_fusion.refs_4_.refs_5_), channel_id=1, source_target_pairs={{0,256},{256,0},{1,257},{257,1},{2,258},{258,2},{3,259},{259,3},{4... | collective-permute-start | bytes 1966088 | tf_op jit(solution)/shard_map/ppermute | solution.py:305
  24.1 2.5 %collective-permute-start.1 = (bf16[128,2560]{1,0:T(8,128)(2,1)S(1)}, bf16[128,2560]{1,0:T(8,128)(2,1)S(1)}, u32[]{:S(2)}, u32[]{:S(2)}) collective-permute-start(bf16[128,2560]{1,0:T(8,128)(2,1)S(1)} %pad_maximum_fusion.refs_4_.refs_5_), channel_id=1, source_target_pairs={{0,192},{64,0},{128,64},{192,128},{1,193},{65,1},{129,65},{193,129... | collective-permute-start | bytes 1966088 | tf_op jit(solution)/shard_map/ppermute | solution.py:310
  26.6 4.0 %collective-permute-start = (bf16[128,2560]{1,0:T(8,128)(2,1)S(1)}, bf16[128,2560]{1,0:T(8,128)(2,1)S(1)}, u32[]{:S(2)}, u32[]{:S(2)}) collective-permute-start(bf16[128,2560]{1,0:T(8,128)(2,1)S(1)} %pad_maximum_fusion.refs_4_.refs_5_), channel_id=1, source_target_pairs={{0,64},{64,128},{128,192},{192,0},{1,65},{65,129},{129,193},{193,1... | collective-permute-start | bytes 1966088 | tf_op jit(solution)/shard_map/ppermute | solution.py:310
  30.6 31.5 %collective-permute-done.4.refs_9_.refs_10_ = bf16[128,2560]{1,0:T(8,128)(2,1)S(1)} collective-permute-done((bf16[128,2560]{1,0:T(8,128)(2,1)S(1)}, bf16[128,2560]{1,0:T(8,128)(2,1)S(1)}, u32[]{:S(2)}, u32[]{:S(2)}) %collective-permute-start.4) | collective-permute-done | bytes 655392 | tf_op jit(solution)/shard_map/ppermute | solution.py:305
  62.1 2.4 %collective-permute-start.6 = (bf16[128,2560]{1,0:T(8,128)(2,1)S(1)}, bf16[128,2560]{1,0:T(8,128)(2,1)S(1)}, u32[]{:S(2)}, u32[]{:S(2)}) collective-permute-start(bf16[128,2560]{1,0:T(8,128)(2,1)S(1)} %collective-permute-done.4.refs_9_.refs_10_), channel_id=1, source_target_pairs={{0,192},{64,0},{128,64},{192,128},{1,193},{65,1},{129,65},{193,129... | collective-permute-start | bytes 1966088 | tf_op jit(solution)/shard_map/ppermute | solution.py:310
  64.6 4.0 %collective-permute-start.5 = (bf16[128,2560]{1,0:T(8,128)(2,1)S(1)}, bf16[128,2560]{1,0:T(8,128)(2,1)S(1)}, u32[]{:S(2)}, u32[]{:S(2)}) collective-permute-start(bf16[128,2560]{1,0:T(8,128)(2,1)S(1)} %collective-permute-done.4.refs_9_.refs_10_), channel_id=1, source_target_pairs={{0,64},{64,128},{128,192},{192,0},{1,65},{65,129},{129,193},{193,1... | collective-permute-start | bytes 1966088 | tf_op jit(solution)/shard_map/ppermute | solution.py:310
  68.7 1.9 %collective-permute-start.3 = (bf16[64,2560]{1,0:T(8,128)(2,1)S(1)}, bf16[64,2560]{1,0:T(8,128)(2,1)S(1)}, u32[]{:S(2)}, u32[]{:S(2)}) collective-permute-start(bf16[64,2560]{1,0:T(8,128)(2,1)S(1)} %slice.26), channel_id=1, source_target_pairs={{0,192},{64,0},{128,64},{192,128},{1,193},{65,1},{129,65},{193,129... | collective-permute-start | bytes 983048 | tf_op jit(solution)/shard_map/ppermute | solution.py:310
  71.4 4.6 %collective-permute-start.2 = (bf16[64,2560]{1,0:T(8,128)(2,1)}, bf16[64,2560]{1,0:T(8,128)(2,1)S(1)}, u32[]{:S(2)}, u32[]{:S(2)}) collective-permute-start(bf16[64,2560]{1,0:T(8,128)(2,1)} %slice.25), channel_id=1, source_target_pairs={{0,64},{64,128},{128,192},{192,0},{1,65},{65,129},{129,193},{193,1... | collective-permute-start | bytes 983048 | tf_op jit(solution)/shard_map/ppermute | solution.py:310
  76.0 4.8 %collective-permute-done.6.refs_11_.refs_12_ = bf16[128,2560]{1,0:T(8,128)(2,1)S(1)} collective-permute-done((bf16[128,2560]{1,0:T(8,128)(2,1)S(1)}, bf16[128,2560]{1,0:T(8,128)(2,1)S(1)}, u32[]{:S(2)}, u32[]{:S(2)}) %collective-permute-start.6) | collective-permute-done | bytes 655392 | tf_op jit(solution)/shard_map/ppermute | solution.py:310
  84.3 4.6 %collective-permute-start.7 = (bf16[64,2560]{1,0:T(8,128)(2,1)}, bf16[64,2560]{1,0:T(8,128)(2,1)S(1)}, u32[]{:S(2)}, u32[]{:S(2)}) collective-permute-start(bf16[64,2560]{1,0:T(8,128)(2,1)} %slice.27), channel_id=1, source_target_pairs={{0,64},{64,128},{128,192},{192,0},{1,65},{65,129},{129,193},{193,1... | collective-permute-start | bytes 983048 | tf_op jit(solution)/shard_map/ppermute | solution.py:310
  88.9 3.6 %slopes.1 = (f32[448,768]{1,0:T(8,128)}, f32[448,768]{1,0:T(8,128)}, bf16[448,768]{1,0:T(8,128)(2,1)}) custom-call(bf16[448,1536]{1,0:T(8,128)(2,1)} %bitcast.27), custom_call_target="tpu_custom_call" | custom-call | tf_op jit(solution)/shard_map/slopes/pallas_call | solution.py:125
  96.0 7.0 %grads.1 = (bf16[3584,128]{1,0:T(8,128)(2,1)}, bf16[448,1536]{1,0:T(8,128)(2,1)}, bf16[448,256]{1,0:T(8,128)(2,1)}) custom-call(s32[2]{0:T(128)} %pad_add_fusion.refs_0_, bf16[7168,128]{1,0:T(8,128)(2,1)S(1)} %bitcast.23, f32[448,768]{1,0:T(8,128)} %get-tuple-element.16.refs_2_, f32[448,768]{1,0:T(8,128)} %get-tuple-element.17.refs_3_, ...), custom_call_target="tpu_custom_call" | custom-call | tf_op jit(solution)/shard_map/grads/pallas_call | solution.py:185
  103.0 30.9 %all-to-all-start.1 = ((bf16[64,56,128]{2,1,0:T(8,128)(2,1)}), bf16[64,56,128]{2,1,0:T(8,128)(2,1)S(1)}, u32[]{:S(2)}, u32[]{:S(2)}) async-start(bf16[64,56,128]{2,1,0:T(8,128)(2,1)} %bitcast.28), calls=%async_computation.1 | async-start | bytes 1835008 | tf_op jit(solution)/shard_map/all_to_all | solution.py:315
  133.9 6.3 %terms.1 = (f32[2,3,32,768]{3,2,1,0:T(8,128)}, bf16[2,3,32,768]{3,2,1,0:T(8,128)(2,1)}, bf16[2,3,32,768]{3,2,1,0:T(8,128)(2,1)}, bf16[2,3,32,768]{3,2,1,0:T(8,128)(2,1)}) custom-call(s32[2]{0:T(128)} %pad_add_fusion.refs_0_, bf16[7168,128]{1,0:T(8,128)(2,1)} %bitcast.24, bf16[448,1536]{1,0:T(8,128)(2,1)} %get-tuple-element.19.refs_2_, ...), custom_call_target="tpu_custom_call" | custom-call | tf_op jit(solution)/shard_map/terms/pallas_call | solution.py:251
  140.1 5.2 %collective-permute-start.9 = (bf16[2,3,32,768]{3,2,1,0:T(8,128)(2,1)}, bf16[2,3,32,768]{3,2,1,0:T(8,128)(2,1)S(1)}, u32[]{:S(2)}, u32[]{:S(2)}) collective-permute-start(bf16[2,3,32,768]{3,2,1,0:T(8,128)(2,1)} %get-tuple-element.23), channel_id=1, source_target_pairs={{0,64},{64,128},{128,192},{192,0},{1,65},{65,129},{129,193},{193,1... | collective-permute-start | bytes 884744 | tf_op jit(solution)/shard_map/ppermute | solution.py:310
  145.4 1.9 %collective-permute-start.10 = (bf16[2,3,32,768]{3,2,1,0:T(8,128)(2,1)}, bf16[2,3,32,768]{3,2,1,0:T(8,128)(2,1)S(1)}, u32[]{:S(2)}, u32[]{:S(2)}) collective-permute-start(bf16[2,3,32,768]{3,2,1,0:T(8,128)(2,1)} %get-tuple-element.24), channel_id=1, source_target_pairs={{0,128},{64,192},{128,0},{192,64},{1,129},{65,193},{129,1},{193,65... | collective-permute-start | bytes 884744 | tf_op jit(solution)/shard_map/ppermute | solution.py:310
  147.3 2.5 %collective-permute-start.11 = (bf16[2,3,32,768]{3,2,1,0:T(8,128)(2,1)}, bf16[2,3,32,768]{3,2,1,0:T(8,128)(2,1)S(1)}, u32[]{:S(2)}, u32[]{:S(2)}) collective-permute-start(bf16[2,3,32,768]{3,2,1,0:T(8,128)(2,1)} %get-tuple-element.25), channel_id=1, source_target_pairs={{0,192},{64,0},{128,64},{192,128},{1,193},{65,1},{129,65},{193,129... | collective-permute-start | bytes 884744 | tf_op jit(solution)/shard_map/ppermute | solution.py:310
  149.8 8.0 %collective-permute-done.9 = bf16[2,3,32,768]{3,2,1,0:T(8,128)(2,1)S(1)} collective-permute-done((bf16[2,3,32,768]{3,2,1,0:T(8,128)(2,1)}, bf16[2,3,32,768]{3,2,1,0:T(8,128)(2,1)S(1)}, u32[]{:S(2)}, u32[]{:S(2)}) %collective-permute-start.9) | collective-permute-done | bytes 294944 | tf_op jit(solution)/shard_map/ppermute | solution.py:310
  157.8 6.4 %collective-permute-done.11 = bf16[2,3,32,768]{3,2,1,0:T(8,128)(2,1)S(1)} collective-permute-done((bf16[2,3,32,768]{3,2,1,0:T(8,128)(2,1)}, bf16[2,3,32,768]{3,2,1,0:T(8,128)(2,1)S(1)}, u32[]{:S(2)}, u32[]{:S(2)}) %collective-permute-start.11) | collective-permute-done | bytes 294944 | tf_op jit(solution)/shard_map/ppermute | solution.py:310
  165.4 4.4 %collective-permute-start.12 = (bf16[3,32,768]{2,1,0:T(8,128)(2,1)S(1)}, bf16[3,32,768]{2,1,0:T(8,128)(2,1)S(1)}, u32[]{:S(2)}, u32[]{:S(2)}) collective-permute-start(bf16[3,32,768]{2,1,0:T(8,128)(2,1)S(1)} %fusion.2), channel_id=1, source_target_pairs={{0,256},{256,0},{1,257},{257,1},{2,258},{258,2},{3,259},{259,3},{4... | collective-permute-start | bytes 442376 | tf_op jit(solution)/shard_map/ppermute | solution.py:305
  169.9 10.1 %collective-permute-done.12 = bf16[3,32,768]{2,1,0:T(8,128)(2,1)S(1)} collective-permute-done((bf16[3,32,768]{2,1,0:T(8,128)(2,1)S(1)}, bf16[3,32,768]{2,1,0:T(8,128)(2,1)S(1)}, u32[]{:S(2)}, u32[]{:S(2)}) %collective-permute-start.12) | collective-permute-done | bytes 147488 | tf_op jit(solution)/shard_map/ppermute | solution.py:305
  180.8 2.2 %combine.1 = bf16[128,1024]{1,0:T(8,128)(2,1)} custom-call(bf16[448,128]{1,0:T(8,128)(2,1)} %get-tuple-element.14.match_ref, bf16[3584,128]{1,0:T(8,128)(2,1)S(1)} %bitcast.25), custom_call_target="tpu_custom_call" | custom-call | tf_op jit(solution)/shard_map/combine/pallas_call | solution.py:296
  (50 shorter events, 9.8 us)
Async XLA Ops:
  4.6 14.7 %copy-start.11 = (bf16[1,128,768]{2,1,0:T(8,128)(2,1)S(1)}, bf16[1,128,768]{2,1,0:T(8,128)(2,1)}, u32[]{:S(2)}) copy-start(bf16[1,128,768]{2,1,0:T(8,128)(2,1)} %param.15) | copy-start | bytes 589828
  4.6 14.7 %copy-start.12 = (bf16[1,128,768]{2,1,0:T(8,128)(2,1)S(1)}, bf16[1,128,768]{2,1,0:T(8,128)(2,1)}, u32[]{:S(2)}) copy-start(bf16[1,128,768]{2,1,0:T(8,128)(2,1)} %param.14) | copy-start | bytes 589828
  4.6 14.7 %copy-start.13 = (bf16[1,128,768]{2,1,0:T(8,128)(2,1)S(1)}, bf16[1,128,768]{2,1,0:T(8,128)(2,1)}, u32[]{:S(2)}) copy-start(bf16[1,128,768]{2,1,0:T(8,128)(2,1)} %param.16) | copy-start | bytes 589828
  4.6 14.7 %copy-start.14 = (bf16[1,128,256]{2,1,0:T(8,128)(2,1)S(1)}, bf16[1,128,256]{2,1,0:T(8,128)(2,1)}, u32[]{:S(2)}) copy-start(bf16[1,128,256]{2,1,0:T(8,128)(2,1)} %param.17) | copy-start | bytes 196612
  4.6 90.6 %all-to-all-start = ((bf16[64,112,128]{2,1,0:T(8,128)(2,1)}), bf16[64,112,128]{2,1,0:T(8,128)(2,1)S(1)}, u32[]{:S(2)}, u32[]{:S(2)}) async-start(bf16[64,112,128]{2,1,0:T(8,128)(2,1)} %bitcast.26), calls=%async_computation | async-start | bytes 3670016 | tf_op jit(solution)/shard_map/all_to_all | solution.py:315
  19.4 64.9 %copy-start.1 = (bf16[128,2560]{1,0:T(8,128)(2,1)}, bf16[128,2560]{1,0:T(8,128)(2,1)S(1)}, u32[]{:S(2)}) copy-start(bf16[128,2560]{1,0:T(8,128)(2,1)S(1)} %pad_maximum_fusion.refs_4_.refs_5_) | copy-start | bytes 1966084
  19.4 42.7 %collective-permute-start.4 = (bf16[128,2560]{1,0:T(8,128)(2,1)S(1)}, bf16[128,2560]{1,0:T(8,128)(2,1)S(1)}, u32[]{:S(2)}, u32[]{:S(2)}) collective-permute-start(bf16[128,2560]{1,0:T(8,128)(2,1)S(1)} %pad_maximum_fusion.refs_4_.refs_5_), channel_id=1, source_target_pairs={{0,256},{256,0},{1,257},{257,1},{2,258},{258,2},{3,259},{259,3},{4... | collective-permute-start | bytes 1966088 | tf_op jit(solution)/shard_map/ppermute | solution.py:305
  24.1 44.5 %collective-permute-start.1 = (bf16[128,2560]{1,0:T(8,128)(2,1)S(1)}, bf16[128,2560]{1,0:T(8,128)(2,1)S(1)}, u32[]{:S(2)}, u32[]{:S(2)}) collective-permute-start(bf16[128,2560]{1,0:T(8,128)(2,1)S(1)} %pad_maximum_fusion.refs_4_.refs_5_), channel_id=1, source_target_pairs={{0,192},{64,0},{128,64},{192,128},{1,193},{65,1},{129,65},{193,129... | collective-permute-start | bytes 1966088 | tf_op jit(solution)/shard_map/ppermute | solution.py:310
  26.6 44.0 %collective-permute-start = (bf16[128,2560]{1,0:T(8,128)(2,1)S(1)}, bf16[128,2560]{1,0:T(8,128)(2,1)S(1)}, u32[]{:S(2)}, u32[]{:S(2)}) collective-permute-start(bf16[128,2560]{1,0:T(8,128)(2,1)S(1)} %pad_maximum_fusion.refs_4_.refs_5_), channel_id=1, source_target_pairs={{0,64},{64,128},{128,192},{192,0},{1,65},{65,129},{129,193},{193,1... | collective-permute-start | bytes 1966088 | tf_op jit(solution)/shard_map/ppermute | solution.py:310
  62.1 26.8 %copy-start.6 = (bf16[128,2560]{1,0:T(8,128)(2,1)}, bf16[128,2560]{1,0:T(8,128)(2,1)S(1)}, u32[]{:S(2)}) copy-start(bf16[128,2560]{1,0:T(8,128)(2,1)S(1)} %collective-permute-done.4.refs_9_.refs_10_) | copy-start | bytes 1966084
  62.1 18.7 %collective-permute-start.6 = (bf16[128,2560]{1,0:T(8,128)(2,1)S(1)}, bf16[128,2560]{1,0:T(8,128)(2,1)S(1)}, u32[]{:S(2)}, u32[]{:S(2)}) collective-permute-start(bf16[128,2560]{1,0:T(8,128)(2,1)S(1)} %collective-permute-done.4.refs_9_.refs_10_), channel_id=1, source_target_pairs={{0,192},{64,0},{128,64},{192,128},{1,193},{65,1},{129,65},{193,129... | collective-permute-start | bytes 1966088 | tf_op jit(solution)/shard_map/ppermute | solution.py:310
  64.6 18.9 %collective-permute-start.5 = (bf16[128,2560]{1,0:T(8,128)(2,1)S(1)}, bf16[128,2560]{1,0:T(8,128)(2,1)S(1)}, u32[]{:S(2)}, u32[]{:S(2)}) collective-permute-start(bf16[128,2560]{1,0:T(8,128)(2,1)S(1)} %collective-permute-done.4.refs_9_.refs_10_), channel_id=1, source_target_pairs={{0,64},{64,128},{128,192},{192,0},{1,65},{65,129},{129,193},{193,1... | collective-permute-start | bytes 1966088 | tf_op jit(solution)/shard_map/ppermute | solution.py:310
  68.6 15.7 %copy-start.2 = (bf16[128,2560]{1,0:T(8,128)(2,1)}, bf16[128,2560]{1,0:T(8,128)(2,1)S(1)}, u32[]{:S(2)}) copy-start(bf16[128,2560]{1,0:T(8,128)(2,1)S(1)} %collective-permute-done.1.refs_6_.refs_7_) | copy-start | bytes 1966084
  68.7 24.4 %collective-permute-start.3 = (bf16[64,2560]{1,0:T(8,128)(2,1)S(1)}, bf16[64,2560]{1,0:T(8,128)(2,1)S(1)}, u32[]{:S(2)}, u32[]{:S(2)}) collective-permute-start(bf16[64,2560]{1,0:T(8,128)(2,1)S(1)} %slice.26), channel_id=1, source_target_pairs={{0,192},{64,0},{128,64},{192,128},{1,193},{65,1},{129,65},{193,129... | collective-permute-start | bytes 983048 | tf_op jit(solution)/shard_map/ppermute | solution.py:310
  70.6 18.3 %copy-start.3 = (bf16[128,2560]{1,0:T(8,128)(2,1)}, bf16[128,2560]{1,0:T(8,128)(2,1)S(1)}, u32[]{:S(2)}) copy-start(bf16[128,2560]{1,0:T(8,128)(2,1)S(1)} %collective-permute-done.refs_5_.refs_6_) | copy-start | bytes 1966084
  71.4 21.7 %collective-permute-start.2 = (bf16[64,2560]{1,0:T(8,128)(2,1)}, bf16[64,2560]{1,0:T(8,128)(2,1)S(1)}, u32[]{:S(2)}, u32[]{:S(2)}) collective-permute-start(bf16[64,2560]{1,0:T(8,128)(2,1)} %slice.25), channel_id=1, source_target_pairs={{0,64},{64,128},{128,192},{192,0},{1,65},{65,129},{129,193},{193,1... | collective-permute-start | bytes 983048 | tf_op jit(solution)/shard_map/ppermute | solution.py:310
  80.8 8.1 %copy-start.4 = (bf16[128,2560]{1,0:T(8,128)(2,1)}, bf16[128,2560]{1,0:T(8,128)(2,1)S(1)}, u32[]{:S(2)}) copy-start(bf16[128,2560]{1,0:T(8,128)(2,1)S(1)} %collective-permute-done.6.refs_11_.refs_12_) | copy-start | bytes 1966084
  81.6 12.6 %collective-permute-start.8 = (bf16[64,2560]{1,0:T(8,128)(2,1)}, bf16[64,2560]{1,0:T(8,128)(2,1)S(1)}, u32[]{:S(2)}, u32[]{:S(2)}) collective-permute-start(bf16[64,2560]{1,0:T(8,128)(2,1)} %slice.28), channel_id=1, source_target_pairs={{0,192},{64,0},{128,64},{192,128},{1,193},{65,1},{129,65},{193,129... | collective-permute-start | bytes 983048 | tf_op jit(solution)/shard_map/ppermute | solution.py:310
  84.3 10.9 %collective-permute-start.7 = (bf16[64,2560]{1,0:T(8,128)(2,1)}, bf16[64,2560]{1,0:T(8,128)(2,1)S(1)}, u32[]{:S(2)}, u32[]{:S(2)}) collective-permute-start(bf16[64,2560]{1,0:T(8,128)(2,1)} %slice.27), channel_id=1, source_target_pairs={{0,64},{64,128},{128,192},{192,0},{1,65},{65,129},{129,193},{193,1... | collective-permute-start | bytes 983048 | tf_op jit(solution)/shard_map/ppermute | solution.py:310
  103.0 77.7 %all-to-all-start.1 = ((bf16[64,56,128]{2,1,0:T(8,128)(2,1)}), bf16[64,56,128]{2,1,0:T(8,128)(2,1)S(1)}, u32[]{:S(2)}, u32[]{:S(2)}) async-start(bf16[64,56,128]{2,1,0:T(8,128)(2,1)} %bitcast.28), calls=%async_computation.1 | async-start | bytes 1835008 | tf_op jit(solution)/shard_map/all_to_all | solution.py:315
  140.1 17.7 %collective-permute-start.9 = (bf16[2,3,32,768]{3,2,1,0:T(8,128)(2,1)}, bf16[2,3,32,768]{3,2,1,0:T(8,128)(2,1)S(1)}, u32[]{:S(2)}, u32[]{:S(2)}) collective-permute-start(bf16[2,3,32,768]{3,2,1,0:T(8,128)(2,1)} %get-tuple-element.23), channel_id=1, source_target_pairs={{0,64},{64,128},{128,192},{192,0},{1,65},{65,129},{129,193},{193,1... | collective-permute-start | bytes 884744 | tf_op jit(solution)/shard_map/ppermute | solution.py:310
  145.4 12.4 %collective-permute-start.10 = (bf16[2,3,32,768]{3,2,1,0:T(8,128)(2,1)}, bf16[2,3,32,768]{3,2,1,0:T(8,128)(2,1)S(1)}, u32[]{:S(2)}, u32[]{:S(2)}) collective-permute-start(bf16[2,3,32,768]{3,2,1,0:T(8,128)(2,1)} %get-tuple-element.24), channel_id=1, source_target_pairs={{0,128},{64,192},{128,0},{192,64},{1,129},{65,193},{129,1},{193,65... | collective-permute-start | bytes 884744 | tf_op jit(solution)/shard_map/ppermute | solution.py:310
  147.3 16.9 %collective-permute-start.11 = (bf16[2,3,32,768]{3,2,1,0:T(8,128)(2,1)}, bf16[2,3,32,768]{3,2,1,0:T(8,128)(2,1)S(1)}, u32[]{:S(2)}, u32[]{:S(2)}) collective-permute-start(bf16[2,3,32,768]{3,2,1,0:T(8,128)(2,1)} %get-tuple-element.25), channel_id=1, source_target_pairs={{0,192},{64,0},{128,64},{192,128},{1,193},{65,1},{129,65},{193,129... | collective-permute-start | bytes 884744 | tf_op jit(solution)/shard_map/ppermute | solution.py:310
  165.4 14.6 %collective-permute-start.12 = (bf16[3,32,768]{2,1,0:T(8,128)(2,1)S(1)}, bf16[3,32,768]{2,1,0:T(8,128)(2,1)S(1)}, u32[]{:S(2)}, u32[]{:S(2)}) collective-permute-start(bf16[3,32,768]{2,1,0:T(8,128)(2,1)S(1)} %fusion.2), channel_id=1, source_target_pairs={{0,256},{256,0},{1,257},{257,1},{2,258},{258,2},{3,259},{259,3},{4... | collective-permute-start | bytes 442376 | tf_op jit(solution)/shard_map/ppermute | solution.py:305
  (6 other events, 19.2 us)

commit v4 on v3

--- a/solution.py
+++ b/solution.py
@@ -145,8 +145,8 @@
     n = len(places)
     where_ref, got_ref, act_hbm, slope_hbm = refs[:4]
     pieces = refs[4 : 4 + n]
-    row_ref, both_ref, proj_ref = refs[4 + n : 7 + n]
-    wide, dy_rows, rows_wide, w1, w2, act, slope, sems = refs[7 + n :]
+    row_hbm, both_hbm, proj_hbm = refs[4 + n : 7 + n]
+    wide, x_rows, dy_rows, rows_wide, w1, w2, act, slope, row, both, proj, sems = refs[7 + n :]
     hidden = act.shape[1]
     slots, width = dy_rows.shape
     n_chunk = width // LANES
@@ -155,26 +155,35 @@
     last = fetch(where_ref, pieces, places, pl.ds(w1.shape[1], w2.shape[1]), w2, sems, n)
     wide[...] = got_ref[...].astype(F32)
     spread(wide, n_chunk, 2 * n_chunk, dy_rows)
+    spread(wide, 0, 2 * n_chunk, x_rows)
     for copy in first:
         copy.wait()
     grad = jnp.dot(dy_rows[...], w1[:, :hidden], preferred_element_type=F32)
     for copy in middle:
         copy.wait()
-    both_ref[:, :hidden] = (grad * slope[...]).astype(BF16)
-    both_ref[:, hidden:] = (grad * act[...]).astype(BF16)
+    both[:, :hidden] = (grad * slope[...]).astype(BF16)
+    both[:, hidden:] = (grad * act[...]).astype(BF16)
+    proj[0] = jnp.dot(x_rows[...], w1[:, hidden:], preferred_element_type=F32).astype(BF16)
+    proj[1] = jnp.dot(dy_rows[...], w1[:, hidden:], preferred_element_type=F32).astype(BF16)
+    sent = fetch_all((both, proj), (both_hbm, proj_hbm), sems, 2 * n + 2)
     for copy in last:
         copy.wait()
     for c in range(0, n_chunk, 2):
         rows = lax.dot_general(
-            both_ref[...],
+            both[...],
             w2[c * LANES : (c + 2) * LANES, :],
             (((1,), (1,)), ((), ())),
             preferred_element_type=F32,
         )
         rows_wide[chunk_rows(c, slots, n_chunk), :] = rows[:, :LANES]
         rows_wide[chunk_rows(c + 1, slots, n_chunk), :] = rows[:, LANES:]
-    row_ref[...] = rows_wide[...].astype(BF16)
-    proj_ref[...] = jnp.dot(dy_rows[...], w1[:, hidden:], preferred_element_type=F32).astype(BF16)
+    size = row.shape[0] // 2
+    for i in range(2):
+        here = slice(i * size, (i + 1) * size)
+        row[here, :] = rows_wide[here, :].astype(BF16)
+        sent += fetch_all((row.at[here, :],), (row_hbm.at[here, :],), sems, 2 * n + 4 + i)
+    for copy in sent:
+        copy.wait()
 
 
 def grads(where, got, act, slope, pieces, places, rank):
@@ -185,53 +194,47 @@
     return pl.pallas_call(
         functools.partial(grads_kernel, places),
         in_specs=[pl.BlockSpec(memory_space=pltpu.SMEM), in_vmem()] + [in_place()] * (2 + n),
+        out_specs=(in_place(),) * 3,
         out_shape=(
             jax.ShapeDtypeStruct((rows, LANES), BF16),
             jax.ShapeDtypeStruct((slots, 2 * hidden), BF16),
-            jax.ShapeDtypeStruct((slots, rank), BF16),
+            jax.ShapeDtypeStruct((2, slots, rank), BF16),
         ),
         scratch_shapes=[
             pltpu.VMEM(got.shape, F32),
+            pltpu.VMEM((slots, width), BF16),
             pltpu.VMEM((slots, width), BF16),
             pltpu.VMEM((rows, LANES), F32),
             pltpu.VMEM((width, hidden + rank), BF16),
             pltpu.VMEM((width, 2 * hidden), BF16),
             pltpu.VMEM((slots, hidden), F32),
             pltpu.VMEM((slots, hidden), F32),
-            pltpu.SemaphoreType.DMA((2 * n + 2,)),
+            pltpu.VMEM((rows, LANES), BF16),
+            pltpu.VMEM((slots, 2 * hidden), BF16),
+            pltpu.VMEM((2, slots, rank), BF16),
+            pltpu.SemaphoreType.DMA((2 * n + 6,)),
         ],
         name="grads",
     )(where, near(got), act, slope, *pieces)
 
 
-def terms_kernel(places, first_column, *refs):
-    n = len(places)
-    where_ref, got_hbm, both_hbm, proj_hbm, hid_hbm = refs[:5]
-    pieces = refs[5 : 5 + n]
-    part_refs = refs[5 + n : 9 + n]
-    got, both, proj, hid, basis, wide, x_rows, term_ref, sems = refs[9 + n :]
+def terms_kernel(where_ref, both_hbm, proj_hbm, hid_hbm, *refs):
+    part_refs = refs[:4]
+    both, proj, hid, term_ref, sems = refs[4:]
     hidden = hid.shape[1]
-    n_chunk = x_rows.shape[1] // LANES
-    (first,) = fetch_all((got_hbm,), (got,), sems, n)
-    middle = fetch(
-        where_ref, pieces, places, pl.ds(first_column, basis.shape[1]), basis, sems, 0
+    proj_in, both_in, hid_in = fetch_all(
+        (proj_hbm, both_hbm, hid_hbm), (proj, both, hid), sems, 0
     )
-    last = fetch_all((both_hbm, proj_hbm, hid_hbm), (both, proj, hid), sems, n + 1)
-    first.wait()
-    wide[...] = got[...].astype(F32)
-    spread(wide, 0, 2 * n_chunk, x_rows)
-    for copy in middle:
-        copy.wait()
-    x_proj = jnp.dot(x_rows[...], basis[...], preferred_element_type=F32).astype(BF16)
-    for copy in last:
-        copy.wait()
     by_rows = (((0,), (0,)), ((), ()))
+    proj_in.wait()
+    both_in.wait()
+    x_proj = proj[0]
     term_ref[0] = lax.dot_general(x_proj, both[:, :hidden], by_rows, preferred_element_type=F32)
     term_ref[1] = lax.dot_general(x_proj, both[:, hidden:], by_rows, preferred_element_type=F32)
-    term_ref[2] = lax.dot_general(proj[...], hid[...], by_rows, preferred_element_type=F32)
+    hid_in.wait()
+    term_ref[2] = lax.dot_general(proj[1], hid[...], by_rows, preferred_element_type=F32)
     high, low = where_ref[0], where_ref[1]
-    n_term, rank, _ = term_ref.shape
-    part = rank // n_chunk
+    n_term, part = term_ref.shape[0], part_refs[0].shape[2]
     for k, out in enumerate(part_refs):
         column = jnp.bitwise_and(low + k, 3)
         for h in range(2):
@@ -242,31 +245,25 @@
                 )
 
 
-def terms(where, got, both, proj, hid, pieces, places):
-    slots, hidden = hid.shape
-    rank = proj.shape[1]
-    width = got.shape[0] * LANES // slots // 2
-    part = rank * LANES // width
-    n = len(pieces)
-    return pl.pallas_call(
-        functools.partial(terms_kernel, places, hidden),
-        in_specs=[pl.BlockSpec(memory_space=pltpu.SMEM)] + [in_place()] * (4 + n),
+def terms(where, both, proj, hid, n_dp):
+    _, hidden = hid.shape
+    rank = proj.shape[2]
+    part = rank // n_dp
+    return pl.pallas_call(
+        terms_kernel,
+        in_specs=[pl.BlockSpec(memory_space=pltpu.SMEM)] + [in_place()] * 3,
         out_shape=tuple(
             jax.ShapeDtypeStruct((2, 3, part, hidden), F32 if k == 0 else BF16) for k in range(4)
         ),
         scratch_shapes=[
-            pltpu.VMEM(got.shape, BF16),
             pltpu.VMEM(both.shape, BF16),
             pltpu.VMEM(proj.shape, BF16),
             pltpu.VMEM(hid.shape, BF16),
-            pltpu.VMEM((width, rank), BF16),
-            pltpu.VMEM(got.shape, F32),
-            pltpu.VMEM((slots, width), BF16),
             pltpu.VMEM((3, rank, hidden), F32),
-            pltpu.SemaphoreType.DMA((n + 4,)),
+            pltpu.SemaphoreType.DMA((3,)),
         ],
         name="terms",
-    )(where, got, both, proj, hid, *pieces)
+    )(where, both, proj, hid)
 
 
 def take_pair(wide_ref, first, second, slots, step):
@@ -343,10 +340,9 @@
     places = tuple(places)
     row_grad, both, proj = grads(where, got, act, slope, pieces, places, rank)
     back = exchange(row_grad, n_owner)
-    parts = terms(where, got, both, proj, hid, pieces, places)
-    size = lax.axis_size("dp_1")
+    parts = terms(where, both, proj, hid, 8)
     summed = parts[0]
-    for k in range(1, size):
+    for k in (2, 1, 3):
         summed = summed + shifted(parts[k], k).astype(F32)
     other = swap(summed[1].astype(BF16))
     proj_grads = (summed[0] + other.astype(F32))[None]

time: 184 us -> 180 us (0.978)
  the two profiles are of different devices: /device:TPU:23 before, /device:TPU:17 now
where the time goes in v4:
time: 180 us; the launch traced here: 179 us
  starting transfers between devices  90.2 us (50%)
  waiting for transfers between devices  60.1 us (33%)
  Pallas kernels  21.6 us (12%)
  local copies, waits for them, and re-layouts  3.31 us (2%)
  other arithmetic  2.58 us (1%)
    all_to_all x2, starting transfers between devices, exchange(): lax.all_to_all(value.reshape(n_owner, rows // n_owner, lanes), 'expert',...  46.3 us
    ppermute x2, waiting for transfers between devices, swap(): return lax.ppermute(value, 'dp_0', [(0, 1), (1, 0)])  41.8 us
    ppermute x11, starting transfers between devices, shifted(): lax.ppermute(value, 'dp_1', [(i, (i + k) % size) for i in range(size)])  34.7 us
    ppermute x11, waiting for transfers between devices, shifted(): lax.ppermute(value, 'dp_1', [(i, (i + k) % size) for i in range(size)])  18.4 us
    ppermute x2, starting transfers between devices, swap(): return lax.ppermute(value, 'dp_0', [(0, 1), (1, 0)])  9.2 us
    pallas_call x1, Pallas kernels, grads(): pl.pallas_call(functools.partial(grads_kernel, places), in_specs=[pl.Bloc...  7.35 us
    pallas_call x1, Pallas kernels, terms(): pl.pallas_call(terms_kernel, in_specs=[pl.BlockSpec(memory_space=pltpu.SM...  4.51 us
    pallas_call x1, Pallas kernels, pack(): pl.pallas_call(functools.partial(pack_kernel, cap), out_shape=(jax.ShapeD...  3.95 us
  transfers between devices with their start and end apart: 15, of which 7 were waited for; matrix products, arithmetic and copies ran while one was open for 3% of the time, Pallas kernels for 5%

profile of v4, /device:TPU:17, one launch (start us, length us, event | category | flops | bytes accessed | tf_op | source)
XLA Modules:
  0.0 178.8 jit_solution(4752737531149829262)
XLA Ops:
  0.6 3.9 %pack.1 = (bf16[7168,128]{1,0:T(8,128)(2,1)}, bf16[448,128]{1,0:T(8,128)(2,1)}) custom-call(s32[3,128]{1,0:T(4,128)} %bitcast.32, f32[3,128]{1,0:T(4,128)} %bitcast.33, bf16[128,1024]{1,0:T(8,128)(2,1)} %tok_ref.1, bf16[128,1024]{1,0:T(8,128)(2,1)} %grad_ref.1), custom_call_target="tpu_custom_call" | custom-call | tf_op jit(solution)/shard_map/pack/pallas_call | solution.py:67
  4.6 14.7 %all-to-all-start = ((bf16[64,112,128]{2,1,0:T(8,128)(2,1)}), bf16[64,112,128]{2,1,0:T(8,128)(2,1)S(1)}, u32[]{:S(2)}, u32[]{:S(2)}) async-start(bf16[64,112,128]{2,1,0:T(8,128)(2,1)} %bitcast.25), calls=%async_computation | async-start | bytes 3670016 | tf_op jit(solution)/shard_map/all_to_all | solution.py:312
  19.4 4.8 %collective-permute-start.4 = (bf16[128,2560]{1,0:T(8,128)(2,1)S(1)}, bf16[128,2560]{1,0:T(8,128)(2,1)S(1)}, u32[]{:S(2)}, u32[]{:S(2)}) collective-permute-start(bf16[128,2560]{1,0:T(8,128)(2,1)S(1)} %pad_maximum_fusion.refs_4_), channel_id=1, source_target_pairs={{0,256},{256,0},{1,257},{257,1},{2,258},{258,2},{3,259},{259,3},{4... | collective-permute-start | bytes 1966088 | tf_op jit(solution)/shard_map/ppermute | solution.py:302
  24.2 4.4 %collective-permute-start.1 = (bf16[128,2560]{1,0:T(8,128)(2,1)S(1)}, bf16[128,2560]{1,0:T(8,128)(2,1)S(1)}, u32[]{:S(2)}, u32[]{:S(2)}) collective-permute-start(bf16[128,2560]{1,0:T(8,128)(2,1)S(1)} %pad_maximum_fusion.refs_4_), channel_id=1, source_target_pairs={{0,192},{64,0},{128,64},{192,128},{1,193},{65,1},{129,65},{193,129... | collective-permute-start | bytes 1966088 | tf_op jit(solution)/shard_map/ppermute | solution.py:307
  28.5 1.9 %collective-permute-start = (bf16[128,2560]{1,0:T(8,128)(2,1)S(1)}, bf16[128,2560]{1,0:T(8,128)(2,1)S(1)}, u32[]{:S(2)}, u32[]{:S(2)}) collective-permute-start(bf16[128,2560]{1,0:T(8,128)(2,1)S(1)} %pad_maximum_fusion.refs_4_), channel_id=1, source_target_pairs={{0,64},{64,128},{128,192},{192,0},{1,65},{65,129},{129,193},{193,1... | collective-permute-start | bytes 1966088 | tf_op jit(solution)/shard_map/ppermute | solution.py:307
  30.5 31.6 %collective-permute-done.4.refs_9_ = bf16[128,2560]{1,0:T(8,128)(2,1)S(1)} collective-permute-done((bf16[128,2560]{1,0:T(8,128)(2,1)S(1)}, bf16[128,2560]{1,0:T(8,128)(2,1)S(1)}, u32[]{:S(2)}, u32[]{:S(2)}) %collective-permute-start.4) | collective-permute-done | bytes 655392 | tf_op jit(solution)/shard_map/ppermute | solution.py:302
  62.1 4.4 %collective-permute-start.6 = (bf16[128,2560]{1,0:T(8,128)(2,1)S(1)}, bf16[128,2560]{1,0:T(8,128)(2,1)S(1)}, u32[]{:S(2)}, u32[]{:S(2)}) collective-permute-start(bf16[128,2560]{1,0:T(8,128)(2,1)S(1)} %collective-permute-done.4.refs_9_), channel_id=1, source_target_pairs={{0,192},{64,0},{128,64},{192,128},{1,193},{65,1},{129,65},{193,129... | collective-permute-start | bytes 1966088 | tf_op jit(solution)/shard_map/ppermute | solution.py:307
  66.5 1.9 %collective-permute-start.5 = (bf16[128,2560]{1,0:T(8,128)(2,1)S(1)}, bf16[128,2560]{1,0:T(8,128)(2,1)S(1)}, u32[]{:S(2)}, u32[]{:S(2)}) collective-permute-start(bf16[128,2560]{1,0:T(8,128)(2,1)S(1)} %collective-permute-done.4.refs_9_), channel_id=1, source_target_pairs={{0,64},{64,128},{128,192},{192,0},{1,65},{65,129},{129,193},{193,1... | collective-permute-start | bytes 1966088 | tf_op jit(solution)/shard_map/ppermute | solution.py:307
  69.3 4.6 %collective-permute-start.3 = (bf16[64,2560]{1,0:T(8,128)(2,1)}, bf16[64,2560]{1,0:T(8,128)(2,1)S(1)}, u32[]{:S(2)}, u32[]{:S(2)}) collective-permute-start(bf16[64,2560]{1,0:T(8,128)(2,1)} %slice.26), channel_id=1, source_target_pairs={{0,192},{64,0},{128,64},{192,128},{1,193},{65,1},{129,65},{193,129... | collective-permute-start | bytes 983048 | tf_op jit(solution)/shard_map/ppermute | solution.py:307
  76.6 3.3 %collective-permute-done.6.refs_11_ = bf16[128,2560]{1,0:T(8,128)(2,1)S(1)} collective-permute-done((bf16[128,2560]{1,0:T(8,128)(2,1)S(1)}, bf16[128,2560]{1,0:T(8,128)(2,1)S(1)}, u32[]{:S(2)}, u32[]{:S(2)}) %collective-permute-start.6) | collective-permute-done | bytes 655392 | tf_op jit(solution)/shard_map/ppermute | solution.py:307
  80.7 5.3 %collective-permute-start.8 = (bf16[64,2560]{1,0:T(8,128)(2,1)}, bf16[64,2560]{1,0:T(8,128)(2,1)}, u32[]{:S(2)}, u32[]{:S(2)}) collective-permute-start(bf16[64,2560]{1,0:T(8,128)(2,1)} %slice.28), channel_id=1, source_target_pairs={{0,192},{64,0},{128,64},{192,128},{1,193},{65,1},{129,65},{193,129... | collective-permute-start | bytes 983048 | tf_op jit(solution)/shard_map/ppermute | solution.py:307
  88.8 3.6 %slopes.1 = (f32[448,768]{1,0:T(8,128)}, f32[448,768]{1,0:T(8,128)}, bf16[448,768]{1,0:T(8,128)(2,1)}) custom-call(bf16[448,1536]{1,0:T(8,128)(2,1)} %bitcast.26), custom_call_target="tpu_custom_call" | custom-call | tf_op jit(solution)/shard_map/slopes/pallas_call | solution.py:125
  93.7 3.9 %collective-permute-done.7.refs_12_ = bf16[64,2560]{1,0:T(8,128)(2,1)} collective-permute-done((bf16[64,2560]{1,0:T(8,128)(2,1)}, bf16[64,2560]{1,0:T(8,128)(2,1)}, u32[]{:S(2)}, u32[]{:S(2)}) %collective-permute-start.7) | collective-permute-done | bytes 327712 | tf_op jit(solution)/shard_map/ppermute | solution.py:307
  97.6 7.4 %grads.1 = (bf16[3584,128]{1,0:T(8,128)(2,1)}, bf16[448,1536]{1,0:T(8,128)(2,1)}, bf16[2,448,256]{2,1,0:T(8,128)(2,1)}) custom-call(s32[2]{0:T(128)} %pad_add_fusion.refs_0_.where_ref, bf16[7168,128]{1,0:T(8,128)(2,1)S(1)} %bitcast.23, f32[448,768]{1,0:T(8,128)} %get-tuple-element.16.refs_2_, f32[448,768]{1,0:T(8,128)} %get-tuple-element.17.refs_3_, ...), custom_call_target="tpu_custom_call" | custom-call | tf_op jit(solution)/shard_map/grads/pallas_call | solution.py:194
  105.0 31.7 %all-to-all-start.1 = ((bf16[64,56,128]{2,1,0:T(8,128)(2,1)}), bf16[64,56,128]{2,1,0:T(8,128)(2,1)S(1)}, u32[]{:S(2)}, u32[]{:S(2)}) async-start(bf16[64,56,128]{2,1,0:T(8,128)(2,1)} %bitcast.27), calls=%async_computation.1 | async-start | bytes 1835008 | tf_op jit(solution)/shard_map/all_to_all | solution.py:312
  136.7 4.5 %terms.1 = (f32[2,3,32,768]{3,2,1,0:T(8,128)}, bf16[2,3,32,768]{3,2,1,0:T(8,128)(2,1)}, bf16[2,3,32,768]{3,2,1,0:T(8,128)(2,1)}, bf16[2,3,32,768]{3,2,1,0:T(8,128)(2,1)}) custom-call(s32[2]{0:T(128)} %pad_add_fusion.refs_0_.where_ref, bf16[448,1536]{1,0:T(8,128)(2,1)} %get-tuple-element.19.both_hbm, bf16[2,448,256]{2,1,0:T(8,128)(2,1)} %get-tuple-element.20.proj_hbm, ...), custom_call_target="tpu_custom_call" | custom-call | tf_op jit(solution)/shard_map/terms/pallas_call | solution.py:252
  141.2 1.9 %collective-permute-start.9 = (bf16[2,3,32,768]{3,2,1,0:T(8,128)(2,1)}, bf16[2,3,32,768]{3,2,1,0:T(8,128)(2,1)S(1)}, u32[]{:S(2)}, u32[]{:S(2)}) collective-permute-start(bf16[2,3,32,768]{3,2,1,0:T(8,128)(2,1)} %get-tuple-element.23), channel_id=1, source_target_pairs={{0,128},{64,192},{128,0},{192,64},{1,129},{65,193},{129,1},{193,65... | collective-permute-start | bytes 884744 | tf_op jit(solution)/shard_map/ppermute | solution.py:307
  143.1 1.9 %collective-permute-start.10 = (bf16[2,3,32,768]{3,2,1,0:T(8,128)(2,1)}, bf16[2,3,32,768]{3,2,1,0:T(8,128)(2,1)S(1)}, u32[]{:S(2)}, u32[]{:S(2)}) collective-permute-start(bf16[2,3,32,768]{3,2,1,0:T(8,128)(2,1)} %get-tuple-element.24), channel_id=1, source_target_pairs={{0,64},{64,128},{128,192},{192,0},{1,65},{65,129},{129,193},{193,1... | collective-permute-start | bytes 884744 | tf_op jit(solution)/shard_map/ppermute | solution.py:307
  145.0 4.6 %collective-permute-start.11 = (bf16[2,3,32,768]{3,2,1,0:T(8,128)(2,1)}, bf16[2,3,32,768]{3,2,1,0:T(8,128)(2,1)S(1)}, u32[]{:S(2)}, u32[]{:S(2)}) collective-permute-start(bf16[2,3,32,768]{3,2,1,0:T(8,128)(2,1)} %get-tuple-element.25), channel_id=1, source_target_pairs={{0,192},{64,0},{128,64},{192,128},{1,193},{65,1},{129,65},{193,129... | collective-permute-start | bytes 884744 | tf_op jit(solution)/shard_map/ppermute | solution.py:307
  149.6 3.4 %collective-permute-done.9 = bf16[2,3,32,768]{3,2,1,0:T(8,128)(2,1)S(1)} collective-permute-done((bf16[2,3,32,768]{3,2,1,0:T(8,128)(2,1)}, bf16[2,3,32,768]{3,2,1,0:T(8,128)(2,1)S(1)}, u32[]{:S(2)}, u32[]{:S(2)}) %collective-permute-start.9) | collective-permute-done | bytes 294944 | tf_op jit(solution)/shard_map/ppermute | solution.py:307
  153.0 7.0 %collective-permute-done.10 = bf16[2,3,32,768]{3,2,1,0:T(8,128)(2,1)S(1)} collective-permute-done((bf16[2,3,32,768]{3,2,1,0:T(8,128)(2,1)}, bf16[2,3,32,768]{3,2,1,0:T(8,128)(2,1)S(1)}, u32[]{:S(2)}, u32[]{:S(2)}) %collective-permute-start.10) | collective-permute-done | bytes 294944 | tf_op jit(solution)/shard_map/ppermute | solution.py:307
  161.3 4.4 %collective-permute-start.12 = (bf16[3,32,768]{2,1,0:T(8,128)(2,1)S(1)}, bf16[3,32,768]{2,1,0:T(8,128)(2,1)S(1)}, u32[]{:S(2)}, u32[]{:S(2)}) collective-permute-start(bf16[3,32,768]{2,1,0:T(8,128)(2,1)S(1)} %fusion.2), channel_id=1, source_target_pairs={{0,256},{256,0},{1,257},{257,1},{2,258},{258,2},{3,259},{259,3},{4... | collective-permute-start | bytes 442376 | tf_op jit(solution)/shard_map/ppermute | solution.py:302
  165.7 10.1 %collective-permute-done.12 = bf16[3,32,768]{2,1,0:T(8,128)(2,1)S(1)} collective-permute-done((bf16[3,32,768]{2,1,0:T(8,128)(2,1)S(1)}, bf16[3,32,768]{2,1,0:T(8,128)(2,1)S(1)}, u32[]{:S(2)}, u32[]{:S(2)}) %collective-permute-start.12) | collective-permute-done | bytes 147488 | tf_op jit(solution)/shard_map/ppermute | solution.py:302
  176.6 2.2 %combine.1 = bf16[128,1024]{1,0:T(8,128)(2,1)} custom-call(bf16[448,128]{1,0:T(8,128)(2,1)} %get-tuple-element.14.match_ref, bf16[3584,128]{1,0:T(8,128)(2,1)S(1)} %bitcast.24), custom_call_target="tpu_custom_call" | custom-call | tf_op jit(solution)/shard_map/combine/pallas_call | solution.py:293
  (42 shorter events, 10.5 us)
Async XLA Ops:
  4.6 14.7 %copy-start.7 = (bf16[1,128,768]{2,1,0:T(8,128)(2,1)S(1)}, bf16[1,128,768]{2,1,0:T(8,128)(2,1)}, u32[]{:S(2)}) copy-start(bf16[1,128,768]{2,1,0:T(8,128)(2,1)} %param.15) | copy-start | bytes 589828
  4.6 14.7 %copy-start.8 = (bf16[1,128,768]{2,1,0:T(8,128)(2,1)S(1)}, bf16[1,128,768]{2,1,0:T(8,128)(2,1)}, u32[]{:S(2)}) copy-start(bf16[1,128,768]{2,1,0:T(8,128)(2,1)} %param.14) | copy-start | bytes 589828
  4.6 14.7 %copy-start.9 = (bf16[1,128,768]{2,1,0:T(8,128)(2,1)S(1)}, bf16[1,128,768]{2,1,0:T(8,128)(2,1)}, u32[]{:S(2)}) copy-start(bf16[1,128,768]{2,1,0:T(8,128)(2,1)} %param.16) | copy-start | bytes 589828
  4.6 14.7 %copy-start.10 = (bf16[1,128,256]{2,1,0:T(8,128)(2,1)S(1)}, bf16[1,128,256]{2,1,0:T(8,128)(2,1)}, u32[]{:S(2)}) copy-start(bf16[1,128,256]{2,1,0:T(8,128)(2,1)} %param.17) | copy-start | bytes 196612
  4.6 93.0 %all-to-all-start = ((bf16[64,112,128]{2,1,0:T(8,128)(2,1)}), bf16[64,112,128]{2,1,0:T(8,128)(2,1)S(1)}, u32[]{:S(2)}, u32[]{:S(2)}) async-start(bf16[64,112,128]{2,1,0:T(8,128)(2,1)} %bitcast.25), calls=%async_computation | async-start | bytes 3670016 | tf_op jit(solution)/shard_map/all_to_all | solution.py:312
  19.4 67.5 %copy-start = (bf16[128,2560]{1,0:T(8,128)(2,1)}, bf16[128,2560]{1,0:T(8,128)(2,1)S(1)}, u32[]{:S(2)}) copy-start(bf16[128,2560]{1,0:T(8,128)(2,1)S(1)} %pad_maximum_fusion.refs_4_) | copy-start | bytes 1966084
  19.4 42.7 %collective-permute-start.4 = (bf16[128,2560]{1,0:T(8,128)(2,1)S(1)}, bf16[128,2560]{1,0:T(8,128)(2,1)S(1)}, u32[]{:S(2)}, u32[]{:S(2)}) collective-permute-start(bf16[128,2560]{1,0:T(8,128)(2,1)S(1)} %pad_maximum_fusion.refs_4_), channel_id=1, source_target_pairs={{0,256},{256,0},{1,257},{257,1},{2,258},{258,2},{3,259},{259,3},{4... | collective-permute-start | bytes 1966088 | tf_op jit(solution)/shard_map/ppermute | solution.py:302
  24.2 44.3 %collective-permute-start.1 = (bf16[128,2560]{1,0:T(8,128)(2,1)S(1)}, bf16[128,2560]{1,0:T(8,128)(2,1)S(1)}, u32[]{:S(2)}, u32[]{:S(2)}) collective-permute-start(bf16[128,2560]{1,0:T(8,128)(2,1)S(1)} %pad_maximum_fusion.refs_4_), channel_id=1, source_target_pairs={{0,192},{64,0},{128,64},{192,128},{1,193},{65,1},{129,65},{193,129... | collective-permute-start | bytes 1966088 | tf_op jit(solution)/shard_map/ppermute | solution.py:307
  28.5 45.3 %collective-permute-start = (bf16[128,2560]{1,0:T(8,128)(2,1)S(1)}, bf16[128,2560]{1,0:T(8,128)(2,1)S(1)}, u32[]{:S(2)}, u32[]{:S(2)}) collective-permute-start(bf16[128,2560]{1,0:T(8,128)(2,1)S(1)} %pad_maximum_fusion.refs_4_), channel_id=1, source_target_pairs={{0,64},{64,128},{128,192},{192,0},{1,65},{65,129},{129,193},{193,1... | collective-permute-start | bytes 1966088 | tf_op jit(solution)/shard_map/ppermute | solution.py:307
  62.1 35.5 %copy-start.5 = (bf16[128,2560]{1,0:T(8,128)(2,1)}, bf16[128,2560]{1,0:T(8,128)(2,1)S(1)}, u32[]{:S(2)}) copy-start(bf16[128,2560]{1,0:T(8,128)(2,1)S(1)} %collective-permute-done.4.refs_9_) | copy-start | bytes 1966084
  62.1 17.8 %collective-permute-start.6 = (bf16[128,2560]{1,0:T(8,128)(2,1)S(1)}, bf16[128,2560]{1,0:T(8,128)(2,1)S(1)}, u32[]{:S(2)}, u32[]{:S(2)}) collective-permute-start(bf16[128,2560]{1,0:T(8,128)(2,1)S(1)} %collective-permute-done.4.refs_9_), channel_id=1, source_target_pairs={{0,192},{64,0},{128,64},{192,128},{1,193},{65,1},{129,65},{193,129... | collective-permute-start | bytes 1966088 | tf_op jit(solution)/shard_map/ppermute | solution.py:307
  66.5 19.5 %collective-permute-start.5 = (bf16[128,2560]{1,0:T(8,128)(2,1)S(1)}, bf16[128,2560]{1,0:T(8,128)(2,1)S(1)}, u32[]{:S(2)}, u32[]{:S(2)}) collective-permute-start(bf16[128,2560]{1,0:T(8,128)(2,1)S(1)} %collective-permute-done.4.refs_9_), channel_id=1, source_target_pairs={{0,64},{64,128},{128,192},{192,0},{1,65},{65,129},{129,193},{193,1... | collective-permute-start | bytes 1966088 | tf_op jit(solution)/shard_map/ppermute | solution.py:307
  68.4 18.4 %copy-start.1 = (bf16[128,2560]{1,0:T(8,128)(2,1)}, bf16[128,2560]{1,0:T(8,128)(2,1)S(1)}, u32[]{:S(2)}) copy-start(bf16[128,2560]{1,0:T(8,128)(2,1)S(1)} %collective-permute-done.1.refs_6_) | copy-start | bytes 1966084
  69.3 23.7 %collective-permute-start.3 = (bf16[64,2560]{1,0:T(8,128)(2,1)}, bf16[64,2560]{1,0:T(8,128)(2,1)S(1)}, u32[]{:S(2)}, u32[]{:S(2)}) collective-permute-start(bf16[64,2560]{1,0:T(8,128)(2,1)} %slice.26), channel_id=1, source_target_pairs={{0,192},{64,0},{128,64},{192,128},{1,193},{65,1},{129,65},{193,129... | collective-permute-start | bytes 983048 | tf_op jit(solution)/shard_map/ppermute | solution.py:307
  73.9 18.5 %copy-start.2 = (bf16[128,2560]{1,0:T(8,128)(2,1)}, bf16[128,2560]{1,0:T(8,128)(2,1)S(1)}, u32[]{:S(2)}) copy-start(bf16[128,2560]{1,0:T(8,128)(2,1)S(1)} %collective-permute-done.refs_5_) | copy-start | bytes 1966084
  74.7 18.3 %collective-permute-start.2 = (bf16[64,2560]{1,0:T(8,128)(2,1)}, bf16[64,2560]{1,0:T(8,128)(2,1)}, u32[]{:S(2)}, u32[]{:S(2)}) collective-permute-start(bf16[64,2560]{1,0:T(8,128)(2,1)} %slice.25), channel_id=1, source_target_pairs={{0,64},{64,128},{128,192},{192,0},{1,65},{65,129},{129,193},{193,1... | collective-permute-start | bytes 983048 | tf_op jit(solution)/shard_map/ppermute | solution.py:307
  79.9 8.9 %copy-start.3 = (bf16[128,2560]{1,0:T(8,128)(2,1)}, bf16[128,2560]{1,0:T(8,128)(2,1)S(1)}, u32[]{:S(2)}) copy-start(bf16[128,2560]{1,0:T(8,128)(2,1)S(1)} %collective-permute-done.6.refs_11_) | copy-start | bytes 1966084
  80.7 13.1 %collective-permute-start.8 = (bf16[64,2560]{1,0:T(8,128)(2,1)}, bf16[64,2560]{1,0:T(8,128)(2,1)}, u32[]{:S(2)}, u32[]{:S(2)}) collective-permute-start(bf16[64,2560]{1,0:T(8,128)(2,1)} %slice.28), channel_id=1, source_target_pairs={{0,192},{64,0},{128,64},{192,128},{1,193},{65,1},{129,65},{193,129... | collective-permute-start | bytes 983048 | tf_op jit(solution)/shard_map/ppermute | solution.py:307
  86.8 10.8 %collective-permute-start.7 = (bf16[64,2560]{1,0:T(8,128)(2,1)}, bf16[64,2560]{1,0:T(8,128)(2,1)}, u32[]{:S(2)}, u32[]{:S(2)}) collective-permute-start(bf16[64,2560]{1,0:T(8,128)(2,1)} %slice.27), channel_id=1, source_target_pairs={{0,64},{64,128},{128,192},{192,0},{1,65},{65,129},{129,193},{193,1... | collective-permute-start | bytes 983048 | tf_op jit(solution)/shard_map/ppermute | solution.py:307
  105.0 71.6 %all-to-all-start.1 = ((bf16[64,56,128]{2,1,0:T(8,128)(2,1)}), bf16[64,56,128]{2,1,0:T(8,128)(2,1)S(1)}, u32[]{:S(2)}, u32[]{:S(2)}) async-start(bf16[64,56,128]{2,1,0:T(8,128)(2,1)} %bitcast.27), calls=%async_computation.1 | async-start | bytes 1835008 | tf_op jit(solution)/shard_map/all_to_all | solution.py:312
  141.2 11.8 %collective-permute-start.9 = (bf16[2,3,32,768]{3,2,1,0:T(8,128)(2,1)}, bf16[2,3,32,768]{3,2,1,0:T(8,128)(2,1)S(1)}, u32[]{:S(2)}, u32[]{:S(2)}) collective-permute-start(bf16[2,3,32,768]{3,2,1,0:T(8,128)(2,1)} %get-tuple-element.23), channel_id=1, source_target_pairs={{0,128},{64,192},{128,0},{192,64},{1,129},{65,193},{129,1},{193,65... | collective-permute-start | bytes 884744 | tf_op jit(solution)/shard_map/ppermute | solution.py:307
  143.1 16.9 %collective-permute-start.10 = (bf16[2,3,32,768]{3,2,1,0:T(8,128)(2,1)}, bf16[2,3,32,768]{3,2,1,0:T(8,128)(2,1)S(1)}, u32[]{:S(2)}, u32[]{:S(2)}) collective-permute-start(bf16[2,3,32,768]{3,2,1,0:T(8,128)(2,1)} %get-tuple-element.24), channel_id=1, source_target_pairs={{0,64},{64,128},{128,192},{192,0},{1,65},{65,129},{129,193},{193,1... | collective-permute-start | bytes 884744 | tf_op jit(solution)/shard_map/ppermute | solution.py:307
  145.0 15.0 %collective-permute-start.11 = (bf16[2,3,32,768]{3,2,1,0:T(8,128)(2,1)}, bf16[2,3,32,768]{3,2,1,0:T(8,128)(2,1)S(1)}, u32[]{:S(2)}, u32[]{:S(2)}) collective-permute-start(bf16[2,3,32,768]{3,2,1,0:T(8,128)(2,1)} %get-tuple-element.25), channel_id=1, source_target_pairs={{0,192},{64,0},{128,64},{192,128},{1,193},{65,1},{129,65},{193,129... | collective-permute-start | bytes 884744 | tf_op jit(solution)/shard_map/ppermute | solution.py:307
  161.3 14.6 %collective-permute-start.12 = (bf16[3,32,768]{2,1,0:T(8,128)(2,1)S(1)}, bf16[3,32,768]{2,1,0:T(8,128)(2,1)S(1)}, u32[]{:S(2)}, u32[]{:S(2)}) collective-permute-start(bf16[3,32,768]{2,1,0:T(8,128)(2,1)S(1)} %fusion.2), channel_id=1, source_target_pairs={{0,256},{256,0},{1,257},{257,1},{2,258},{258,2},{3,259},{259,3},{4... | collective-permute-start | bytes 442376 | tf_op jit(solution)/shard_map/ppermute | solution.py:302
  (2 other events, 7.4 us)

commit v5 on v4

--- a/solution.py
+++ b/solution.py
@@ -20,7 +20,13 @@
     return pl.ds(start, slots, stride=step)
 
 
-def pack_kernel(cap, ids_ref, probs_ref, tok_ref, grad_ref, out_ref, match_ref, wide_ref):
+def write_rows(rows, first, wide_ref, step):
+    slots = rows.shape[0]
+    for i in range(rows.shape[1] // LANES):
+        wide_ref[chunk_rows(first + i, slots, step), :] = rows[:, i * LANES : (i + 1) * LANES]
+
+
+def pack_grad_kernel(cap, ids_ref, probs_ref, grad_ref, out_ref, match_ref, wide_ref):
     slots, n_tok = match_ref.shape
     topk = ids_ref.shape[0]
     n_owner = slots // cap
@@ -45,34 +51,48 @@
     weight = jnp.sum(weight, axis=1, keepdims=True)
     match = match.astype(BF16)
     match_ref[...] = match
-    n_chunk = tok_ref.shape[1] // LANES
-    for half, src in enumerate((tok_ref, grad_ref)):
-        for c in range(0, n_chunk, 2):
-            rows = jnp.dot(
-                match, src[:, c * LANES : (c + 2) * LANES], preferred_element_type=F32
-            )
-            if half:
-                rows = rows * weight
-            for i in range(2):
-                wide_ref[chunk_rows(half * n_chunk + c + i, slots, 2 * n_chunk), :] = rows[
-                    :, i * LANES : (i + 1) * LANES
-                ]
+    n_chunk = grad_ref.shape[1] // LANES
+    for c in range(0, n_chunk, 2):
+        rows = jnp.dot(
+            match, grad_ref[:, c * LANES : (c + 2) * LANES], preferred_element_type=F32
+        )
+        write_rows(rows * weight, c, wide_ref, n_chunk)
     out_ref[...] = wide_ref[...].astype(BF16)
 
 
-def pack(ids, probs, tokens, out_grad, n_owner, cap):
-    n_tok, width = tokens.shape
+def pack_grad(ids, probs, out_grad, n_owner, cap):
+    n_tok, width = out_grad.shape
     slots = n_owner * cap
-    rows = slots * 2 * width // LANES
-    return pl.pallas_call(
-        functools.partial(pack_kernel, cap),
+    rows = slots * width // LANES
+    return pl.pallas_call(
+        functools.partial(pack_grad_kernel, cap),
         out_shape=(
             jax.ShapeDtypeStruct((rows, LANES), BF16),
             jax.ShapeDtypeStruct((slots, n_tok), BF16),
         ),
         scratch_shapes=[pltpu.VMEM((rows, LANES), F32)],
-        name="pack",
-    )(ids, probs, tokens, out_grad)
+        name="pack_grad",
+    )(ids, probs, out_grad)
+
+
+def pack_token_kernel(match_ref, tok_ref, out_ref, wide_ref):
+    n_chunk = tok_ref.shape[1] // LANES
+    for c in range(0, n_chunk, 2):
+        rows = jnp.dot(
+            match_ref[...], tok_ref[:, c * LANES : (c + 2) * LANES], preferred_element_type=F32
+        )
+        write_rows(rows, c, wide_ref, n_chunk)
+    out_ref[...] = wide_ref[...].astype(BF16)
+
+
+def pack_token(match, tokens):
+    rows = match.shape[0] * tokens.shape[1] // LANES
+    return pl.pallas_call(
+        pack_token_kernel,
+        out_shape=jax.ShapeDtypeStruct((rows, LANES), BF16),
+        scratch_shapes=[pltpu.VMEM((rows, LANES), F32)],
+        name="pack_token",
+    )(match, tokens)
 
 
 def near(value):
@@ -133,12 +153,13 @@
     )(pre)
 
 
-def spread(wide_ref, first, step, into):
+def spread(wide_ref, into):
     slots, width = into.shape
-    for c in range(width // LANES):
-        into[:, c * LANES : (c + 1) * LANES] = wide_ref[
-            chunk_rows(first + c, slots, step), :
-        ].astype(BF16)
+    n_chunk = width // LANES
+    for c in range(n_chunk):
+        into[:, c * LANES : (c + 1) * LANES] = wide_ref[chunk_rows(c, slots, n_chunk), :].astype(
+            BF16
+        )
 
 
 def grads_kernel(places, *refs):
@@ -146,16 +167,15 @@
     where_ref, got_ref, act_hbm, slope_hbm = refs[:4]
     pieces = refs[4 : 4 + n]
     row_hbm, both_hbm, proj_hbm = refs[4 + n : 7 + n]
-    wide, x_rows, dy_rows, rows_wide, w1, w2, act, slope, row, both, proj, sems = refs[7 + n :]
+    wide, dy_rows, rows_wide, w1, w2, act, slope, row, both, proj, sems = refs[7 + n :]
     hidden = act.shape[1]
-    slots, width = dy_rows.shape
+    _, width = dy_rows.shape
     n_chunk = width // LANES
     first = fetch(where_ref, pieces, places, pl.ds(0, w1.shape[1]), w1, sems, 0)
     middle = fetch_all((slope_hbm, act_hbm), (slope, act), sems, 2 * n)
     last = fetch(where_ref, pieces, places, pl.ds(w1.shape[1], w2.shape[1]), w2, sems, n)
     wide[...] = got_ref[...].astype(F32)
-    spread(wide, n_chunk, 2 * n_chunk, dy_rows)
-    spread(wide, 0, 2 * n_chunk, x_rows)
+    spread(wide, dy_rows)
     for copy in first:
         copy.wait()
     grad = jnp.dot(dy_rows[...], w1[:, :hidden], preferred_element_type=F32)
@@ -163,9 +183,6 @@
         copy.wait()
     both[:, :hidden] = (grad * slope[...]).astype(BF16)
     both[:, hidden:] = (grad * act[...]).astype(BF16)
-    proj[0] = jnp.dot(x_rows[...], w1[:, hidden:], preferred_element_type=F32).astype(BF16)
-    proj[1] = jnp.dot(dy_rows[...], w1[:, hidden:], preferred_element_type=F32).astype(BF16)
-    sent = fetch_all((both, proj), (both_hbm, proj_hbm), sems, 2 * n + 2)
     for copy in last:
         copy.wait()
     for c in range(0, n_chunk, 2):
@@ -175,64 +192,67 @@
             (((1,), (1,)), ((), ())),
             preferred_element_type=F32,
         )
-        rows_wide[chunk_rows(c, slots, n_chunk), :] = rows[:, :LANES]
-        rows_wide[chunk_rows(c + 1, slots, n_chunk), :] = rows[:, LANES:]
-    size = row.shape[0] // 2
-    for i in range(2):
-        here = slice(i * size, (i + 1) * size)
-        row[here, :] = rows_wide[here, :].astype(BF16)
-        sent += fetch_all((row.at[here, :],), (row_hbm.at[here, :],), sems, 2 * n + 4 + i)
-    for copy in sent:
+        write_rows(rows, c, rows_wide, n_chunk)
+    row[...] = rows_wide[...].astype(BF16)
+    proj[...] = jnp.dot(dy_rows[...], w1[:, hidden:], preferred_element_type=F32).astype(BF16)
+    for copy in fetch_all((row, both, proj), (row_hbm, both_hbm, proj_hbm), sems, 2 * n + 2):
         copy.wait()
 
 
 def grads(where, got, act, slope, pieces, places, rank):
     slots, hidden = act.shape
-    width = got.shape[0] * LANES // slots // 2
-    rows = slots * width // LANES
+    width = got.shape[0] * LANES // slots
     n = len(pieces)
     return pl.pallas_call(
         functools.partial(grads_kernel, places),
         in_specs=[pl.BlockSpec(memory_space=pltpu.SMEM), in_vmem()] + [in_place()] * (2 + n),
         out_specs=(in_place(),) * 3,
         out_shape=(
-            jax.ShapeDtypeStruct((rows, LANES), BF16),
+            jax.ShapeDtypeStruct(got.shape, BF16),
             jax.ShapeDtypeStruct((slots, 2 * hidden), BF16),
-            jax.ShapeDtypeStruct((2, slots, rank), BF16),
+            jax.ShapeDtypeStruct((slots, rank), BF16),
         ),
         scratch_shapes=[
             pltpu.VMEM(got.shape, F32),
             pltpu.VMEM((slots, width), BF16),
-            pltpu.VMEM((slots, width), BF16),
-            pltpu.VMEM((rows, LANES), F32),
+            pltpu.VMEM(got.shape, F32),
             pltpu.VMEM((width, hidden + rank), BF16),
             pltpu.VMEM((width, 2 * hidden), BF16),
             pltpu.VMEM((slots, hidden), F32),
             pltpu.VMEM((slots, hidden), F32),
-            pltpu.VMEM((rows, LANES), BF16),
+            pltpu.VMEM(got.shape, BF16),
             pltpu.VMEM((slots, 2 * hidden), BF16),
-            pltpu.VMEM((2, slots, rank), BF16),
-            pltpu.SemaphoreType.DMA((2 * n + 6,)),
+            pltpu.VMEM((slots, rank), BF16),
+            pltpu.SemaphoreType.DMA((2 * n + 5,)),
         ],
         name="grads",
     )(where, near(got), act, slope, *pieces)
 
 
-def terms_kernel(where_ref, both_hbm, proj_hbm, hid_hbm, *refs):
-    part_refs = refs[:4]
-    both, proj, hid, term_ref, sems = refs[4:]
+def terms_kernel(places, *refs):
+    n = len(places)
+    where_ref, got_ref, both_hbm, proj_hbm, hid_hbm = refs[:5]
+    pieces = refs[5 : 5 + n]
+    part_refs = refs[5 + n : 9 + n]
+    both, proj, hid, basis, wide, x_rows, term_ref, sems = refs[9 + n :]
     hidden = hid.shape[1]
-    proj_in, both_in, hid_in = fetch_all(
-        (proj_hbm, both_hbm, hid_hbm), (proj, both, hid), sems, 0
+    columns = pl.ds(hidden, basis.shape[1])
+    first = fetch(where_ref, pieces, places, columns, basis, sems, 0)
+    proj_in, hid_in, both_in = fetch_all(
+        (proj_hbm, hid_hbm, both_hbm), (proj, hid, both), sems, n
     )
+    wide[...] = got_ref[...].astype(F32)
+    spread(wide, x_rows)
+    for copy in first:
+        copy.wait()
+    x_proj = jnp.dot(x_rows[...], basis[...], preferred_element_type=F32).astype(BF16)
     by_rows = (((0,), (0,)), ((), ()))
     proj_in.wait()
+    hid_in.wait()
+    term_ref[2] = lax.dot_general(proj[...], hid[...], by_rows, preferred_element_type=F32)
     both_in.wait()
-    x_proj = proj[0]
     term_ref[0] = lax.dot_general(x_proj, both[:, :hidden], by_rows, preferred_element_type=F32)
     term_ref[1] = lax.dot_general(x_proj, both[:, hidden:], by_rows, preferred_element_type=F32)
-    hid_in.wait()
-    term_ref[2] = lax.dot_general(proj[1], hid[...], by_rows, preferred_element_type=F32)
     high, low = where_ref[0], where_ref[1]
     n_term, part = term_ref.shape[0], part_refs[0].shape[2]
     for k, out in enumerate(part_refs):
@@ -245,13 +265,15 @@
                 )
 
 
-def terms(where, both, proj, hid, n_dp):
-    _, hidden = hid.shape
-    rank = proj.shape[2]
+def terms(where, got, both, proj, hid, pieces, places, n_dp):
+    slots, hidden = hid.shape
+    rank = proj.shape[1]
+    width = got.shape[0] * LANES // slots
     part = rank // n_dp
-    return pl.pallas_call(
-        terms_kernel,
-        in_specs=[pl.BlockSpec(memory_space=pltpu.SMEM)] + [in_place()] * 3,
+    n = len(pieces)
+    return pl.pallas_call(
+        functools.partial(terms_kernel, places),
+        in_specs=[pl.BlockSpec(memory_space=pltpu.SMEM), in_vmem()] + [in_place()] * (3 + n),
         out_shape=tuple(
             jax.ShapeDtypeStruct((2, 3, part, hidden), F32 if k == 0 else BF16) for k in range(4)
         ),
@@ -259,11 +281,14 @@
             pltpu.VMEM(both.shape, BF16),
             pltpu.VMEM(proj.shape, BF16),
             pltpu.VMEM(hid.shape, BF16),
+            pltpu.VMEM((width, rank), BF16),
+            pltpu.VMEM(got.shape, F32),
+            pltpu.VMEM((slots, width), BF16),
             pltpu.VMEM((3, rank, hidden), F32),
-            pltpu.SemaphoreType.DMA((3,)),
+            pltpu.SemaphoreType.DMA((n + 3,)),
         ],
         name="terms",
-    )(where, both, proj, hid)
+    )(where, near(got), both, proj, hid, *pieces)
 
 
 def take_pair(wide_ref, first, second, slots, step):
@@ -326,21 +351,23 @@
 
     own = jnp.concatenate([down_weight[0], basis[0], gate_weight[0], up_weight[0]], axis=1)
     far = swap(own)
-    sent, match = pack(expert_ids.T, gate_probs.T, tokens, out_grad, n_owner, cap)
-    got = exchange(sent, n_owner)
-    pieces, places = [], []
+    sent_grad, match = pack_grad(expert_ids.T, gate_probs.T, out_grad, n_owner, cap)
+    got_grad = exchange(sent_grad, n_owner)
+    sent_token = pack_token(match, tokens)
+    got_token = exchange(sent_token, n_owner)
     half = own.shape[0] // 2
-    for other, block in enumerate((own, far)):
-        left, right = shifted(block, 1), shifted(block, -1)
-        top, bottom = shifted(left[:half], 1), shifted(right[half:], -1)
-        pieces += [block, left, right, top, bottom]
-        places += [(other, 0, 0), (other, 1, 0), (other, 3, 0), (other, 2, 0), (other, 2, half)]
+    pieces = [own] + [shifted(own, k) for k in (2, 1, 3)]
+    places = [(0, 0, 0), (0, 2, 0), (0, 1, 0), (0, 3, 0)]
+    left, right = shifted(far, 1), shifted(far, -1)
+    top, bottom = shifted(left[:half], 1), shifted(right[half:], -1)
+    pieces += [far, left, right, top, bottom]
+    places += [(1, 0, 0), (1, 1, 0), (1, 3, 0), (1, 2, 0), (1, 2, half)]
+    places = tuple(places)
     rank = basis.shape[2]
     act, slope, hid = slopes(saved_pre[0, 0])
-    places = tuple(places)
-    row_grad, both, proj = grads(where, got, act, slope, pieces, places, rank)
+    row_grad, both, proj = grads(where, got_grad, act, slope, pieces, places, rank)
     back = exchange(row_grad, n_owner)
-    parts = terms(where, both, proj, hid, 8)
+    parts = terms(where, got_token, both, proj, hid, pieces, places, 8)
     summed = parts[0]
     for k in (2, 1, 3):
         summed = summed + shifted(parts[k], k).astype(F32)

time: 180 us -> 217 us (1.21)
  the two profiles are of different devices: /device:TPU:17 before, /device:TPU:24 now
where the time goes in v5:
time: 217 us; the launch traced here: 216 us
  waiting for transfers between devices  111 us (51%)
  starting transfers between devices  75.9 us (35%)
  Pallas kernels  23 us (11%)
  other arithmetic  2.56 us (1%)
  local copies, waits for them, and re-layouts  2.46 us (1%)
    ppermute x2, waiting for transfers between devices, swap(): return lax.ppermute(value, 'dp_0', [(0, 1), (1, 0)])  50.6 us
    ppermute x10, waiting for transfers between devices, shifted(): lax.ppermute(value, 'dp_1', [(i, (i + k) % size) for i in range(size)])  37.5 us
    ppermute x10, starting transfers between devices, shifted(): lax.ppermute(value, 'dp_1', [(i, (i + k) % size) for i in range(size)])  35.6 us
    all_to_all x3, starting transfers between devices, exchange(): lax.all_to_all(value.reshape(n_owner, rows // n_owner, lanes), 'expert',...  30.6 us
    all_to_all x3, waiting for transfers between devices, exchange(): lax.all_to_all(value.reshape(n_owner, rows // n_owner, lanes), 'expert',...  23.4 us
    ppermute x2, starting transfers between devices, swap(): return lax.ppermute(value, 'dp_0', [(0, 1), (1, 0)])  9.75 us
    pallas_call x1, Pallas kernels, grads(): pl.pallas_call(functools.partial(grads_kernel, places), in_specs=[pl.Bloc...  7.31 us
    pallas_call x1, Pallas kernels, terms(): pl.pallas_call(functools.partial(terms_kernel, places), in_specs=[pl.Bloc...  4.82 us
  transfers between devices with their start and end apart: 15, of which 10 were waited for; matrix products, arithmetic and copies ran while one was open for 2% of the time, Pallas kernels for 8%

profile of v5, /device:TPU:24, one launch (start us, length us, event | category | flops | bytes accessed | tf_op | source)
XLA Modules:
  0.0 216.3 jit_solution(9992938368825788391)
XLA Ops:
  0.6 2.6 %pack_grad.1 = (bf16[3584,128]{1,0:T(8,128)(2,1)}, bf16[448,128]{1,0:T(8,128)(2,1)}) custom-call(s32[3,128]{1,0:T(4,128)} %bitcast.36, f32[3,128]{1,0:T(4,128)} %bitcast.37, bf16[128,1024]{1,0:T(8,128)(2,1)} %grad_ref.1), custom_call_target="tpu_custom_call" | custom-call | tf_op jit(solution)/shard_map/pack_grad/pallas_call | solution.py:67
  3.2 14.1 %all-to-all-start = ((bf16[64,56,128]{2,1,0:T(8,128)(2,1)}), bf16[64,56,128]{2,1,0:T(8,128)(2,1)S(1)}, u32[]{:S(2)}, u32[]{:S(2)}) async-start(bf16[64,56,128]{2,1,0:T(8,128)(2,1)} %bitcast.31), calls=%async_computation | async-start | bytes 1835008 | tf_op jit(solution)/shard_map/all_to_all | solution.py:337
  17.4 2.5 %pack_token.1 = bf16[3584,128]{1,0:T(8,128)(2,1)} custom-call(bf16[448,128]{1,0:T(8,128)(2,1)} %get-tuple-element.14.match_ref, bf16[128,1024]{1,0:T(8,128)(2,1)} %tok_ref.1), custom_call_target="tpu_custom_call" | custom-call | tf_op jit(solution)/shard_map/pack_token/pallas_call | solution.py:90
  20.0 23.4 %all-to-all-done = bf16[64,56,128]{2,1,0:T(8,128)(2,1)S(1)} async-done(((bf16[64,56,128]{2,1,0:T(8,128)(2,1)}), bf16[64,56,128]{2,1,0:T(8,128)(2,1)S(1)}, u32[]{:S(2)}, u32[]{:S(2)}) %all-to-all-start) | async-done | bytes 917536 | tf_op jit(solution)/shard_map/all_to_all | solution.py:337
  43.4 5.8 %all-to-all-start.2 = ((bf16[64,56,128]{2,1,0:T(8,128)(2,1)}), bf16[64,56,128]{2,1,0:T(8,128)(2,1)S(1)}, u32[]{:S(2)}, u32[]{:S(2)}) async-start(bf16[64,56,128]{2,1,0:T(8,128)(2,1)} %bitcast.28), calls=%async_computation.2 | async-start | bytes 1835008 | tf_op jit(solution)/shard_map/all_to_all | solution.py:337
  49.3 5.0 %collective-permute-start.3 = (bf16[128,2560]{1,0:T(8,128)(2,1)S(1)}, bf16[128,2560]{1,0:T(8,128)(2,1)S(1)}, u32[]{:S(2)}, u32[]{:S(2)}) collective-permute-start(bf16[128,2560]{1,0:T(8,128)(2,1)S(1)} %pad_maximum_fusion.refs_4_.refs_5_), channel_id=1, source_target_pairs={{0,256},{256,0},{1,257},{257,1},{2,258},{258,2},{3,259},{259,3},{4... | collective-permute-start | bytes 1966088 | tf_op jit(solution)/shard_map/ppermute | solution.py:327
  54.3 41.6 %collective-permute-done.3.refs_8_.refs_9_ = bf16[128,2560]{1,0:T(8,128)(2,1)S(1)} collective-permute-done((bf16[128,2560]{1,0:T(8,128)(2,1)S(1)}, bf16[128,2560]{1,0:T(8,128)(2,1)S(1)}, u32[]{:S(2)}, u32[]{:S(2)}) %collective-permute-start.3) | collective-permute-done | bytes 655392 | tf_op jit(solution)/shard_map/ppermute | solution.py:327
  96.0 3.4 %collective-permute-start.4 = (bf16[128,2560]{1,0:T(8,128)(2,1)S(1)}, bf16[128,2560]{1,0:T(8,128)(2,1)S(1)}, u32[]{:S(2)}, u32[]{:S(2)}) collective-permute-start(bf16[128,2560]{1,0:T(8,128)(2,1)S(1)} %collective-permute-done.3.refs_8_.refs_9_), channel_id=1, source_target_pairs={{0,64},{64,128},{128,192},{192,0},{1,65},{65,129},{129,193},{193,1... | collective-permute-start | bytes 1966088 | tf_op jit(solution)/shard_map/ppermute | solution.py:332
  99.4 3.7 %collective-permute-start.5 = (bf16[128,2560]{1,0:T(8,128)(2,1)S(1)}, bf16[128,2560]{1,0:T(8,128)(2,1)S(1)}, u32[]{:S(2)}, u32[]{:S(2)}) collective-permute-start(bf16[128,2560]{1,0:T(8,128)(2,1)S(1)} %collective-permute-done.3.refs_8_.refs_9_), channel_id=1, source_target_pairs={{0,192},{64,0},{128,64},{192,128},{1,193},{65,1},{129,65},{193,129... | collective-permute-start | bytes 1966088 | tf_op jit(solution)/shard_map/ppermute | solution.py:332
  103.0 3.7 %collective-permute-start = (bf16[128,2560]{1,0:T(8,128)(2,1)S(1)}, bf16[128,2560]{1,0:T(8,128)(2,1)}, u32[]{:S(2)}, u32[]{:S(2)}) collective-permute-start(bf16[128,2560]{1,0:T(8,128)(2,1)S(1)} %pad_maximum_fusion.refs_4_.refs_5_), channel_id=1, source_target_pairs={{0,128},{64,192},{128,0},{192,64},{1,129},{65,193},{129,1},{193,65... | collective-permute-start | bytes 1966088 | tf_op jit(solution)/shard_map/ppermute | solution.py:332
  106.8 2.5 %collective-permute-start.1 = (bf16[128,2560]{1,0:T(8,128)(2,1)S(1)}, bf16[128,2560]{1,0:T(8,128)(2,1)}, u32[]{:S(2)}, u32[]{:S(2)}) collective-permute-start(bf16[128,2560]{1,0:T(8,128)(2,1)S(1)} %pad_maximum_fusion.refs_4_.refs_5_), channel_id=1, source_target_pairs={{0,64},{64,128},{128,192},{192,0},{1,65},{65,129},{129,193},{193,1... | collective-permute-start | bytes 1966088 | tf_op jit(solution)/shard_map/ppermute | solution.py:332
  109.3 4.6 %collective-permute-start.2 = (bf16[128,2560]{1,0:T(8,128)(2,1)S(1)}, bf16[128,2560]{1,0:T(8,128)(2,1)}, u32[]{:S(2)}, u32[]{:S(2)}) collective-permute-start(bf16[128,2560]{1,0:T(8,128)(2,1)S(1)} %pad_maximum_fusion.refs_4_.refs_5_), channel_id=1, source_target_pairs={{0,192},{64,0},{128,64},{192,128},{1,193},{65,1},{129,65},{193,129... | collective-permute-start | bytes 1966088 | tf_op jit(solution)/shard_map/ppermute | solution.py:332
  113.8 15.8 %collective-permute-done.4.refs_9_.refs_10_ = bf16[128,2560]{1,0:T(8,128)(2,1)S(1)} collective-permute-done((bf16[128,2560]{1,0:T(8,128)(2,1)S(1)}, bf16[128,2560]{1,0:T(8,128)(2,1)S(1)}, u32[]{:S(2)}, u32[]{:S(2)}) %collective-permute-start.4) | collective-permute-done | bytes 655392 | tf_op jit(solution)/shard_map/ppermute | solution.py:332
  134.0 5.3 %collective-permute-start.7 = (bf16[64,2560]{1,0:T(8,128)(2,1)}, bf16[64,2560]{1,0:T(8,128)(2,1)}, u32[]{:S(2)}, u32[]{:S(2)}) collective-permute-start(bf16[64,2560]{1,0:T(8,128)(2,1)} %slice.18), channel_id=1, source_target_pairs={{0,192},{64,0},{128,64},{192,128},{1,193},{65,1},{129,65},{193,129... | collective-permute-start | bytes 983048 | tf_op jit(solution)/shard_map/ppermute | solution.py:332
  139.4 3.5 %slopes.1 = (f32[448,768]{1,0:T(8,128)}, f32[448,768]{1,0:T(8,128)}, bf16[448,768]{1,0:T(8,128)(2,1)}) custom-call(bf16[448,1536]{1,0:T(8,128)(2,1)} %bitcast.29), custom_call_target="tpu_custom_call" | custom-call | tf_op jit(solution)/shard_map/slopes/pallas_call | solution.py:145
  147.1 3.2 %collective-permute-done.6.refs_11_.refs_12_ = bf16[64,2560]{1,0:T(8,128)(2,1)S(1)} collective-permute-done((bf16[64,2560]{1,0:T(8,128)(2,1)}, bf16[64,2560]{1,0:T(8,128)(2,1)S(1)}, u32[]{:S(2)}, u32[]{:S(2)}) %collective-permute-start.6) | collective-permute-done | bytes 327712 | tf_op jit(solution)/shard_map/ppermute | solution.py:332
  152.4 7.3 %grads.1 = (bf16[3584,128]{1,0:T(8,128)(2,1)}, bf16[448,1536]{1,0:T(8,128)(2,1)}, bf16[448,256]{1,0:T(8,128)(2,1)}) custom-call(s32[2]{0:T(128)} %pad_add_fusion.refs_0_, bf16[3584,128]{1,0:T(8,128)(2,1)S(1)} %bitcast.26, f32[448,768]{1,0:T(8,128)} %get-tuple-element.16.refs_2_, f32[448,768]{1,0:T(8,128)} %get-tuple-element.17.refs_3_, ...), custom_call_target="tpu_custom_call" | custom-call | tf_op jit(solution)/shard_map/grads/pallas_call | solution.py:206
  159.7 10.6 %all-to-all-start.1 = ((bf16[64,56,128]{2,1,0:T(8,128)(2,1)}), bf16[64,56,128]{2,1,0:T(8,128)(2,1)S(1)}, u32[]{:S(2)}, u32[]{:S(2)}) async-start(bf16[64,56,128]{2,1,0:T(8,128)(2,1)} %bitcast.30), calls=%async_computation.1 | async-start | bytes 1835008 | tf_op jit(solution)/shard_map/all_to_all | solution.py:337
  170.4 4.8 %terms.1 = (f32[2,3,32,768]{3,2,1,0:T(8,128)}, bf16[2,3,32,768]{3,2,1,0:T(8,128)(2,1)}, bf16[2,3,32,768]{3,2,1,0:T(8,128)(2,1)}, bf16[2,3,32,768]{3,2,1,0:T(8,128)(2,1)}) custom-call(s32[2]{0:T(128)} %pad_add_fusion.refs_0_, bf16[3584,128]{1,0:T(8,128)(2,1)S(1)} %bitcast.25, bf16[448,1536]{1,0:T(8,128)(2,1)} %get-tuple-element.19.refs_2_, ...), custom_call_target="tpu_custom_call" | custom-call | tf_op jit(solution)/shard_map/terms/pallas_call | solution.py:274
  175.2 4.8 %collective-permute-start.10 = (bf16[2,3,32,768]{3,2,1,0:T(8,128)(2,1)}, bf16[2,3,32,768]{3,2,1,0:T(8,128)(2,1)S(1)}, u32[]{:S(2)}, u32[]{:S(2)}) collective-permute-start(bf16[2,3,32,768]{3,2,1,0:T(8,128)(2,1)} %get-tuple-element.25), channel_id=1, source_target_pairs={{0,192},{64,0},{128,64},{192,128},{1,193},{65,1},{129,65},{193,129... | collective-permute-start | bytes 884744 | tf_op jit(solution)/shard_map/ppermute | solution.py:332
  182.0 3.7 %collective-permute-start.8 = (bf16[2,3,32,768]{3,2,1,0:T(8,128)(2,1)}, bf16[2,3,32,768]{3,2,1,0:T(8,128)(2,1)S(1)}, u32[]{:S(2)}, u32[]{:S(2)}) collective-permute-start(bf16[2,3,32,768]{3,2,1,0:T(8,128)(2,1)} %get-tuple-element.23), channel_id=1, source_target_pairs={{0,128},{64,192},{128,0},{192,64},{1,129},{65,193},{129,1},{193,65... | collective-permute-start | bytes 884744 | tf_op jit(solution)/shard_map/ppermute | solution.py:332
  186.9 11.5 %collective-permute-done.9 = bf16[2,3,32,768]{3,2,1,0:T(8,128)(2,1)S(1)} collective-permute-done((bf16[2,3,32,768]{3,2,1,0:T(8,128)(2,1)}, bf16[2,3,32,768]{3,2,1,0:T(8,128)(2,1)S(1)}, u32[]{:S(2)}, u32[]{:S(2)}) %collective-permute-start.9) | collective-permute-done | bytes 294944 | tf_op jit(solution)/shard_map/ppermute | solution.py:332
  199.6 4.7 %collective-permute-start.11 = (bf16[3,32,768]{2,1,0:T(8,128)(2,1)S(1)}, bf16[3,32,768]{2,1,0:T(8,128)(2,1)S(1)}, u32[]{:S(2)}, u32[]{:S(2)}) collective-permute-start(bf16[3,32,768]{2,1,0:T(8,128)(2,1)S(1)} %fusion.2), channel_id=1, source_target_pairs={{0,256},{256,0},{1,257},{257,1},{2,258},{258,2},{3,259},{259,3},{4... | collective-permute-start | bytes 442376 | tf_op jit(solution)/shard_map/ppermute | solution.py:327
  204.4 9.0 %collective-permute-done.11 = bf16[3,32,768]{2,1,0:T(8,128)(2,1)S(1)} collective-permute-done((bf16[3,32,768]{2,1,0:T(8,128)(2,1)S(1)}, bf16[3,32,768]{2,1,0:T(8,128)(2,1)S(1)}, u32[]{:S(2)}, u32[]{:S(2)}) %collective-permute-start.11) | collective-permute-done | bytes 147488 | tf_op jit(solution)/shard_map/ppermute | solution.py:327
  (37 shorter events, 17.9 us)
Async XLA Ops:
  3.2 40.1 %all-to-all-start = ((bf16[64,56,128]{2,1,0:T(8,128)(2,1)}), bf16[64,56,128]{2,1,0:T(8,128)(2,1)S(1)}, u32[]{:S(2)}, u32[]{:S(2)}) async-start(bf16[64,56,128]{2,1,0:T(8,128)(2,1)} %bitcast.31), calls=%async_computation | async-start | bytes 1835008 | tf_op jit(solution)/shard_map/all_to_all | solution.py:337
  17.4 31.8 %copy-start.5 = (bf16[1,128,768]{2,1,0:T(8,128)(2,1)S(1)}, bf16[1,128,768]{2,1,0:T(8,128)(2,1)}, u32[]{:S(2)}) copy-start(bf16[1,128,768]{2,1,0:T(8,128)(2,1)} %param.15) | copy-start | bytes 589828
  17.4 31.8 %copy-start.6 = (bf16[1,128,768]{2,1,0:T(8,128)(2,1)S(1)}, bf16[1,128,768]{2,1,0:T(8,128)(2,1)}, u32[]{:S(2)}) copy-start(bf16[1,128,768]{2,1,0:T(8,128)(2,1)} %param.14) | copy-start | bytes 589828
  17.4 31.8 %copy-start.7 = (bf16[1,128,768]{2,1,0:T(8,128)(2,1)S(1)}, bf16[1,128,768]{2,1,0:T(8,128)(2,1)}, u32[]{:S(2)}) copy-start(bf16[1,128,768]{2,1,0:T(8,128)(2,1)} %param.16) | copy-start | bytes 589828
  17.4 31.8 %copy-start.8 = (bf16[1,128,256]{2,1,0:T(8,128)(2,1)S(1)}, bf16[1,128,256]{2,1,0:T(8,128)(2,1)}, u32[]{:S(2)}) copy-start(bf16[1,128,256]{2,1,0:T(8,128)(2,1)} %param.17) | copy-start | bytes 196612
  43.4 116.4 %all-to-all-start.2 = ((bf16[64,56,128]{2,1,0:T(8,128)(2,1)}), bf16[64,56,128]{2,1,0:T(8,128)(2,1)S(1)}, u32[]{:S(2)}, u32[]{:S(2)}) async-start(bf16[64,56,128]{2,1,0:T(8,128)(2,1)} %bitcast.28), calls=%async_computation.2 | async-start | bytes 1835008 | tf_op jit(solution)/shard_map/all_to_all | solution.py:337
  49.3 93.6 %copy-start = (bf16[128,2560]{1,0:T(8,128)(2,1)}, bf16[128,2560]{1,0:T(8,128)(2,1)S(1)}, u32[]{:S(2)}) copy-start(bf16[128,2560]{1,0:T(8,128)(2,1)S(1)} %pad_maximum_fusion.refs_4_.refs_5_) | copy-start | bytes 1966084
  49.3 46.7 %collective-permute-start.3 = (bf16[128,2560]{1,0:T(8,128)(2,1)S(1)}, bf16[128,2560]{1,0:T(8,128)(2,1)S(1)}, u32[]{:S(2)}, u32[]{:S(2)}) collective-permute-start(bf16[128,2560]{1,0:T(8,128)(2,1)S(1)} %pad_maximum_fusion.refs_4_.refs_5_), channel_id=1, source_target_pairs={{0,256},{256,0},{1,257},{257,1},{2,258},{258,2},{3,259},{259,3},{4... | collective-permute-start | bytes 1966088 | tf_op jit(solution)/shard_map/ppermute | solution.py:327
  96.0 38.1 %copy-start.3 = (bf16[128,2560]{1,0:T(8,128)(2,1)}, bf16[128,2560]{1,0:T(8,128)(2,1)S(1)}, u32[]{:S(2)}) copy-start(bf16[128,2560]{1,0:T(8,128)(2,1)S(1)} %collective-permute-done.3.refs_8_.refs_9_) | copy-start | bytes 1966084
  96.0 33.7 %collective-permute-start.4 = (bf16[128,2560]{1,0:T(8,128)(2,1)S(1)}, bf16[128,2560]{1,0:T(8,128)(2,1)S(1)}, u32[]{:S(2)}, u32[]{:S(2)}) collective-permute-start(bf16[128,2560]{1,0:T(8,128)(2,1)S(1)} %collective-permute-done.3.refs_8_.refs_9_), channel_id=1, source_target_pairs={{0,64},{64,128},{128,192},{192,0},{1,65},{65,129},{129,193},{193,1... | collective-permute-start | bytes 1966088 | tf_op jit(solution)/shard_map/ppermute | solution.py:332
  99.4 33.0 %collective-permute-start.5 = (bf16[128,2560]{1,0:T(8,128)(2,1)S(1)}, bf16[128,2560]{1,0:T(8,128)(2,1)S(1)}, u32[]{:S(2)}, u32[]{:S(2)}) collective-permute-start(bf16[128,2560]{1,0:T(8,128)(2,1)S(1)} %collective-permute-done.3.refs_8_.refs_9_), channel_id=1, source_target_pairs={{0,192},{64,0},{128,64},{192,128},{1,193},{65,1},{129,65},{193,129... | collective-permute-start | bytes 1966088 | tf_op jit(solution)/shard_map/ppermute | solution.py:332
  103.0 40.5 %collective-permute-start = (bf16[128,2560]{1,0:T(8,128)(2,1)S(1)}, bf16[128,2560]{1,0:T(8,128)(2,1)}, u32[]{:S(2)}, u32[]{:S(2)}) collective-permute-start(bf16[128,2560]{1,0:T(8,128)(2,1)S(1)} %pad_maximum_fusion.refs_4_.refs_5_), channel_id=1, source_target_pairs={{0,128},{64,192},{128,0},{192,64},{1,129},{65,193},{129,1},{193,65... | collective-permute-start | bytes 1966088 | tf_op jit(solution)/shard_map/ppermute | solution.py:332
  106.8 38.1 %collective-permute-start.1 = (bf16[128,2560]{1,0:T(8,128)(2,1)S(1)}, bf16[128,2560]{1,0:T(8,128)(2,1)}, u32[]{:S(2)}, u32[]{:S(2)}) collective-permute-start(bf16[128,2560]{1,0:T(8,128)(2,1)S(1)} %pad_maximum_fusion.refs_4_.refs_5_), channel_id=1, source_target_pairs={{0,64},{64,128},{128,192},{192,0},{1,65},{65,129},{129,193},{193,1... | collective-permute-start | bytes 1966088 | tf_op jit(solution)/shard_map/ppermute | solution.py:332
  109.3 37.8 %collective-permute-start.2 = (bf16[128,2560]{1,0:T(8,128)(2,1)S(1)}, bf16[128,2560]{1,0:T(8,128)(2,1)}, u32[]{:S(2)}, u32[]{:S(2)}) collective-permute-start(bf16[128,2560]{1,0:T(8,128)(2,1)S(1)} %pad_maximum_fusion.refs_4_.refs_5_), channel_id=1, source_target_pairs={{0,192},{64,0},{128,64},{192,128},{1,193},{65,1},{129,65},{193,129... | collective-permute-start | bytes 1966088 | tf_op jit(solution)/shard_map/ppermute | solution.py:332
  129.7 13.2 %copy-start.1 = (bf16[128,2560]{1,0:T(8,128)(2,1)}, bf16[128,2560]{1,0:T(8,128)(2,1)S(1)}, u32[]{:S(2)}) copy-start(bf16[128,2560]{1,0:T(8,128)(2,1)S(1)} %collective-permute-done.4.refs_9_.refs_10_) | copy-start | bytes 1966084
  130.5 19.9 %collective-permute-start.6 = (bf16[64,2560]{1,0:T(8,128)(2,1)}, bf16[64,2560]{1,0:T(8,128)(2,1)S(1)}, u32[]{:S(2)}, u32[]{:S(2)}) collective-permute-start(bf16[64,2560]{1,0:T(8,128)(2,1)} %slice.17), channel_id=1, source_target_pairs={{0,64},{64,128},{128,192},{192,0},{1,65},{65,129},{129,193},{193,1... | collective-permute-start | bytes 983048 | tf_op jit(solution)/shard_map/ppermute | solution.py:332
  132.4 0.8 copy-start.2
  134.0 18.4 %collective-permute-start.7 = (bf16[64,2560]{1,0:T(8,128)(2,1)}, bf16[64,2560]{1,0:T(8,128)(2,1)}, u32[]{:S(2)}, u32[]{:S(2)}) collective-permute-start(bf16[64,2560]{1,0:T(8,128)(2,1)} %slice.18), channel_id=1, source_target_pairs={{0,192},{64,0},{128,64},{192,128},{1,193},{65,1},{129,65},{193,129... | collective-permute-start | bytes 983048 | tf_op jit(solution)/shard_map/ppermute | solution.py:332
  150.3 2.1 copy-start.4
  159.7 54.3 %all-to-all-start.1 = ((bf16[64,56,128]{2,1,0:T(8,128)(2,1)}), bf16[64,56,128]{2,1,0:T(8,128)(2,1)S(1)}, u32[]{:S(2)}, u32[]{:S(2)}) async-start(bf16[64,56,128]{2,1,0:T(8,128)(2,1)} %bitcast.30), calls=%async_computation.1 | async-start | bytes 1835008 | tf_op jit(solution)/shard_map/all_to_all | solution.py:337
  175.2 11.7 %collective-permute-start.10 = (bf16[2,3,32,768]{3,2,1,0:T(8,128)(2,1)}, bf16[2,3,32,768]{3,2,1,0:T(8,128)(2,1)S(1)}, u32[]{:S(2)}, u32[]{:S(2)}) collective-permute-start(bf16[2,3,32,768]{3,2,1,0:T(8,128)(2,1)} %get-tuple-element.25), channel_id=1, source_target_pairs={{0,192},{64,0},{128,64},{192,128},{1,193},{65,1},{129,65},{193,129... | collective-permute-start | bytes 884744 | tf_op jit(solution)/shard_map/ppermute | solution.py:332
  180.0 18.4 %collective-permute-start.9 = (bf16[2,3,32,768]{3,2,1,0:T(8,128)(2,1)}, bf16[2,3,32,768]{3,2,1,0:T(8,128)(2,1)S(1)}, u32[]{:S(2)}, u32[]{:S(2)}) collective-permute-start(bf16[2,3,32,768]{3,2,1,0:T(8,128)(2,1)} %get-tuple-element.24), channel_id=1, source_target_pairs={{0,64},{64,128},{128,192},{192,0},{1,65},{65,129},{129,193},{193,1... | collective-permute-start | bytes 884744 | tf_op jit(solution)/shard_map/ppermute | solution.py:332
  182.0 16.5 %collective-permute-start.8 = (bf16[2,3,32,768]{3,2,1,0:T(8,128)(2,1)}, bf16[2,3,32,768]{3,2,1,0:T(8,128)(2,1)S(1)}, u32[]{:S(2)}, u32[]{:S(2)}) collective-permute-start(bf16[2,3,32,768]{3,2,1,0:T(8,128)(2,1)} %get-tuple-element.23), channel_id=1, source_target_pairs={{0,128},{64,192},{128,0},{192,64},{1,129},{65,193},{129,1},{193,65... | collective-permute-start | bytes 884744 | tf_op jit(solution)/shard_map/ppermute | solution.py:332
  199.6 13.7 %collective-permute-start.11 = (bf16[3,32,768]{2,1,0:T(8,128)(2,1)S(1)}, bf16[3,32,768]{2,1,0:T(8,128)(2,1)S(1)}, u32[]{:S(2)}, u32[]{:S(2)}) collective-permute-start(bf16[3,32,768]{2,1,0:T(8,128)(2,1)S(1)} %fusion.2), channel_id=1, source_target_pairs={{0,256},{256,0},{1,257},{257,1},{2,258},{258,2},{3,259},{259,3},{4... | collective-permute-start | bytes 442376 | tf_op jit(solution)/shard_map/ppermute | solution.py:327

commit v6 on v4

--- a/solution.py
+++ b/solution.py
@@ -141,18 +141,19 @@
         ].astype(BF16)
 
 
-def grads_kernel(places, *refs):
+def core_kernel(places, *refs):
     n = len(places)
-    where_ref, got_ref, act_hbm, slope_hbm = refs[:4]
-    pieces = refs[4 : 4 + n]
-    row_hbm, both_hbm, proj_hbm = refs[4 + n : 7 + n]
-    wide, x_rows, dy_rows, rows_wide, w1, w2, act, slope, row, both, proj, sems = refs[7 + n :]
+    where_ref, got_ref, act_hbm, slope_hbm, hid_hbm = refs[:5]
+    pieces = refs[5 : 5 + n]
+    row_hbm, part_refs = refs[5 + n], refs[6 + n : 10 + n]
+    wide, x_rows, dy_rows, rows_wide, w1, w2, act, slope, hid, row, both, term, sems = refs[10 + n :]
     hidden = act.shape[1]
     slots, width = dy_rows.shape
     n_chunk = width // LANES
     first = fetch(where_ref, pieces, places, pl.ds(0, w1.shape[1]), w1, sems, 0)
     middle = fetch_all((slope_hbm, act_hbm), (slope, act), sems, 2 * n)
     last = fetch(where_ref, pieces, places, pl.ds(w1.shape[1], w2.shape[1]), w2, sems, n)
+    last += fetch_all((hid_hbm,), (hid,), sems, 2 * n + 2)
     wide[...] = got_ref[...].astype(F32)
     spread(wide, n_chunk, 2 * n_chunk, dy_rows)
     spread(wide, 0, 2 * n_chunk, x_rows)
@@ -163,9 +164,6 @@
         copy.wait()
     both[:, :hidden] = (grad * slope[...]).astype(BF16)
     both[:, hidden:] = (grad * act[...]).astype(BF16)
-    proj[0] = jnp.dot(x_rows[...], w1[:, hidden:], preferred_element_type=F32).astype(BF16)
-    proj[1] = jnp.dot(dy_rows[...], w1[:, hidden:], preferred_element_type=F32).astype(BF16)
-    sent = fetch_all((both, proj), (both_hbm, proj_hbm), sems, 2 * n + 2)
     for copy in last:
         copy.wait()
     for c in range(0, n_chunk, 2):
@@ -177,28 +175,40 @@
         )
         rows_wide[chunk_rows(c, slots, n_chunk), :] = rows[:, :LANES]
         rows_wide[chunk_rows(c + 1, slots, n_chunk), :] = rows[:, LANES:]
-    size = row.shape[0] // 2
-    for i in range(2):
-        here = slice(i * size, (i + 1) * size)
-        row[here, :] = rows_wide[here, :].astype(BF16)
-        sent += fetch_all((row.at[here, :],), (row_hbm.at[here, :],), sems, 2 * n + 4 + i)
+    row[...] = rows_wide[...].astype(BF16)
+    sent = fetch_all((row,), (row_hbm,), sems, 2 * n + 3)
+    x_proj = jnp.dot(x_rows[...], w1[:, hidden:], preferred_element_type=F32).astype(BF16)
+    dy_proj = jnp.dot(dy_rows[...], w1[:, hidden:], preferred_element_type=F32).astype(BF16)
+    by_rows = (((0,), (0,)), ((), ()))
+    for t, (left, right) in enumerate(
+        ((x_proj, both[:, :hidden]), (x_proj, both[:, hidden:]), (dy_proj, hid[...]))
+    ):
+        term[t] = lax.dot_general(left, right, by_rows, preferred_element_type=F32).astype(BF16)
+    high, low = where_ref[0], where_ref[1]
+    part = part_refs[0].shape[2]
+    for k, out in enumerate(part_refs):
+        column = jnp.bitwise_and(low + k, 3)
+        for h in range(2):
+            begin = (jnp.bitwise_and(high + h, 1) * 4 + column) * part
+            rows = term.at[:, pl.ds(pl.multiple_of(begin, part), part), :]
+            sent += fetch_all((rows,), (out.at[h],), sems, 2 * n + 4 + 2 * k + h)
     for copy in sent:
         copy.wait()
 
 
-def grads(where, got, act, slope, pieces, places, rank):
+def core(where, got, act, slope, hid, pieces, places, rank, n_dp):
     slots, hidden = act.shape
     width = got.shape[0] * LANES // slots // 2
     rows = slots * width // LANES
+    part = rank // n_dp
     n = len(pieces)
     return pl.pallas_call(
-        functools.partial(grads_kernel, places),
-        in_specs=[pl.BlockSpec(memory_space=pltpu.SMEM), in_vmem()] + [in_place()] * (2 + n),
-        out_specs=(in_place(),) * 3,
+        functools.partial(core_kernel, places),
+        in_specs=[pl.BlockSpec(memory_space=pltpu.SMEM), in_vmem()] + [in_place()] * (3 + n),
+        out_specs=(in_place(),) * 5,
         out_shape=(
             jax.ShapeDtypeStruct((rows, LANES), BF16),
-            jax.ShapeDtypeStruct((slots, 2 * hidden), BF16),
-            jax.ShapeDtypeStruct((2, slots, rank), BF16),
+            *(jax.ShapeDtypeStruct((2, 3, part, hidden), BF16) for _ in range(4)),
         ),
         scratch_shapes=[
             pltpu.VMEM(got.shape, F32),
@@ -209,61 +219,14 @@
             pltpu.VMEM((width, 2 * hidden), BF16),
             pltpu.VMEM((slots, hidden), F32),
             pltpu.VMEM((slots, hidden), F32),
+            pltpu.VMEM((slots, hidden), BF16),
             pltpu.VMEM((rows, LANES), BF16),
             pltpu.VMEM((slots, 2 * hidden), BF16),
-            pltpu.VMEM((2, slots, rank), BF16),
-            pltpu.SemaphoreType.DMA((2 * n + 6,)),
+            pltpu.VMEM((3, rank, hidden), BF16),
+            pltpu.SemaphoreType.DMA((2 * n + 12,)),
         ],
-        name="grads",
-    )(where, near(got), act, slope, *pieces)
-
-
-def terms_kernel(where_ref, both_hbm, proj_hbm, hid_hbm, *refs):
-    part_refs = refs[:4]
-    both, proj, hid, term_ref, sems = refs[4:]
-    hidden = hid.shape[1]
-    proj_in, both_in, hid_in = fetch_all(
-        (proj_hbm, both_hbm, hid_hbm), (proj, both, hid), sems, 0
-    )
-    by_rows = (((0,), (0,)), ((), ()))
-    proj_in.wait()
-    both_in.wait()
-    x_proj = proj[0]
-    term_ref[0] = lax.dot_general(x_proj, both[:, :hidden], by_rows, preferred_element_type=F32)
-    term_ref[1] = lax.dot_general(x_proj, both[:, hidden:], by_rows, preferred_element_type=F32)
-    hid_in.wait()
-    term_ref[2] = lax.dot_general(proj[1], hid[...], by_rows, preferred_element_type=F32)
-    high, low = where_ref[0], where_ref[1]
-    n_term, part = term_ref.shape[0], part_refs[0].shape[2]
-    for k, out in enumerate(part_refs):
-        column = jnp.bitwise_and(low + k, 3)
-        for h in range(2):
-            begin = (jnp.bitwise_and(high + h, 1) * 4 + column) * part
-            for t in range(n_term):
-                out[h, t] = term_ref[t, pl.ds(pl.multiple_of(begin, part), part), :].astype(
-                    out.dtype
-                )
-
-
-def terms(where, both, proj, hid, n_dp):
-    _, hidden = hid.shape
-    rank = proj.shape[2]
-    part = rank // n_dp
-    return pl.pallas_call(
-        terms_kernel,
-        in_specs=[pl.BlockSpec(memory_space=pltpu.SMEM)] + [in_place()] * 3,
-        out_shape=tuple(
-            jax.ShapeDtypeStruct((2, 3, part, hidden), F32 if k == 0 else BF16) for k in range(4)
-        ),
-        scratch_shapes=[
-            pltpu.VMEM(both.shape, BF16),
-            pltpu.VMEM(proj.shape, BF16),
-            pltpu.VMEM(hid.shape, BF16),
-            pltpu.VMEM((3, rank, hidden), F32),
-            pltpu.SemaphoreType.DMA((3,)),
-        ],
-        name="terms",
-    )(where, both, proj, hid)
+        name="core",
+    )(where, near(got), act, slope, hid, *pieces)
 
 
 def take_pair(wide_ref, first, second, slots, step):
@@ -338,10 +301,9 @@
     rank = basis.shape[2]
     act, slope, hid = slopes(saved_pre[0, 0])
     places = tuple(places)
-    row_grad, both, proj = grads(where, got, act, slope, pieces, places, rank)
+    row_grad, *parts = core(where, got, act, slope, hid, pieces, places, rank, 8)
     back = exchange(row_grad, n_owner)
-    parts = terms(where, both, proj, hid, 8)
-    summed = parts[0]
+    summed = parts[0].astype(F32)
     for k in (2, 1, 3):
         summed = summed + shifted(parts[k], k).astype(F32)
     other = swap(summed[1].astype(BF16))

time: 180 us -> 175 us (0.972)
  Pallas kernels: 21.6 us -> 18.4 us
    pallas_call x2 -> x1, Pallas kernels: 11.9 us -> 8.67 us  [core(): pl.pallas_call(functools.partial(core_kernel, places), in_specs=[pl.Block...]
  transfers between devices with their start and end apart: 15 -> 15, of which waited for: 7 -> 7; matrix products, arithmetic and copies ran while one was open for 3% -> 2% of each run, Pallas kernels for 5% -> 2%
where the time goes in v6:
time: 175 us; the launch traced here: 174 us
  starting transfers between devices  90.4 us (52%)
  waiting for transfers between devices  60.7 us (35%)
  Pallas kernels  18.4 us (11%)
  local copies, waits for them, and re-layouts  2.51 us (1%)
    all_to_all x2, starting transfers between devices, exchange(): lax.all_to_all(value.reshape(n_owner, rows // n_owner, lanes), 'expert',...  46.5 us
    ppermute x2, waiting for transfers between devices, swap(): return lax.ppermute(value, 'dp_0', [(0, 1), (1, 0)])  41.8 us
    ppermute x11, starting transfers between devices, shifted(): lax.ppermute(value, 'dp_1', [(i, (i + k) % size) for i in range(size)])  34.7 us
    ppermute x11, waiting for transfers between devices, shifted(): lax.ppermute(value, 'dp_1', [(i, (i + k) % size) for i in range(size)])  18.9 us
    ppermute x2, starting transfers between devices, swap(): return lax.ppermute(value, 'dp_0', [(0, 1), (1, 0)])  9.2 us
    pallas_call x1, Pallas kernels, core(): pl.pallas_call(functools.partial(core_kernel, places), in_specs=[pl.Block...  8.67 us
    pallas_call x1, Pallas kernels, pack(): pl.pallas_call(functools.partial(pack_kernel, cap), out_shape=(jax.ShapeD...  3.95 us
    pallas_call x1, Pallas kernels, slopes(): pl.pallas_call(slopes_kernel, out_shape=(jax.ShapeDtypeStruct((slots, hid...  3.59 us
  transfers between devices with their start and end apart: 15, of which 7 were waited for; matrix products, arithmetic and copies ran while one was open for 2% of the time, Pallas kernels for 2%

profile of v6, /device:TPU:17, one launch (start us, length us, event | category | flops | bytes accessed | tf_op | source)
XLA Modules:
  0.0 174.5 jit_solution(13277008428881148233)
XLA Ops:
  0.6 4.0 %pack.1 = (bf16[7168,128]{1,0:T(8,128)(2,1)}, bf16[448,128]{1,0:T(8,128)(2,1)}) custom-call(s32[3,128]{1,0:T(4,128)} %bitcast.32, f32[3,128]{1,0:T(4,128)} %bitcast.33, bf16[128,1024]{1,0:T(8,128)(2,1)} %tok_ref.1, bf16[128,1024]{1,0:T(8,128)(2,1)} %grad_ref.1), custom_call_target="tpu_custom_call" | custom-call | tf_op jit(solution)/shard_map/pack/pallas_call | solution.py:67
  4.6 14.7 %all-to-all-start = ((bf16[64,112,128]{2,1,0:T(8,128)(2,1)}), bf16[64,112,128]{2,1,0:T(8,128)(2,1)S(1)}, u32[]{:S(2)}, u32[]{:S(2)}) async-start(bf16[64,112,128]{2,1,0:T(8,128)(2,1)} %bitcast.25), calls=%async_computation | async-start | bytes 3670016 | tf_op jit(solution)/shard_map/all_to_all | solution.py:275
  19.4 4.8 %collective-permute-start.4 = (bf16[128,2560]{1,0:T(8,128)(2,1)S(1)}, bf16[128,2560]{1,0:T(8,128)(2,1)S(1)}, u32[]{:S(2)}, u32[]{:S(2)}) collective-permute-start(bf16[128,2560]{1,0:T(8,128)(2,1)S(1)} %pad_maximum_fusion.refs_5_), channel_id=1, source_target_pairs={{0,256},{256,0},{1,257},{257,1},{2,258},{258,2},{3,259},{259,3},{4... | collective-permute-start | bytes 1966088 | tf_op jit(solution)/shard_map/ppermute | solution.py:265
  24.2 4.4 %collective-permute-start.1 = (bf16[128,2560]{1,0:T(8,128)(2,1)S(1)}, bf16[128,2560]{1,0:T(8,128)(2,1)S(1)}, u32[]{:S(2)}, u32[]{:S(2)}) collective-permute-start(bf16[128,2560]{1,0:T(8,128)(2,1)S(1)} %pad_maximum_fusion.refs_5_), channel_id=1, source_target_pairs={{0,192},{64,0},{128,64},{192,128},{1,193},{65,1},{129,65},{193,129... | collective-permute-start | bytes 1966088 | tf_op jit(solution)/shard_map/ppermute | solution.py:270
  28.5 1.9 %collective-permute-start = (bf16[128,2560]{1,0:T(8,128)(2,1)S(1)}, bf16[128,2560]{1,0:T(8,128)(2,1)S(1)}, u32[]{:S(2)}, u32[]{:S(2)}) collective-permute-start(bf16[128,2560]{1,0:T(8,128)(2,1)S(1)} %pad_maximum_fusion.refs_5_), channel_id=1, source_target_pairs={{0,64},{64,128},{128,192},{192,0},{1,65},{65,129},{129,193},{193,1... | collective-permute-start | bytes 1966088 | tf_op jit(solution)/shard_map/ppermute | solution.py:270
  30.5 31.6 %collective-permute-done.4.refs_10_ = bf16[128,2560]{1,0:T(8,128)(2,1)S(1)} collective-permute-done((bf16[128,2560]{1,0:T(8,128)(2,1)S(1)}, bf16[128,2560]{1,0:T(8,128)(2,1)S(1)}, u32[]{:S(2)}, u32[]{:S(2)}) %collective-permute-start.4) | collective-permute-done | bytes 655392 | tf_op jit(solution)/shard_map/ppermute | solution.py:265
  62.1 4.4 %collective-permute-start.6 = (bf16[128,2560]{1,0:T(8,128)(2,1)S(1)}, bf16[128,2560]{1,0:T(8,128)(2,1)S(1)}, u32[]{:S(2)}, u32[]{:S(2)}) collective-permute-start(bf16[128,2560]{1,0:T(8,128)(2,1)S(1)} %collective-permute-done.4.refs_10_), channel_id=1, source_target_pairs={{0,192},{64,0},{128,64},{192,128},{1,193},{65,1},{129,65},{193,129... | collective-permute-start | bytes 1966088 | tf_op jit(solution)/shard_map/ppermute | solution.py:270
  66.5 1.9 %collective-permute-start.5 = (bf16[128,2560]{1,0:T(8,128)(2,1)S(1)}, bf16[128,2560]{1,0:T(8,128)(2,1)S(1)}, u32[]{:S(2)}, u32[]{:S(2)}) collective-permute-start(bf16[128,2560]{1,0:T(8,128)(2,1)S(1)} %collective-permute-done.4.refs_10_), channel_id=1, source_target_pairs={{0,64},{64,128},{128,192},{192,0},{1,65},{65,129},{129,193},{193,1... | collective-permute-start | bytes 1966088 | tf_op jit(solution)/shard_map/ppermute | solution.py:270
  68.5 4.6 %collective-permute-start.3 = (bf16[64,2560]{1,0:T(8,128)(2,1)S(1)}, bf16[64,2560]{1,0:T(8,128)(2,1)}, u32[]{:S(2)}, u32[]{:S(2)}) collective-permute-start(bf16[64,2560]{1,0:T(8,128)(2,1)S(1)} %slice.26), channel_id=1, source_target_pairs={{0,192},{64,0},{128,64},{192,128},{1,193},{65,1},{129,65},{193,129... | collective-permute-start | bytes 983048 | tf_op jit(solution)/shard_map/ppermute | solution.py:270
  75.8 4.1 %collective-permute-done.6.refs_12_ = bf16[128,2560]{1,0:T(8,128)(2,1)S(1)} collective-permute-done((bf16[128,2560]{1,0:T(8,128)(2,1)S(1)}, bf16[128,2560]{1,0:T(8,128)(2,1)S(1)}, u32[]{:S(2)}, u32[]{:S(2)}) %collective-permute-start.6) | collective-permute-done | bytes 655392 | tf_op jit(solution)/shard_map/ppermute | solution.py:270
  80.7 5.3 %collective-permute-start.8 = (bf16[64,2560]{1,0:T(8,128)(2,1)}, bf16[64,2560]{1,0:T(8,128)(2,1)}, u32[]{:S(2)}, u32[]{:S(2)}) collective-permute-start(bf16[64,2560]{1,0:T(8,128)(2,1)} %slice.28), channel_id=1, source_target_pairs={{0,192},{64,0},{128,64},{192,128},{1,193},{65,1},{129,65},{193,129... | collective-permute-start | bytes 983048 | tf_op jit(solution)/shard_map/ppermute | solution.py:270
  86.8 1.9 %collective-permute-start.7 = (bf16[64,2560]{1,0:T(8,128)(2,1)}, bf16[64,2560]{1,0:T(8,128)(2,1)}, u32[]{:S(2)}, u32[]{:S(2)}) collective-permute-start(bf16[64,2560]{1,0:T(8,128)(2,1)} %slice.27), channel_id=1, source_target_pairs={{0,64},{64,128},{128,192},{192,0},{1,65},{65,129},{129,193},{193,1... | collective-permute-start | bytes 983048 | tf_op jit(solution)/shard_map/ppermute | solution.py:270
  88.8 3.6 %slopes.1 = (f32[448,768]{1,0:T(8,128)}, f32[448,768]{1,0:T(8,128)}, bf16[448,768]{1,0:T(8,128)(2,1)}) custom-call(bf16[448,1536]{1,0:T(8,128)(2,1)} %bitcast.26), custom_call_target="tpu_custom_call" | custom-call | tf_op jit(solution)/shard_map/slopes/pallas_call | solution.py:125
  93.8 3.9 %collective-permute-done.7.refs_13_ = bf16[64,2560]{1,0:T(8,128)(2,1)} collective-permute-done((bf16[64,2560]{1,0:T(8,128)(2,1)}, bf16[64,2560]{1,0:T(8,128)(2,1)}, u32[]{:S(2)}, u32[]{:S(2)}) %collective-permute-start.7) | collective-permute-done | bytes 327712 | tf_op jit(solution)/shard_map/ppermute | solution.py:270
  97.6 8.7 %core.1 = (bf16[3584,128]{1,0:T(8,128)(2,1)}, bf16[2,3,32,768]{3,2,1,0:T(8,128)(2,1)}, bf16[2,3,32,768]{3,2,1,0:T(8,128)(2,1)}, bf16[2,3,32,768]{3,2,1,0:T(8,128)(2,1)}, bf16[2,3,32,768]{3,2,1,0:T(8,128)(2,1)}) custom-call(s32[2]{0:T(128)} %pad_add_fusion.refs_0_, bf16[7168,128]{1,0:T(8,128)(2,1)S(1)} %bitcast.23, f32[448,768]{1,0:T(8,128)} %get-tuple-element.14.refs_2_, ...), custom_call_target="tpu_custom_call" | custom-call | tf_op jit(solution)/shard_map/core/pallas_call | solution.py:205
  106.4 31.8 %all-to-all-start.1 = ((bf16[64,56,128]{2,1,0:T(8,128)(2,1)}), bf16[64,56,128]{2,1,0:T(8,128)(2,1)S(1)}, u32[]{:S(2)}, u32[]{:S(2)}) async-start(bf16[64,56,128]{2,1,0:T(8,128)(2,1)} %bitcast.27), calls=%async_computation.1 | async-start | bytes 1835008 | tf_op jit(solution)/shard_map/all_to_all | solution.py:275
  138.2 1.9 %collective-permute-start.9 = (bf16[2,3,32,768]{3,2,1,0:T(8,128)(2,1)S(1)}, bf16[2,3,32,768]{3,2,1,0:T(8,128)(2,1)S(1)}, u32[]{:S(2)}, u32[]{:S(2)}) collective-permute-start(bf16[2,3,32,768]{3,2,1,0:T(8,128)(2,1)S(1)} %copy-done.13), channel_id=1, source_target_pairs={{0,128},{64,192},{128,0},{192,64},{1,129},{65,193},{129,1},{193,65... | collective-permute-start | bytes 884744 | tf_op jit(solution)/shard_map/ppermute | solution.py:270
  140.1 1.9 %collective-permute-start.10 = (bf16[2,3,32,768]{3,2,1,0:T(8,128)(2,1)S(1)}, bf16[2,3,32,768]{3,2,1,0:T(8,128)(2,1)S(1)}, u32[]{:S(2)}, u32[]{:S(2)}) collective-permute-start(bf16[2,3,32,768]{3,2,1,0:T(8,128)(2,1)S(1)} %copy-done.12), channel_id=1, source_target_pairs={{0,64},{64,128},{128,192},{192,0},{1,65},{65,129},{129,193},{193,1... | collective-permute-start | bytes 884744 | tf_op jit(solution)/shard_map/ppermute | solution.py:270
  142.0 4.6 %collective-permute-start.11 = (bf16[2,3,32,768]{3,2,1,0:T(8,128)(2,1)S(1)}, bf16[2,3,32,768]{3,2,1,0:T(8,128)(2,1)S(1)}, u32[]{:S(2)}, u32[]{:S(2)}) collective-permute-start(bf16[2,3,32,768]{3,2,1,0:T(8,128)(2,1)S(1)} %copy-done.11), channel_id=1, source_target_pairs={{0,192},{64,0},{128,64},{192,128},{1,193},{65,1},{129,65},{193,129... | collective-permute-start | bytes 884744 | tf_op jit(solution)/shard_map/ppermute | solution.py:270
  146.6 3.2 %collective-permute-done.9 = bf16[2,3,32,768]{3,2,1,0:T(8,128)(2,1)S(1)} collective-permute-done((bf16[2,3,32,768]{3,2,1,0:T(8,128)(2,1)S(1)}, bf16[2,3,32,768]{3,2,1,0:T(8,128)(2,1)S(1)}, u32[]{:S(2)}, u32[]{:S(2)}) %collective-permute-start.9) | collective-permute-done | bytes 294944 | tf_op jit(solution)/shard_map/ppermute | solution.py:270
  149.8 7.0 %collective-permute-done.10 = bf16[2,3,32,768]{3,2,1,0:T(8,128)(2,1)S(1)} collective-permute-done((bf16[2,3,32,768]{3,2,1,0:T(8,128)(2,1)S(1)}, bf16[2,3,32,768]{3,2,1,0:T(8,128)(2,1)S(1)}, u32[]{:S(2)}, u32[]{:S(2)}) %collective-permute-start.10) | collective-permute-done | bytes 294944 | tf_op jit(solution)/shard_map/ppermute | solution.py:270
  157.0 4.4 %collective-permute-start.12 = (bf16[3,32,768]{2,1,0:T(8,128)(2,1)S(1)}, bf16[3,32,768]{2,1,0:T(8,128)(2,1)S(1)}, u32[]{:S(2)}, u32[]{:S(2)}) collective-permute-start(bf16[3,32,768]{2,1,0:T(8,128)(2,1)S(1)} %fusion.2), channel_id=1, source_target_pairs={{0,256},{256,0},{1,257},{257,1},{2,258},{258,2},{3,259},{259,3},{4... | collective-permute-start | bytes 442376 | tf_op jit(solution)/shard_map/ppermute | solution.py:265
  161.5 10.1 %collective-permute-done.12 = bf16[3,32,768]{2,1,0:T(8,128)(2,1)S(1)} collective-permute-done((bf16[3,32,768]{2,1,0:T(8,128)(2,1)S(1)}, bf16[3,32,768]{2,1,0:T(8,128)(2,1)S(1)}, u32[]{:S(2)}, u32[]{:S(2)}) %collective-permute-start.12) | collective-permute-done | bytes 147488 | tf_op jit(solution)/shard_map/ppermute | solution.py:265
  172.3 2.2 %combine.1 = bf16[128,1024]{1,0:T(8,128)(2,1)} custom-call(bf16[448,128]{1,0:T(8,128)(2,1)} %get-tuple-element.12.match_ref, bf16[3584,128]{1,0:T(8,128)(2,1)S(1)} %bitcast.24), custom_call_target="tpu_custom_call" | custom-call | tf_op jit(solution)/shard_map/combine/pallas_call | solution.py:256
  (47 shorter events, 6.8 us)
Async XLA Ops:
  4.6 14.7 %copy-start.10 = (bf16[1,128,256]{2,1,0:T(8,128)(2,1)S(1)}, bf16[1,128,256]{2,1,0:T(8,128)(2,1)}, u32[]{:S(2)}) copy-start(bf16[1,128,256]{2,1,0:T(8,128)(2,1)} %param.17) | copy-start | bytes 196612
  4.6 93.0 %all-to-all-start = ((bf16[64,112,128]{2,1,0:T(8,128)(2,1)}), bf16[64,112,128]{2,1,0:T(8,128)(2,1)S(1)}, u32[]{:S(2)}, u32[]{:S(2)}) async-start(bf16[64,112,128]{2,1,0:T(8,128)(2,1)} %bitcast.25), calls=%async_computation | async-start | bytes 3670016 | tf_op jit(solution)/shard_map/all_to_all | solution.py:275
  19.4 67.4 %copy-start = (bf16[128,2560]{1,0:T(8,128)(2,1)}, bf16[128,2560]{1,0:T(8,128)(2,1)S(1)}, u32[]{:S(2)}) copy-start(bf16[128,2560]{1,0:T(8,128)(2,1)S(1)} %pad_maximum_fusion.refs_5_) | copy-start | bytes 1966084
  19.4 42.7 %collective-permute-start.4 = (bf16[128,2560]{1,0:T(8,128)(2,1)S(1)}, bf16[128,2560]{1,0:T(8,128)(2,1)S(1)}, u32[]{:S(2)}, u32[]{:S(2)}) collective-permute-start(bf16[128,2560]{1,0:T(8,128)(2,1)S(1)} %pad_maximum_fusion.refs_5_), channel_id=1, source_target_pairs={{0,256},{256,0},{1,257},{257,1},{2,258},{258,2},{3,259},{259,3},{4... | collective-permute-start | bytes 1966088 | tf_op jit(solution)/shard_map/ppermute | solution.py:265
  24.2 44.3 %collective-permute-start.1 = (bf16[128,2560]{1,0:T(8,128)(2,1)S(1)}, bf16[128,2560]{1,0:T(8,128)(2,1)S(1)}, u32[]{:S(2)}, u32[]{:S(2)}) collective-permute-start(bf16[128,2560]{1,0:T(8,128)(2,1)S(1)} %pad_maximum_fusion.refs_5_), channel_id=1, source_target_pairs={{0,192},{64,0},{128,64},{192,128},{1,193},{65,1},{129,65},{193,129... | collective-permute-start | bytes 1966088 | tf_op jit(solution)/shard_map/ppermute | solution.py:270
  28.5 44.5 %collective-permute-start = (bf16[128,2560]{1,0:T(8,128)(2,1)S(1)}, bf16[128,2560]{1,0:T(8,128)(2,1)S(1)}, u32[]{:S(2)}, u32[]{:S(2)}) collective-permute-start(bf16[128,2560]{1,0:T(8,128)(2,1)S(1)} %pad_maximum_fusion.refs_5_), channel_id=1, source_target_pairs={{0,64},{64,128},{128,192},{192,0},{1,65},{65,129},{129,193},{193,1... | collective-permute-start | bytes 1966088 | tf_op jit(solution)/shard_map/ppermute | solution.py:270
  62.1 35.5 %copy-start.5 = (bf16[128,2560]{1,0:T(8,128)(2,1)}, bf16[128,2560]{1,0:T(8,128)(2,1)S(1)}, u32[]{:S(2)}) copy-start(bf16[128,2560]{1,0:T(8,128)(2,1)S(1)} %collective-permute-done.4.refs_10_) | copy-start | bytes 1966084
  62.1 17.8 %collective-permute-start.6 = (bf16[128,2560]{1,0:T(8,128)(2,1)S(1)}, bf16[128,2560]{1,0:T(8,128)(2,1)S(1)}, u32[]{:S(2)}, u32[]{:S(2)}) collective-permute-start(bf16[128,2560]{1,0:T(8,128)(2,1)S(1)} %collective-permute-done.4.refs_10_), channel_id=1, source_target_pairs={{0,192},{64,0},{128,64},{192,128},{1,193},{65,1},{129,65},{193,129... | collective-permute-start | bytes 1966088 | tf_op jit(solution)/shard_map/ppermute | solution.py:270
  66.5 19.5 %collective-permute-start.5 = (bf16[128,2560]{1,0:T(8,128)(2,1)S(1)}, bf16[128,2560]{1,0:T(8,128)(2,1)S(1)}, u32[]{:S(2)}, u32[]{:S(2)}) collective-permute-start(bf16[128,2560]{1,0:T(8,128)(2,1)S(1)} %collective-permute-done.4.refs_10_), channel_id=1, source_target_pairs={{0,64},{64,128},{128,192},{192,0},{1,65},{65,129},{129,193},{193,1... | collective-permute-start | bytes 1966088 | tf_op jit(solution)/shard_map/ppermute | solution.py:270
  68.4 18.4 %copy-start.1 = (bf16[128,2560]{1,0:T(8,128)(2,1)}, bf16[128,2560]{1,0:T(8,128)(2,1)S(1)}, u32[]{:S(2)}) copy-start(bf16[128,2560]{1,0:T(8,128)(2,1)S(1)} %collective-permute-done.1.refs_7_) | copy-start | bytes 1966084
  68.5 24.5 %collective-permute-start.3 = (bf16[64,2560]{1,0:T(8,128)(2,1)S(1)}, bf16[64,2560]{1,0:T(8,128)(2,1)}, u32[]{:S(2)}, u32[]{:S(2)}) collective-permute-start(bf16[64,2560]{1,0:T(8,128)(2,1)S(1)} %slice.26), channel_id=1, source_target_pairs={{0,192},{64,0},{128,64},{192,128},{1,193},{65,1},{129,65},{193,129... | collective-permute-start | bytes 983048 | tf_op jit(solution)/shard_map/ppermute | solution.py:270
  73.1 19.3 %copy-start.2 = (bf16[128,2560]{1,0:T(8,128)(2,1)}, bf16[128,2560]{1,0:T(8,128)(2,1)S(1)}, u32[]{:S(2)}) copy-start(bf16[128,2560]{1,0:T(8,128)(2,1)S(1)} %collective-permute-done.refs_6_) | copy-start | bytes 1966084
  73.9 19.1 %collective-permute-start.2 = (bf16[64,2560]{1,0:T(8,128)(2,1)}, bf16[64,2560]{1,0:T(8,128)(2,1)}, u32[]{:S(2)}, u32[]{:S(2)}) collective-permute-start(bf16[64,2560]{1,0:T(8,128)(2,1)} %slice.25), channel_id=1, source_target_pairs={{0,64},{64,128},{128,192},{192,0},{1,65},{65,129},{129,193},{193,1... | collective-permute-start | bytes 983048 | tf_op jit(solution)/shard_map/ppermute | solution.py:270
  80.7 13.1 %collective-permute-start.8 = (bf16[64,2560]{1,0:T(8,128)(2,1)}, bf16[64,2560]{1,0:T(8,128)(2,1)}, u32[]{:S(2)}, u32[]{:S(2)}) collective-permute-start(bf16[64,2560]{1,0:T(8,128)(2,1)} %slice.28), channel_id=1, source_target_pairs={{0,192},{64,0},{128,64},{192,128},{1,193},{65,1},{129,65},{193,129... | collective-permute-start | bytes 983048 | tf_op jit(solution)/shard_map/ppermute | solution.py:270
  86.8 10.8 %collective-permute-start.7 = (bf16[64,2560]{1,0:T(8,128)(2,1)}, bf16[64,2560]{1,0:T(8,128)(2,1)}, u32[]{:S(2)}, u32[]{:S(2)}) collective-permute-start(bf16[64,2560]{1,0:T(8,128)(2,1)} %slice.27), channel_id=1, source_target_pairs={{0,64},{64,128},{128,192},{192,0},{1,65},{65,129},{129,193},{193,1... | collective-permute-start | bytes 983048 | tf_op jit(solution)/shard_map/ppermute | solution.py:270
  106.3 31.8 %copy-start.13 = (bf16[2,3,32,768]{3,2,1,0:T(8,128)(2,1)S(1)}, bf16[2,3,32,768]{3,2,1,0:T(8,128)(2,1)}, u32[]{:S(2)}) copy-start(bf16[2,3,32,768]{3,2,1,0:T(8,128)(2,1)} %get-tuple-element.19) | copy-start | bytes 884740
  106.3 33.8 %copy-start.12 = (bf16[2,3,32,768]{3,2,1,0:T(8,128)(2,1)S(1)}, bf16[2,3,32,768]{3,2,1,0:T(8,128)(2,1)}, u32[]{:S(2)}) copy-start(bf16[2,3,32,768]{3,2,1,0:T(8,128)(2,1)} %get-tuple-element.20) | copy-start | bytes 884740
  106.3 35.7 %copy-start.11 = (bf16[2,3,32,768]{3,2,1,0:T(8,128)(2,1)S(1)}, bf16[2,3,32,768]{3,2,1,0:T(8,128)(2,1)}, u32[]{:S(2)}) copy-start(bf16[2,3,32,768]{3,2,1,0:T(8,128)(2,1)} %get-tuple-element.21) | copy-start | bytes 884740
  106.3 50.5 %copy-start.6 = (bf16[2,3,32,768]{3,2,1,0:T(8,128)(2,1)S(1)}, bf16[2,3,32,768]{3,2,1,0:T(8,128)(2,1)}, u32[]{:S(2)}) copy-start(bf16[2,3,32,768]{3,2,1,0:T(8,128)(2,1)} %get-tuple-element.18) | copy-start | bytes 884740
  106.4 66.0 %all-to-all-start.1 = ((bf16[64,56,128]{2,1,0:T(8,128)(2,1)}), bf16[64,56,128]{2,1,0:T(8,128)(2,1)S(1)}, u32[]{:S(2)}, u32[]{:S(2)}) async-start(bf16[64,56,128]{2,1,0:T(8,128)(2,1)} %bitcast.27), calls=%async_computation.1 | async-start | bytes 1835008 | tf_op jit(solution)/shard_map/all_to_all | solution.py:275
  138.2 11.6 %collective-permute-start.9 = (bf16[2,3,32,768]{3,2,1,0:T(8,128)(2,1)S(1)}, bf16[2,3,32,768]{3,2,1,0:T(8,128)(2,1)S(1)}, u32[]{:S(2)}, u32[]{:S(2)}) collective-permute-start(bf16[2,3,32,768]{3,2,1,0:T(8,128)(2,1)S(1)} %copy-done.13), channel_id=1, source_target_pairs={{0,128},{64,192},{128,0},{192,64},{1,129},{65,193},{129,1},{193,65... | collective-permute-start | bytes 884744 | tf_op jit(solution)/shard_map/ppermute | solution.py:270
  140.1 16.7 %collective-permute-start.10 = (bf16[2,3,32,768]{3,2,1,0:T(8,128)(2,1)S(1)}, bf16[2,3,32,768]{3,2,1,0:T(8,128)(2,1)S(1)}, u32[]{:S(2)}, u32[]{:S(2)}) collective-permute-start(bf16[2,3,32,768]{3,2,1,0:T(8,128)(2,1)S(1)} %copy-done.12), channel_id=1, source_target_pairs={{0,64},{64,128},{128,192},{192,0},{1,65},{65,129},{129,193},{193,1... | collective-permute-start | bytes 884744 | tf_op jit(solution)/shard_map/ppermute | solution.py:270
  142.0 14.8 %collective-permute-start.11 = (bf16[2,3,32,768]{3,2,1,0:T(8,128)(2,1)S(1)}, bf16[2,3,32,768]{3,2,1,0:T(8,128)(2,1)S(1)}, u32[]{:S(2)}, u32[]{:S(2)}) collective-permute-start(bf16[2,3,32,768]{3,2,1,0:T(8,128)(2,1)S(1)} %copy-done.11), channel_id=1, source_target_pairs={{0,192},{64,0},{128,64},{192,128},{1,193},{65,1},{129,65},{193,129... | collective-permute-start | bytes 884744 | tf_op jit(solution)/shard_map/ppermute | solution.py:270
  157.0 14.6 %collective-permute-start.12 = (bf16[3,32,768]{2,1,0:T(8,128)(2,1)S(1)}, bf16[3,32,768]{2,1,0:T(8,128)(2,1)S(1)}, u32[]{:S(2)}, u32[]{:S(2)}) collective-permute-start(bf16[3,32,768]{2,1,0:T(8,128)(2,1)S(1)} %fusion.2), channel_id=1, source_target_pairs={{0,256},{256,0},{1,257},{257,1},{2,258},{258,2},{3,259},{259,3},{4... | collective-permute-start | bytes 442376 | tf_op jit(solution)/shard_map/ppermute | solution.py:265
  (5 other events, 55.7 us)

commit v7 on v6

--- a/solution.py
+++ b/solution.py
@@ -133,38 +133,54 @@
     )(pre)
 
 
-def spread(wide_ref, first, step, into):
-    slots, width = into.shape
-    for c in range(width // LANES):
-        into[:, c * LANES : (c + 1) * LANES] = wide_ref[
-            chunk_rows(first + c, slots, step), :
-        ].astype(BF16)
-
-
 def core_kernel(places, *refs):
     n = len(places)
     where_ref, got_ref, act_hbm, slope_hbm, hid_hbm = refs[:5]
     pieces = refs[5 : 5 + n]
     row_hbm, part_refs = refs[5 + n], refs[6 + n : 10 + n]
-    wide, x_rows, dy_rows, rows_wide, w1, w2, act, slope, hid, row, both, term, sems = refs[10 + n :]
+    _, x_rows, dy_rows, rows_wide, w1, w2, act, slope, hid, row, both, term, sems = refs[10 + n :]
     hidden = act.shape[1]
+    rank = w1.shape[1] - hidden
     slots, width = dy_rows.shape
     n_chunk = width // LANES
-    first = fetch(where_ref, pieces, places, pl.ds(0, w1.shape[1]), w1, sems, 0)
-    middle = fetch_all((slope_hbm, act_hbm), (slope, act), sems, 2 * n)
-    last = fetch(where_ref, pieces, places, pl.ds(w1.shape[1], w2.shape[1]), w2, sems, n)
-    last += fetch_all((hid_hbm,), (hid,), sems, 2 * n + 2)
-    wide[...] = got_ref[...].astype(F32)
-    spread(wide, n_chunk, 2 * n_chunk, dy_rows)
-    spread(wide, 0, 2 * n_chunk, x_rows)
-    for copy in first:
-        copy.wait()
+    down_in = fetch(where_ref, pieces, places, pl.ds(0, hidden), w1.at[:, pl.ds(0, hidden)], sems, 0)
+    factors_in = fetch_all((slope_hbm, act_hbm), (slope, act), sems, 3 * n)
+    tiles = got_ref[...].reshape(slots, 2 * n_chunk, LANES)
+    dy_rows[...] = tiles[:, n_chunk:, :].reshape(slots, width)
+    x_rows[...] = tiles[:, :n_chunk, :].reshape(slots, width)
+    for copy in down_in:
+        copy.wait()
+    basis_in = fetch(
+        where_ref, pieces, places, pl.ds(hidden, rank), w1.at[:, pl.ds(hidden, rank)], sems, n
+    )
+    basis_in += fetch_all((hid_hbm,), (hid,), sems, 3 * n + 2)
+    w2_in = fetch(
+        where_ref, pieces, places, pl.ds(hidden + rank, w2.shape[1]), w2, sems, 2 * n
+    )
     grad = jnp.dot(dy_rows[...], w1[:, :hidden], preferred_element_type=F32)
-    for copy in middle:
+    for copy in factors_in:
         copy.wait()
     both[:, :hidden] = (grad * slope[...]).astype(BF16)
     both[:, hidden:] = (grad * act[...]).astype(BF16)
-    for copy in last:
+    for copy in basis_in:
+        copy.wait()
+    dy_proj = jnp.dot(dy_rows[...], w1[:, hidden:], preferred_element_type=F32).astype(BF16)
+    x_proj = jnp.dot(x_rows[...], w1[:, hidden:], preferred_element_type=F32).astype(BF16)
+    by_rows = (((0,), (0,)), ((), ()))
+    for t, (left, right) in enumerate(
+        ((x_proj, both[:, :hidden]), (x_proj, both[:, hidden:]), (dy_proj, hid[...]))
+    ):
+        term[t] = lax.dot_general(left, right, by_rows, preferred_element_type=F32).astype(BF16)
+    high, low = where_ref[0], where_ref[1]
+    part = part_refs[0].shape[2]
+    sent = []
+    for k, out in enumerate(part_refs):
+        column = jnp.bitwise_and(low + k, 3)
+        for h in range(2):
+            begin = (jnp.bitwise_and(high + h, 1) * 4 + column) * part
+            rows = term.at[:, pl.ds(pl.multiple_of(begin, part), part), :]
+            sent += fetch_all((rows,), (out.at[h],), sems, 3 * n + 3 + 2 * k + h)
+    for copy in w2_in:
         copy.wait()
     for c in range(0, n_chunk, 2):
         rows = lax.dot_general(
@@ -175,23 +191,11 @@
         )
         rows_wide[chunk_rows(c, slots, n_chunk), :] = rows[:, :LANES]
         rows_wide[chunk_rows(c + 1, slots, n_chunk), :] = rows[:, LANES:]
-    row[...] = rows_wide[...].astype(BF16)
-    sent = fetch_all((row,), (row_hbm,), sems, 2 * n + 3)
-    x_proj = jnp.dot(x_rows[...], w1[:, hidden:], preferred_element_type=F32).astype(BF16)
-    dy_proj = jnp.dot(dy_rows[...], w1[:, hidden:], preferred_element_type=F32).astype(BF16)
-    by_rows = (((0,), (0,)), ((), ()))
-    for t, (left, right) in enumerate(
-        ((x_proj, both[:, :hidden]), (x_proj, both[:, hidden:]), (dy_proj, hid[...]))
-    ):
-        term[t] = lax.dot_general(left, right, by_rows, preferred_element_type=F32).astype(BF16)
-    high, low = where_ref[0], where_ref[1]
-    part = part_refs[0].shape[2]
-    for k, out in enumerate(part_refs):
-        column = jnp.bitwise_and(low + k, 3)
-        for h in range(2):
-            begin = (jnp.bitwise_and(high + h, 1) * 4 + column) * part
-            rows = term.at[:, pl.ds(pl.multiple_of(begin, part), part), :]
-            sent += fetch_all((rows,), (out.at[h],), sems, 2 * n + 4 + 2 * k + h)
+    size = row.shape[0] // 4
+    for i in range(4):
+        here = pl.ds(i * size, size)
+        row[here, :] = rows_wide[here, :].astype(BF16)
+        sent += fetch_all((row.at[here, :],), (row_hbm.at[here, :],), sems, 3 * n + 11 + i)
     for copy in sent:
         copy.wait()
 
@@ -223,7 +227,7 @@
             pltpu.VMEM((rows, LANES), BF16),
             pltpu.VMEM((slots, 2 * hidden), BF16),
             pltpu.VMEM((3, rank, hidden), BF16),
-            pltpu.SemaphoreType.DMA((2 * n + 12,)),
+            pltpu.SemaphoreType.DMA((3 * n + 15,)),
         ],
         name="core",
     )(where, near(got), act, slope, hid, *pieces)
@@ -258,7 +262,7 @@
         out_shape=jax.ShapeDtypeStruct((n_tok, width), BF16),
         scratch_shapes=[pltpu.VMEM(got.shape, F32)],
         name="combine",
-    )(match, near(got))
+    )(near(match), near(got))
 
 
 def swap(value):

time: 175 us -> 174 us (level)
  no operation moved by 1% of the time
where the time goes in v7:
time: 174 us; the launch traced here: 173 us
  starting transfers between devices  90.4 us (52%)
  waiting for transfers between devices  60.6 us (35%)
  Pallas kernels  17 us (10%)
  local copies, waits for them, and re-layouts  2.53 us (1%)
    all_to_all x2, starting transfers between devices, exchange(): lax.all_to_all(value.reshape(n_owner, rows // n_owner, lanes), 'expert',...  46.5 us
    ppermute x2, waiting for transfers between devices, swap(): return lax.ppermute(value, 'dp_0', [(0, 1), (1, 0)])  41.8 us
    ppermute x11, starting transfers between devices, shifted(): lax.ppermute(value, 'dp_1', [(i, (i + k) % size) for i in range(size)])  34.7 us
    ppermute x11, waiting for transfers between devices, shifted(): lax.ppermute(value, 'dp_1', [(i, (i + k) % size) for i in range(size)])  18.9 us
    ppermute x2, starting transfers between devices, swap(): return lax.ppermute(value, 'dp_0', [(0, 1), (1, 0)])  9.2 us
    pallas_call x1, Pallas kernels, core(): pl.pallas_call(functools.partial(core_kernel, places), in_specs=[pl.Block...  8.18 us
    pallas_call x1, Pallas kernels, pack(): pl.pallas_call(functools.partial(pack_kernel, cap), out_shape=(jax.ShapeD...  3.95 us
    pallas_call x1, Pallas kernels, slopes(): pl.pallas_call(slopes_kernel, out_shape=(jax.ShapeDtypeStruct((slots, hid...  3.58 us
  transfers between devices with their start and end apart: 15, of which 7 were waited for; matrix products, arithmetic and copies ran while one was open for 2% of the time, Pallas kernels for 2%

profile of v7, /device:TPU:17, one launch (start us, length us, event | category | flops | bytes accessed | tf_op | source)
XLA Modules:
  0.0 173.1 jit_solution(769296991070043460)
XLA Ops:
  0.6 3.9 %pack.1 = (bf16[7168,128]{1,0:T(8,128)(2,1)}, bf16[448,128]{1,0:T(8,128)(2,1)}) custom-call(s32[3,128]{1,0:T(4,128)} %bitcast.32, f32[3,128]{1,0:T(4,128)} %bitcast.33, bf16[128,1024]{1,0:T(8,128)(2,1)} %tok_ref.1, bf16[128,1024]{1,0:T(8,128)(2,1)} %grad_ref.1), custom_call_target="tpu_custom_call" | custom-call | tf_op jit(solution)/shard_map/pack/pallas_call | solution.py:67
  4.6 14.7 %all-to-all-start = ((bf16[64,112,128]{2,1,0:T(8,128)(2,1)}), bf16[64,112,128]{2,1,0:T(8,128)(2,1)S(1)}, u32[]{:S(2)}, u32[]{:S(2)}) async-start(bf16[64,112,128]{2,1,0:T(8,128)(2,1)} %bitcast.25), calls=%async_computation | async-start | bytes 3670016 | tf_op jit(solution)/shard_map/all_to_all | solution.py:279
  19.4 4.8 %collective-permute-start.4 = (bf16[128,2560]{1,0:T(8,128)(2,1)S(1)}, bf16[128,2560]{1,0:T(8,128)(2,1)S(1)}, u32[]{:S(2)}, u32[]{:S(2)}) collective-permute-start(bf16[128,2560]{1,0:T(8,128)(2,1)S(1)} %pad_maximum_fusion.refs_5_), channel_id=1, source_target_pairs={{0,256},{256,0},{1,257},{257,1},{2,258},{258,2},{3,259},{259,3},{4... | collective-permute-start | bytes 1966088 | tf_op jit(solution)/shard_map/ppermute | solution.py:269
  24.2 4.4 %collective-permute-start.1 = (bf16[128,2560]{1,0:T(8,128)(2,1)S(1)}, bf16[128,2560]{1,0:T(8,128)(2,1)S(1)}, u32[]{:S(2)}, u32[]{:S(2)}) collective-permute-start(bf16[128,2560]{1,0:T(8,128)(2,1)S(1)} %pad_maximum_fusion.refs_5_), channel_id=1, source_target_pairs={{0,192},{64,0},{128,64},{192,128},{1,193},{65,1},{129,65},{193,129... | collective-permute-start | bytes 1966088 | tf_op jit(solution)/shard_map/ppermute | solution.py:274
  28.5 1.9 %collective-permute-start = (bf16[128,2560]{1,0:T(8,128)(2,1)S(1)}, bf16[128,2560]{1,0:T(8,128)(2,1)S(1)}, u32[]{:S(2)}, u32[]{:S(2)}) collective-permute-start(bf16[128,2560]{1,0:T(8,128)(2,1)S(1)} %pad_maximum_fusion.refs_5_), channel_id=1, source_target_pairs={{0,64},{64,128},{128,192},{192,0},{1,65},{65,129},{129,193},{193,1... | collective-permute-start | bytes 1966088 | tf_op jit(solution)/shard_map/ppermute | solution.py:274
  30.5 31.6 %collective-permute-done.4.refs_10_ = bf16[128,2560]{1,0:T(8,128)(2,1)S(1)} collective-permute-done((bf16[128,2560]{1,0:T(8,128)(2,1)S(1)}, bf16[128,2560]{1,0:T(8,128)(2,1)S(1)}, u32[]{:S(2)}, u32[]{:S(2)}) %collective-permute-start.4) | collective-permute-done | bytes 655392 | tf_op jit(solution)/shard_map/ppermute | solution.py:269
  62.1 4.4 %collective-permute-start.6 = (bf16[128,2560]{1,0:T(8,128)(2,1)S(1)}, bf16[128,2560]{1,0:T(8,128)(2,1)S(1)}, u32[]{:S(2)}, u32[]{:S(2)}) collective-permute-start(bf16[128,2560]{1,0:T(8,128)(2,1)S(1)} %collective-permute-done.4.refs_10_), channel_id=1, source_target_pairs={{0,192},{64,0},{128,64},{192,128},{1,193},{65,1},{129,65},{193,129... | collective-permute-start | bytes 1966088 | tf_op jit(solution)/shard_map/ppermute | solution.py:274
  66.5 1.9 %collective-permute-start.5 = (bf16[128,2560]{1,0:T(8,128)(2,1)S(1)}, bf16[128,2560]{1,0:T(8,128)(2,1)S(1)}, u32[]{:S(2)}, u32[]{:S(2)}) collective-permute-start(bf16[128,2560]{1,0:T(8,128)(2,1)S(1)} %collective-permute-done.4.refs_10_), channel_id=1, source_target_pairs={{0,64},{64,128},{128,192},{192,0},{1,65},{65,129},{129,193},{193,1... | collective-permute-start | bytes 1966088 | tf_op jit(solution)/shard_map/ppermute | solution.py:274
  68.5 4.6 %collective-permute-start.3 = (bf16[64,2560]{1,0:T(8,128)(2,1)S(1)}, bf16[64,2560]{1,0:T(8,128)(2,1)}, u32[]{:S(2)}, u32[]{:S(2)}) collective-permute-start(bf16[64,2560]{1,0:T(8,128)(2,1)S(1)} %slice.26), channel_id=1, source_target_pairs={{0,192},{64,0},{128,64},{192,128},{1,193},{65,1},{129,65},{193,129... | collective-permute-start | bytes 983048 | tf_op jit(solution)/shard_map/ppermute | solution.py:274
  73.9 1.9 %collective-permute-start.2 = (bf16[64,2560]{1,0:T(8,128)(2,1)}, bf16[64,2560]{1,0:T(8,128)(2,1)}, u32[]{:S(2)}, u32[]{:S(2)}) collective-permute-start(bf16[64,2560]{1,0:T(8,128)(2,1)} %slice.25), channel_id=1, source_target_pairs={{0,64},{64,128},{128,192},{192,0},{1,65},{65,129},{129,193},{193,1... | collective-permute-start | bytes 983048 | tf_op jit(solution)/shard_map/ppermute | solution.py:274
  75.8 4.1 %collective-permute-done.6.refs_12_ = bf16[128,2560]{1,0:T(8,128)(2,1)S(1)} collective-permute-done((bf16[128,2560]{1,0:T(8,128)(2,1)S(1)}, bf16[128,2560]{1,0:T(8,128)(2,1)S(1)}, u32[]{:S(2)}, u32[]{:S(2)}) %collective-permute-start.6) | collective-permute-done | bytes 655392 | tf_op jit(solution)/shard_map/ppermute | solution.py:274
  80.7 5.3 %collective-permute-start.8 = (bf16[64,2560]{1,0:T(8,128)(2,1)}, bf16[64,2560]{1,0:T(8,128)(2,1)}, u32[]{:S(2)}, u32[]{:S(2)}) collective-permute-start(bf16[64,2560]{1,0:T(8,128)(2,1)} %slice.28), channel_id=1, source_target_pairs={{0,192},{64,0},{128,64},{192,128},{1,193},{65,1},{129,65},{193,129... | collective-permute-start | bytes 983048 | tf_op jit(solution)/shard_map/ppermute | solution.py:274
  86.8 1.9 %collective-permute-start.7 = (bf16[64,2560]{1,0:T(8,128)(2,1)}, bf16[64,2560]{1,0:T(8,128)(2,1)}, u32[]{:S(2)}, u32[]{:S(2)}) collective-permute-start(bf16[64,2560]{1,0:T(8,128)(2,1)} %slice.27), channel_id=1, source_target_pairs={{0,64},{64,128},{128,192},{192,0},{1,65},{65,129},{129,193},{193,1... | collective-permute-start | bytes 983048 | tf_op jit(solution)/shard_map/ppermute | solution.py:274
  88.8 3.6 %slopes.1 = (f32[448,768]{1,0:T(8,128)}, f32[448,768]{1,0:T(8,128)}, bf16[448,768]{1,0:T(8,128)(2,1)}) custom-call(bf16[448,1536]{1,0:T(8,128)(2,1)} %bitcast.26), custom_call_target="tpu_custom_call" | custom-call | tf_op jit(solution)/shard_map/slopes/pallas_call | solution.py:125
  93.7 3.9 %collective-permute-done.7.refs_13_ = bf16[64,2560]{1,0:T(8,128)(2,1)} collective-permute-done((bf16[64,2560]{1,0:T(8,128)(2,1)}, bf16[64,2560]{1,0:T(8,128)(2,1)}, u32[]{:S(2)}, u32[]{:S(2)}) %collective-permute-start.7) | collective-permute-done | bytes 327712 | tf_op jit(solution)/shard_map/ppermute | solution.py:274
  97.6 8.2 %core.1 = (bf16[3584,128]{1,0:T(8,128)(2,1)}, bf16[2,3,32,768]{3,2,1,0:T(8,128)(2,1)}, bf16[2,3,32,768]{3,2,1,0:T(8,128)(2,1)}, bf16[2,3,32,768]{3,2,1,0:T(8,128)(2,1)}, bf16[2,3,32,768]{3,2,1,0:T(8,128)(2,1)}) custom-call(s32[2]{0:T(128)} %pad_add_fusion.refs_0_, bf16[7168,128]{1,0:T(8,128)(2,1)S(1)} %bitcast.23, f32[448,768]{1,0:T(8,128)} %get-tuple-element.14.refs_2_, ...), custom_call_target="tpu_custom_call" | custom-call | tf_op jit(solution)/shard_map/core/pallas_call | solution.py:209
  105.8 31.8 %all-to-all-start.1 = ((bf16[64,56,128]{2,1,0:T(8,128)(2,1)}), bf16[64,56,128]{2,1,0:T(8,128)(2,1)S(1)}, u32[]{:S(2)}, u32[]{:S(2)}) async-start(bf16[64,56,128]{2,1,0:T(8,128)(2,1)} %bitcast.27), calls=%async_computation.1 | async-start | bytes 1835008 | tf_op jit(solution)/shard_map/all_to_all | solution.py:279
  137.7 1.9 %collective-permute-start.9 = (bf16[2,3,32,768]{3,2,1,0:T(8,128)(2,1)S(1)}, bf16[2,3,32,768]{3,2,1,0:T(8,128)(2,1)S(1)}, u32[]{:S(2)}, u32[]{:S(2)}) collective-permute-start(bf16[2,3,32,768]{3,2,1,0:T(8,128)(2,1)S(1)} %copy-done.14), channel_id=1, source_target_pairs={{0,128},{64,192},{128,0},{192,64},{1,129},{65,193},{129,1},{193,65... | collective-permute-start | bytes 884744 | tf_op jit(solution)/shard_map/ppermute | solution.py:274
  139.6 1.9 %collective-permute-start.10 = (bf16[2,3,32,768]{3,2,1,0:T(8,128)(2,1)S(1)}, bf16[2,3,32,768]{3,2,1,0:T(8,128)(2,1)S(1)}, u32[]{:S(2)}, u32[]{:S(2)}) collective-permute-start(bf16[2,3,32,768]{3,2,1,0:T(8,128)(2,1)S(1)} %copy-done.13), channel_id=1, source_target_pairs={{0,64},{64,128},{128,192},{192,0},{1,65},{65,129},{129,193},{193,1... | collective-permute-start | bytes 884744 | tf_op jit(solution)/shard_map/ppermute | solution.py:274
  141.6 4.6 %collective-permute-start.11 = (bf16[2,3,32,768]{3,2,1,0:T(8,128)(2,1)S(1)}, bf16[2,3,32,768]{3,2,1,0:T(8,128)(2,1)S(1)}, u32[]{:S(2)}, u32[]{:S(2)}) collective-permute-start(bf16[2,3,32,768]{3,2,1,0:T(8,128)(2,1)S(1)} %copy-done.12), channel_id=1, source_target_pairs={{0,192},{64,0},{128,64},{192,128},{1,193},{65,1},{129,65},{193,129... | collective-permute-start | bytes 884744 | tf_op jit(solution)/shard_map/ppermute | solution.py:274
  146.1 3.2 %collective-permute-done.9 = bf16[2,3,32,768]{3,2,1,0:T(8,128)(2,1)S(1)} collective-permute-done((bf16[2,3,32,768]{3,2,1,0:T(8,128)(2,1)S(1)}, bf16[2,3,32,768]{3,2,1,0:T(8,128)(2,1)S(1)}, u32[]{:S(2)}, u32[]{:S(2)}) %collective-permute-start.9) | collective-permute-done | bytes 294944 | tf_op jit(solution)/shard_map/ppermute | solution.py:274
  149.3 7.0 %collective-permute-done.10 = bf16[2,3,32,768]{3,2,1,0:T(8,128)(2,1)S(1)} collective-permute-done((bf16[2,3,32,768]{3,2,1,0:T(8,128)(2,1)S(1)}, bf16[2,3,32,768]{3,2,1,0:T(8,128)(2,1)S(1)}, u32[]{:S(2)}, u32[]{:S(2)}) %collective-permute-start.10) | collective-permute-done | bytes 294944 | tf_op jit(solution)/shard_map/ppermute | solution.py:274
  156.5 4.4 %collective-permute-start.12 = (bf16[3,32,768]{2,1,0:T(8,128)(2,1)S(1)}, bf16[3,32,768]{2,1,0:T(8,128)(2,1)S(1)}, u32[]{:S(2)}, u32[]{:S(2)}) collective-permute-start(bf16[3,32,768]{2,1,0:T(8,128)(2,1)S(1)} %fusion.2), channel_id=1, source_target_pairs={{0,256},{256,0},{1,257},{257,1},{2,258},{258,2},{3,259},{259,3},{4... | collective-permute-start | bytes 442376 | tf_op jit(solution)/shard_map/ppermute | solution.py:269
  161.0 10.1 %collective-permute-done.12 = bf16[3,32,768]{2,1,0:T(8,128)(2,1)S(1)} collective-permute-done((bf16[3,32,768]{2,1,0:T(8,128)(2,1)S(1)}, bf16[3,32,768]{2,1,0:T(8,128)(2,1)S(1)}, u32[]{:S(2)}, u32[]{:S(2)}) %collective-permute-start.12) | collective-permute-done | bytes 147488 | tf_op jit(solution)/shard_map/ppermute | solution.py:269
  (49 shorter events, 6.2 us)
Async XLA Ops:
  4.6 93.0 %all-to-all-start = ((bf16[64,112,128]{2,1,0:T(8,128)(2,1)}), bf16[64,112,128]{2,1,0:T(8,128)(2,1)S(1)}, u32[]{:S(2)}, u32[]{:S(2)}) async-start(bf16[64,112,128]{2,1,0:T(8,128)(2,1)} %bitcast.25), calls=%async_computation | async-start | bytes 3670016 | tf_op jit(solution)/shard_map/all_to_all | solution.py:279
  19.4 67.4 %copy-start.1 = (bf16[128,2560]{1,0:T(8,128)(2,1)}, bf16[128,2560]{1,0:T(8,128)(2,1)S(1)}, u32[]{:S(2)}) copy-start(bf16[128,2560]{1,0:T(8,128)(2,1)S(1)} %pad_maximum_fusion.refs_5_) | copy-start | bytes 1966084
  19.4 42.7 %collective-permute-start.4 = (bf16[128,2560]{1,0:T(8,128)(2,1)S(1)}, bf16[128,2560]{1,0:T(8,128)(2,1)S(1)}, u32[]{:S(2)}, u32[]{:S(2)}) collective-permute-start(bf16[128,2560]{1,0:T(8,128)(2,1)S(1)} %pad_maximum_fusion.refs_5_), channel_id=1, source_target_pairs={{0,256},{256,0},{1,257},{257,1},{2,258},{258,2},{3,259},{259,3},{4... | collective-permute-start | bytes 1966088 | tf_op jit(solution)/shard_map/ppermute | solution.py:269
  24.2 44.3 %collective-permute-start.1 = (bf16[128,2560]{1,0:T(8,128)(2,1)S(1)}, bf16[128,2560]{1,0:T(8,128)(2,1)S(1)}, u32[]{:S(2)}, u32[]{:S(2)}) collective-permute-start(bf16[128,2560]{1,0:T(8,128)(2,1)S(1)} %pad_maximum_fusion.refs_5_), channel_id=1, source_target_pairs={{0,192},{64,0},{128,64},{192,128},{1,193},{65,1},{129,65},{193,129... | collective-permute-start | bytes 1966088 | tf_op jit(solution)/shard_map/ppermute | solution.py:274
  28.5 44.5 %collective-permute-start = (bf16[128,2560]{1,0:T(8,128)(2,1)S(1)}, bf16[128,2560]{1,0:T(8,128)(2,1)S(1)}, u32[]{:S(2)}, u32[]{:S(2)}) collective-permute-start(bf16[128,2560]{1,0:T(8,128)(2,1)S(1)} %pad_maximum_fusion.refs_5_), channel_id=1, source_target_pairs={{0,64},{64,128},{128,192},{192,0},{1,65},{65,129},{129,193},{193,1... | collective-permute-start | bytes 1966088 | tf_op jit(solution)/shard_map/ppermute | solution.py:274
  62.1 35.5 %copy-start.6 = (bf16[128,2560]{1,0:T(8,128)(2,1)}, bf16[128,2560]{1,0:T(8,128)(2,1)S(1)}, u32[]{:S(2)}) copy-start(bf16[128,2560]{1,0:T(8,128)(2,1)S(1)} %collective-permute-done.4.refs_10_) | copy-start | bytes 1966084
  62.1 17.8 %collective-permute-start.6 = (bf16[128,2560]{1,0:T(8,128)(2,1)S(1)}, bf16[128,2560]{1,0:T(8,128)(2,1)S(1)}, u32[]{:S(2)}, u32[]{:S(2)}) collective-permute-start(bf16[128,2560]{1,0:T(8,128)(2,1)S(1)} %collective-permute-done.4.refs_10_), channel_id=1, source_target_pairs={{0,192},{64,0},{128,64},{192,128},{1,193},{65,1},{129,65},{193,129... | collective-permute-start | bytes 1966088 | tf_op jit(solution)/shard_map/ppermute | solution.py:274
  66.5 19.5 %collective-permute-start.5 = (bf16[128,2560]{1,0:T(8,128)(2,1)S(1)}, bf16[128,2560]{1,0:T(8,128)(2,1)S(1)}, u32[]{:S(2)}, u32[]{:S(2)}) collective-permute-start(bf16[128,2560]{1,0:T(8,128)(2,1)S(1)} %collective-permute-done.4.refs_10_), channel_id=1, source_target_pairs={{0,64},{64,128},{128,192},{192,0},{1,65},{65,129},{129,193},{193,1... | collective-permute-start | bytes 1966088 | tf_op jit(solution)/shard_map/ppermute | solution.py:274
  68.4 18.4 %copy-start.2 = (bf16[128,2560]{1,0:T(8,128)(2,1)}, bf16[128,2560]{1,0:T(8,128)(2,1)S(1)}, u32[]{:S(2)}) copy-start(bf16[128,2560]{1,0:T(8,128)(2,1)S(1)} %collective-permute-done.1.refs_7_) | copy-start | bytes 1966084
  68.5 24.5 %collective-permute-start.3 = (bf16[64,2560]{1,0:T(8,128)(2,1)S(1)}, bf16[64,2560]{1,0:T(8,128)(2,1)}, u32[]{:S(2)}, u32[]{:S(2)}) collective-permute-start(bf16[64,2560]{1,0:T(8,128)(2,1)S(1)} %slice.26), channel_id=1, source_target_pairs={{0,192},{64,0},{128,64},{192,128},{1,193},{65,1},{129,65},{193,129... | collective-permute-start | bytes 983048 | tf_op jit(solution)/shard_map/ppermute | solution.py:274
  73.1 19.3 %copy-start.3 = (bf16[128,2560]{1,0:T(8,128)(2,1)}, bf16[128,2560]{1,0:T(8,128)(2,1)S(1)}, u32[]{:S(2)}) copy-start(bf16[128,2560]{1,0:T(8,128)(2,1)S(1)} %collective-permute-done.refs_6_) | copy-start | bytes 1966084
  73.9 19.1 %collective-permute-start.2 = (bf16[64,2560]{1,0:T(8,128)(2,1)}, bf16[64,2560]{1,0:T(8,128)(2,1)}, u32[]{:S(2)}, u32[]{:S(2)}) collective-permute-start(bf16[64,2560]{1,0:T(8,128)(2,1)} %slice.25), channel_id=1, source_target_pairs={{0,64},{64,128},{128,192},{192,0},{1,65},{65,129},{129,193},{193,1... | collective-permute-start | bytes 983048 | tf_op jit(solution)/shard_map/ppermute | solution.py:274
  80.7 13.1 %collective-permute-start.8 = (bf16[64,2560]{1,0:T(8,128)(2,1)}, bf16[64,2560]{1,0:T(8,128)(2,1)}, u32[]{:S(2)}, u32[]{:S(2)}) collective-permute-start(bf16[64,2560]{1,0:T(8,128)(2,1)} %slice.28), channel_id=1, source_target_pairs={{0,192},{64,0},{128,64},{192,128},{1,193},{65,1},{129,65},{193,129... | collective-permute-start | bytes 983048 | tf_op jit(solution)/shard_map/ppermute | solution.py:274
  86.8 10.8 %collective-permute-start.7 = (bf16[64,2560]{1,0:T(8,128)(2,1)}, bf16[64,2560]{1,0:T(8,128)(2,1)}, u32[]{:S(2)}, u32[]{:S(2)}) collective-permute-start(bf16[64,2560]{1,0:T(8,128)(2,1)} %slice.27), channel_id=1, source_target_pairs={{0,64},{64,128},{128,192},{192,0},{1,65},{65,129},{129,193},{193,1... | collective-permute-start | bytes 983048 | tf_op jit(solution)/shard_map/ppermute | solution.py:274
  105.8 31.9 %copy-start.14 = (bf16[2,3,32,768]{3,2,1,0:T(8,128)(2,1)S(1)}, bf16[2,3,32,768]{3,2,1,0:T(8,128)(2,1)}, u32[]{:S(2)}) copy-start(bf16[2,3,32,768]{3,2,1,0:T(8,128)(2,1)} %get-tuple-element.19) | copy-start | bytes 884740
  105.8 33.8 %copy-start.13 = (bf16[2,3,32,768]{3,2,1,0:T(8,128)(2,1)S(1)}, bf16[2,3,32,768]{3,2,1,0:T(8,128)(2,1)}, u32[]{:S(2)}) copy-start(bf16[2,3,32,768]{3,2,1,0:T(8,128)(2,1)} %get-tuple-element.20) | copy-start | bytes 884740
  105.8 35.7 %copy-start.12 = (bf16[2,3,32,768]{3,2,1,0:T(8,128)(2,1)S(1)}, bf16[2,3,32,768]{3,2,1,0:T(8,128)(2,1)}, u32[]{:S(2)}) copy-start(bf16[2,3,32,768]{3,2,1,0:T(8,128)(2,1)} %get-tuple-element.21) | copy-start | bytes 884740
  105.8 50.5 %copy-start.7 = (bf16[2,3,32,768]{3,2,1,0:T(8,128)(2,1)S(1)}, bf16[2,3,32,768]{3,2,1,0:T(8,128)(2,1)}, u32[]{:S(2)}) copy-start(bf16[2,3,32,768]{3,2,1,0:T(8,128)(2,1)} %get-tuple-element.18) | copy-start | bytes 884740
  105.8 66.0 %all-to-all-start.1 = ((bf16[64,56,128]{2,1,0:T(8,128)(2,1)}), bf16[64,56,128]{2,1,0:T(8,128)(2,1)S(1)}, u32[]{:S(2)}, u32[]{:S(2)}) async-start(bf16[64,56,128]{2,1,0:T(8,128)(2,1)} %bitcast.27), calls=%async_computation.1 | async-start | bytes 1835008 | tf_op jit(solution)/shard_map/all_to_all | solution.py:279
  137.7 11.6 %collective-permute-start.9 = (bf16[2,3,32,768]{3,2,1,0:T(8,128)(2,1)S(1)}, bf16[2,3,32,768]{3,2,1,0:T(8,128)(2,1)S(1)}, u32[]{:S(2)}, u32[]{:S(2)}) collective-permute-start(bf16[2,3,32,768]{3,2,1,0:T(8,128)(2,1)S(1)} %copy-done.14), channel_id=1, source_target_pairs={{0,128},{64,192},{128,0},{192,64},{1,129},{65,193},{129,1},{193,65... | collective-permute-start | bytes 884744 | tf_op jit(solution)/shard_map/ppermute | solution.py:274
  139.6 16.7 %collective-permute-start.10 = (bf16[2,3,32,768]{3,2,1,0:T(8,128)(2,1)S(1)}, bf16[2,3,32,768]{3,2,1,0:T(8,128)(2,1)S(1)}, u32[]{:S(2)}, u32[]{:S(2)}) collective-permute-start(bf16[2,3,32,768]{3,2,1,0:T(8,128)(2,1)S(1)} %copy-done.13), channel_id=1, source_target_pairs={{0,64},{64,128},{128,192},{192,0},{1,65},{65,129},{129,193},{193,1... | collective-permute-start | bytes 884744 | tf_op jit(solution)/shard_map/ppermute | solution.py:274
  141.6 14.8 %collective-permute-start.11 = (bf16[2,3,32,768]{3,2,1,0:T(8,128)(2,1)S(1)}, bf16[2,3,32,768]{3,2,1,0:T(8,128)(2,1)S(1)}, u32[]{:S(2)}, u32[]{:S(2)}) collective-permute-start(bf16[2,3,32,768]{3,2,1,0:T(8,128)(2,1)S(1)} %copy-done.12), channel_id=1, source_target_pairs={{0,192},{64,0},{128,64},{192,128},{1,193},{65,1},{129,65},{193,129... | collective-permute-start | bytes 884744 | tf_op jit(solution)/shard_map/ppermute | solution.py:274
  156.3 15.5 %copy-start = (bf16[448,128]{1,0:T(8,128)(2,1)S(1)}, bf16[448,128]{1,0:T(8,128)(2,1)}, u32[]{:S(2)}) copy-start(bf16[448,128]{1,0:T(8,128)(2,1)} %get-tuple-element.12.match_ref) | copy-start | bytes 344068
  156.5 14.6 %collective-permute-start.12 = (bf16[3,32,768]{2,1,0:T(8,128)(2,1)S(1)}, bf16[3,32,768]{2,1,0:T(8,128)(2,1)S(1)}, u32[]{:S(2)}, u32[]{:S(2)}) collective-permute-start(bf16[3,32,768]{2,1,0:T(8,128)(2,1)S(1)} %fusion.2), channel_id=1, source_target_pairs={{0,256},{256,0},{1,257},{257,1},{2,258},{258,2},{3,259},{259,3},{4... | collective-permute-start | bytes 442376 | tf_op jit(solution)/shard_map/ppermute | solution.py:269
  (6 other events, 70.5 us)

commit v8 on v7

--- a/solution.py
+++ b/solution.py
@@ -160,15 +160,15 @@
     grad = jnp.dot(dy_rows[...], w1[:, :hidden], preferred_element_type=F32)
     for copy in factors_in:
         copy.wait()
-    both[:, :hidden] = (grad * slope[...]).astype(BF16)
-    both[:, hidden:] = (grad * act[...]).astype(BF16)
+    both[:, :hidden] = (grad * act[...]).astype(BF16)
+    both[:, hidden:] = (grad * slope[...]).astype(BF16)
     for copy in basis_in:
         copy.wait()
     dy_proj = jnp.dot(dy_rows[...], w1[:, hidden:], preferred_element_type=F32).astype(BF16)
     x_proj = jnp.dot(x_rows[...], w1[:, hidden:], preferred_element_type=F32).astype(BF16)
     by_rows = (((0,), (0,)), ((), ()))
     for t, (left, right) in enumerate(
-        ((x_proj, both[:, :hidden]), (x_proj, both[:, hidden:]), (dy_proj, hid[...]))
+        ((x_proj, both[:, hidden:]), (x_proj, both[:, :hidden]), (dy_proj, hid[...]))
     ):
         term[t] = lax.dot_general(left, right, by_rows, preferred_element_type=F32).astype(BF16)
     high, low = where_ref[0], where_ref[1]
@@ -291,10 +291,13 @@
     cap = slots // n_owner
     where = jnp.stack([lax.axis_index("dp_0"), lax.axis_index("dp_1")]).astype(jnp.int32)
 
-    own = jnp.concatenate([down_weight[0], basis[0], gate_weight[0], up_weight[0]], axis=1)
-    far = swap(own)
+    far_gate = swap(gate_weight[0])
+    rest = jnp.concatenate([down_weight[0], basis[0], up_weight[0]], axis=1)
+    far_rest = swap(rest)
     sent, match = pack(expert_ids.T, gate_probs.T, tokens, out_grad, n_owner, cap)
     got = exchange(sent, n_owner)
+    own = jnp.concatenate([rest, gate_weight[0]], axis=1)
+    far = jnp.concatenate([far_rest, far_gate], axis=1)
     pieces, places = [], []
     half = own.shape[0] // 2
     for other, block in enumerate((own, far)):

time: 174 us -> 174 us (level)
  starting transfers between devices: 90.4 us -> 94.1 us
  waiting for transfers between devices: 60.6 us -> 58.4 us
    ppermute x2 -> x3, waiting for transfers between devices: 41.8 us -> 37.3 us  [swap(): return lax.ppermute(value, 'dp_0', [(0, 1), (1, 0)])]
    ppermute x2 -> x3, starting transfers between devices: 9.2 us -> 13.6 us  [swap(): return lax.ppermute(value, 'dp_0', [(0, 1), (1, 0)])]
    ppermute x11, waiting for transfers between devices: 18.9 us -> 21.2 us  [shifted(): lax.ppermute(value, 'dp_1', [(i, (i + k) % size) for i in range(size)])]
  transfers between devices with their start and end apart: 15 -> 16, of which waited for: 7 -> 8; matrix products, arithmetic and copies ran while one was open for 2% -> 1% of each run, Pallas kernels for 2% -> 2%
where the time goes in v8:
time: 174 us; the launch traced here: 173 us
  starting transfers between devices  94.1 us (54%)
  waiting for transfers between devices  58.4 us (34%)
  Pallas kernels  16.9 us (10%)
    all_to_all x2, starting transfers between devices, exchange(): lax.all_to_all(value.reshape(n_owner, rows // n_owner, lanes), 'expert',...  45.7 us
    ppermute x3, waiting for transfers between devices, swap(): return lax.ppermute(value, 'dp_0', [(0, 1), (1, 0)])  37.3 us
    ppermute x11, starting transfers between devices, shifted(): lax.ppermute(value, 'dp_1', [(i, (i + k) % size) for i in range(size)])  34.8 us
    ppermute x11, waiting for transfers between devices, shifted(): lax.ppermute(value, 'dp_1', [(i, (i + k) % size) for i in range(size)])  21.2 us
    ppermute x3, starting transfers between devices, swap(): return lax.ppermute(value, 'dp_0', [(0, 1), (1, 0)])  13.6 us
    pallas_call x1, Pallas kernels, core(): pl.pallas_call(functools.partial(core_kernel, places), in_specs=[pl.Block...  8.14 us
    pallas_call x1, Pallas kernels, pack(): pl.pallas_call(functools.partial(pack_kernel, cap), out_shape=(jax.ShapeD...  3.94 us
    pallas_call x1, Pallas kernels, slopes(): pl.pallas_call(slopes_kernel, out_shape=(jax.ShapeDtypeStruct((slots, hid...  3.58 us
  transfers between devices with their start and end apart: 16, of which 8 were waited for; matrix products, arithmetic and copies ran while one was open for 1% of the time, Pallas kernels for 2%

profile of v8, /device:TPU:17, one launch (start us, length us, event | category | flops | bytes accessed | tf_op | source)
XLA Modules:
  0.0 173.1 jit_solution(3778678070950050550)
XLA Ops:
  0.6 3.9 %pack.1 = (bf16[7168,128]{1,0:T(8,128)(2,1)}, bf16[448,128]{1,0:T(8,128)(2,1)}) custom-call(s32[3,128]{1,0:T(4,128)} %bitcast.36, f32[3,128]{1,0:T(4,128)} %bitcast.37, bf16[128,1024]{1,0:T(8,128)(2,1)} %tok_ref.1, bf16[128,1024]{1,0:T(8,128)(2,1)} %grad_ref.1), custom_call_target="tpu_custom_call" | custom-call | tf_op jit(solution)/shard_map/pack/pallas_call | solution.py:67
  4.6 14.7 %all-to-all-start = ((bf16[64,112,128]{2,1,0:T(8,128)(2,1)}), bf16[64,112,128]{2,1,0:T(8,128)(2,1)S(1)}, u32[]{:S(2)}, u32[]{:S(2)}) async-start(bf16[64,112,128]{2,1,0:T(8,128)(2,1)} %bitcast.25), calls=%async_computation | async-start | bytes 3670016 | tf_op jit(solution)/shard_map/all_to_all | solution.py:279
  19.3 4.8 %collective-permute-start.4 = (bf16[128,1792]{1,0:T(8,128)(2,1)S(1)}, bf16[128,1792]{1,0:T(8,128)(2,1)S(1)}, u32[]{:S(2)}, u32[]{:S(2)}) collective-permute-start(bf16[128,1792]{1,0:T(8,128)(2,1)S(1)} %pad_maximum_fusion.1), channel_id=1, source_target_pairs={{0,256},{256,0},{1,257},{257,1},{2,258},{258,2},{3,259},{259,3},{4... | collective-permute-start | bytes 1376264 | tf_op jit(solution)/shard_map/ppermute | solution.py:269
  24.1 4.4 %collective-permute-start.5 = (bf16[128,768]{1,0:T(8,128)(2,1)S(1)}, bf16[128,768]{1,0:T(8,128)(2,1)S(1)}, u32[]{:S(2)}, u32[]{:S(2)}) collective-permute-start(bf16[128,768]{1,0:T(8,128)(2,1)S(1)} %bitcast.34), channel_id=1, source_target_pairs={{0,256},{256,0},{1,257},{257,1},{2,258},{258,2},{3,259},{259,3},{4... | collective-permute-start | bytes 589832 | tf_op jit(solution)/shard_map/ppermute | solution.py:269
  28.6 4.4 %collective-permute-start.1 = (bf16[128,2560]{1,0:T(8,128)(2,1)S(1)}, bf16[128,2560]{1,0:T(8,128)(2,1)S(1)}, u32[]{:S(2)}, u32[]{:S(2)}) collective-permute-start(bf16[128,2560]{1,0:T(8,128)(2,1)S(1)} %pad_maximum_fusion.refs_5_), channel_id=1, source_target_pairs={{0,192},{64,0},{128,64},{192,128},{1,193},{65,1},{129,65},{193,129... | collective-permute-start | bytes 1966088 | tf_op jit(solution)/shard_map/ppermute | solution.py:274
  33.0 1.9 %collective-permute-start = (bf16[128,2560]{1,0:T(8,128)(2,1)S(1)}, bf16[128,2560]{1,0:T(8,128)(2,1)S(1)}, u32[]{:S(2)}, u32[]{:S(2)}) collective-permute-start(bf16[128,2560]{1,0:T(8,128)(2,1)S(1)} %pad_maximum_fusion.refs_5_), channel_id=1, source_target_pairs={{0,64},{64,128},{128,192},{192,0},{1,65},{65,129},{129,193},{193,1... | collective-permute-start | bytes 1966088 | tf_op jit(solution)/shard_map/ppermute | solution.py:274
  34.9 22.9 %collective-permute-done.4 = bf16[128,1792]{1,0:T(8,128)(2,1)S(1)} collective-permute-done((bf16[128,1792]{1,0:T(8,128)(2,1)S(1)}, bf16[128,1792]{1,0:T(8,128)(2,1)S(1)}, u32[]{:S(2)}, u32[]{:S(2)}) %collective-permute-start.4) | collective-permute-done | bytes 458784 | tf_op jit(solution)/shard_map/ppermute | solution.py:269
  57.9 4.2 %collective-permute-done.5 = bf16[128,768]{1,0:T(8,128)(2,1)S(1)} collective-permute-done((bf16[128,768]{1,0:T(8,128)(2,1)S(1)}, bf16[128,768]{1,0:T(8,128)(2,1)S(1)}, u32[]{:S(2)}, u32[]{:S(2)}) %collective-permute-start.5) | collective-permute-done | bytes 196640 | tf_op jit(solution)/shard_map/ppermute | solution.py:269
  62.1 4.4 %collective-permute-start.7 = (bf16[128,2560]{1,0:T(8,128)(2,1)S(1)}, bf16[128,2560]{1,0:T(8,128)(2,1)S(1)}, u32[]{:S(2)}, u32[]{:S(2)}) collective-permute-start(bf16[128,2560]{1,0:T(8,128)(2,1)S(1)} %constant_dynamic-update-slice_fusion.refs_10_), channel_id=1, source_target_pairs={{0,192},{64,0},{128,64},{192,128},{1,193},{65,1},{129,65},{193,129... | collective-permute-start | bytes 1966088 | tf_op jit(solution)/shard_map/ppermute | solution.py:274
  66.5 1.9 %collective-permute-start.6 = (bf16[128,2560]{1,0:T(8,128)(2,1)S(1)}, bf16[128,2560]{1,0:T(8,128)(2,1)S(1)}, u32[]{:S(2)}, u32[]{:S(2)}) collective-permute-start(bf16[128,2560]{1,0:T(8,128)(2,1)S(1)} %constant_dynamic-update-slice_fusion.refs_10_), channel_id=1, source_target_pairs={{0,64},{64,128},{128,192},{192,0},{1,65},{65,129},{129,193},{193,1... | collective-permute-start | bytes 1966088 | tf_op jit(solution)/shard_map/ppermute | solution.py:274
  68.5 4.6 %collective-permute-start.3 = (bf16[64,2560]{1,0:T(8,128)(2,1)S(1)}, bf16[64,2560]{1,0:T(8,128)(2,1)}, u32[]{:S(2)}, u32[]{:S(2)}) collective-permute-start(bf16[64,2560]{1,0:T(8,128)(2,1)S(1)} %slice.26), channel_id=1, source_target_pairs={{0,192},{64,0},{128,64},{192,128},{1,193},{65,1},{129,65},{193,129... | collective-permute-start | bytes 983048 | tf_op jit(solution)/shard_map/ppermute | solution.py:274
  73.1 1.9 %collective-permute-start.2 = (bf16[64,2560]{1,0:T(8,128)(2,1)S(1)}, bf16[64,2560]{1,0:T(8,128)(2,1)}, u32[]{:S(2)}, u32[]{:S(2)}) collective-permute-start(bf16[64,2560]{1,0:T(8,128)(2,1)S(1)} %slice.25), channel_id=1, source_target_pairs={{0,64},{64,128},{128,192},{192,0},{1,65},{65,129},{129,193},{193,1... | collective-permute-start | bytes 983048 | tf_op jit(solution)/shard_map/ppermute | solution.py:274
  75.1 4.8 %collective-permute-done.7.refs_12_ = bf16[128,2560]{1,0:T(8,128)(2,1)S(1)} collective-permute-done((bf16[128,2560]{1,0:T(8,128)(2,1)S(1)}, bf16[128,2560]{1,0:T(8,128)(2,1)S(1)}, u32[]{:S(2)}, u32[]{:S(2)}) %collective-permute-start.7) | collective-permute-done | bytes 655392 | tf_op jit(solution)/shard_map/ppermute | solution.py:274
  79.9 5.3 %collective-permute-start.9 = (bf16[64,2560]{1,0:T(8,128)(2,1)S(1)}, bf16[64,2560]{1,0:T(8,128)(2,1)}, u32[]{:S(2)}, u32[]{:S(2)}) collective-permute-start(bf16[64,2560]{1,0:T(8,128)(2,1)S(1)} %slice.28), channel_id=1, source_target_pairs={{0,192},{64,0},{128,64},{192,128},{1,193},{65,1},{129,65},{193,129... | collective-permute-start | bytes 983048 | tf_op jit(solution)/shard_map/ppermute | solution.py:274
  88.0 3.6 %slopes.1 = (f32[448,768]{1,0:T(8,128)}, f32[448,768]{1,0:T(8,128)}, bf16[448,768]{1,0:T(8,128)(2,1)}) custom-call(bf16[448,1536]{1,0:T(8,128)(2,1)} %bitcast.26), custom_call_target="tpu_custom_call" | custom-call | tf_op jit(solution)/shard_map/slopes/pallas_call | solution.py:125
  93.9 4.5 %collective-permute-done.8.refs_13_ = bf16[64,2560]{1,0:T(8,128)(2,1)} collective-permute-done((bf16[64,2560]{1,0:T(8,128)(2,1)}, bf16[64,2560]{1,0:T(8,128)(2,1)}, u32[]{:S(2)}, u32[]{:S(2)}) %collective-permute-start.8) | collective-permute-done | bytes 327712 | tf_op jit(solution)/shard_map/ppermute | solution.py:274
  98.4 8.1 %core.1 = (bf16[3584,128]{1,0:T(8,128)(2,1)}, bf16[2,3,32,768]{3,2,1,0:T(8,128)(2,1)}, bf16[2,3,32,768]{3,2,1,0:T(8,128)(2,1)}, bf16[2,3,32,768]{3,2,1,0:T(8,128)(2,1)}, bf16[2,3,32,768]{3,2,1,0:T(8,128)(2,1)}) custom-call(s32[2]{0:T(128)} %pad_add_fusion.refs_0_, bf16[7168,128]{1,0:T(8,128)(2,1)S(1)} %bitcast.23, f32[448,768]{1,0:T(8,128)} %get-tuple-element.14.refs_2_, ...), custom_call_target="tpu_custom_call" | custom-call | tf_op jit(solution)/shard_map/core/pallas_call | solution.py:209
  106.6 31.0 %all-to-all-start.1 = ((bf16[64,56,128]{2,1,0:T(8,128)(2,1)}), bf16[64,56,128]{2,1,0:T(8,128)(2,1)S(1)}, u32[]{:S(2)}, u32[]{:S(2)}) async-start(bf16[64,56,128]{2,1,0:T(8,128)(2,1)} %bitcast.27), calls=%async_computation.1 | async-start | bytes 1835008 | tf_op jit(solution)/shard_map/all_to_all | solution.py:279
  137.7 1.9 %collective-permute-start.10 = (bf16[2,3,32,768]{3,2,1,0:T(8,128)(2,1)S(1)}, bf16[2,3,32,768]{3,2,1,0:T(8,128)(2,1)S(1)}, u32[]{:S(2)}, u32[]{:S(2)}) collective-permute-start(bf16[2,3,32,768]{3,2,1,0:T(8,128)(2,1)S(1)} %copy-done.14), channel_id=1, source_target_pairs={{0,128},{64,192},{128,0},{192,64},{1,129},{65,193},{129,1},{193,65... | collective-permute-start | bytes 884744 | tf_op jit(solution)/shard_map/ppermute | solution.py:274
  141.5 4.6 %collective-permute-start.12 = (bf16[2,3,32,768]{3,2,1,0:T(8,128)(2,1)S(1)}, bf16[2,3,32,768]{3,2,1,0:T(8,128)(2,1)S(1)}, u32[]{:S(2)}, u32[]{:S(2)}) collective-permute-start(bf16[2,3,32,768]{3,2,1,0:T(8,128)(2,1)S(1)} %copy-done.12), channel_id=1, source_target_pairs={{0,192},{64,0},{128,64},{192,128},{1,193},{65,1},{129,65},{193,129... | collective-permute-start | bytes 884744 | tf_op jit(solution)/shard_map/ppermute | solution.py:274
  146.1 3.2 %collective-permute-done.10 = bf16[2,3,32,768]{3,2,1,0:T(8,128)(2,1)S(1)} collective-permute-done((bf16[2,3,32,768]{3,2,1,0:T(8,128)(2,1)S(1)}, bf16[2,3,32,768]{3,2,1,0:T(8,128)(2,1)S(1)}, u32[]{:S(2)}, u32[]{:S(2)}) %collective-permute-start.10) | collective-permute-done | bytes 294944 | tf_op jit(solution)/shard_map/ppermute | solution.py:274
  149.3 7.0 %collective-permute-done.11 = bf16[2,3,32,768]{3,2,1,0:T(8,128)(2,1)S(1)} collective-permute-done((bf16[2,3,32,768]{3,2,1,0:T(8,128)(2,1)S(1)}, bf16[2,3,32,768]{3,2,1,0:T(8,128)(2,1)S(1)}, u32[]{:S(2)}, u32[]{:S(2)}) %collective-permute-start.11) | collective-permute-done | bytes 294944 | tf_op jit(solution)/shard_map/ppermute | solution.py:274
  156.5 4.4 %collective-permute-start.13 = (bf16[3,32,768]{2,1,0:T(8,128)(2,1)S(1)}, bf16[3,32,768]{2,1,0:T(8,128)(2,1)S(1)}, u32[]{:S(2)}, u32[]{:S(2)}) collective-permute-start(bf16[3,32,768]{2,1,0:T(8,128)(2,1)S(1)} %fusion.2), channel_id=1, source_target_pairs={{0,256},{256,0},{1,257},{257,1},{2,258},{258,2},{3,259},{259,3},{4... | collective-permute-start | bytes 442376 | tf_op jit(solution)/shard_map/ppermute | solution.py:269
  161.0 10.1 %collective-permute-done.13 = bf16[3,32,768]{2,1,0:T(8,128)(2,1)S(1)} collective-permute-done((bf16[3,32,768]{2,1,0:T(8,128)(2,1)S(1)}, bf16[3,32,768]{2,1,0:T(8,128)(2,1)S(1)}, u32[]{:S(2)}, u32[]{:S(2)}) %collective-permute-start.13) | collective-permute-done | bytes 147488 | tf_op jit(solution)/shard_map/ppermute | solution.py:269
  (54 shorter events, 9.4 us)
Async XLA Ops:
  4.6 19.5 %copy-start.11 = (bf16[1,128,768]{2,1,0:T(8,128)(2,1)S(1)}, bf16[1,128,768]{2,1,0:T(8,128)(2,1)}, u32[]{:S(2)}) copy-start(bf16[1,128,768]{2,1,0:T(8,128)(2,1)} %param.14) | copy-start | bytes 589828
  4.6 93.8 %all-to-all-start = ((bf16[64,112,128]{2,1,0:T(8,128)(2,1)}), bf16[64,112,128]{2,1,0:T(8,128)(2,1)S(1)}, u32[]{:S(2)}, u32[]{:S(2)}) async-start(bf16[64,112,128]{2,1,0:T(8,128)(2,1)} %bitcast.25), calls=%async_computation | async-start | bytes 3670016 | tf_op jit(solution)/shard_map/all_to_all | solution.py:279
  19.3 38.5 %collective-permute-start.4 = (bf16[128,1792]{1,0:T(8,128)(2,1)S(1)}, bf16[128,1792]{1,0:T(8,128)(2,1)S(1)}, u32[]{:S(2)}, u32[]{:S(2)}) collective-permute-start(bf16[128,1792]{1,0:T(8,128)(2,1)S(1)} %pad_maximum_fusion.1), channel_id=1, source_target_pairs={{0,256},{256,0},{1,257},{257,1},{2,258},{258,2},{3,259},{259,3},{4... | collective-permute-start | bytes 1376264 | tf_op jit(solution)/shard_map/ppermute | solution.py:269
  24.1 38.0 %collective-permute-start.5 = (bf16[128,768]{1,0:T(8,128)(2,1)S(1)}, bf16[128,768]{1,0:T(8,128)(2,1)S(1)}, u32[]{:S(2)}, u32[]{:S(2)}) collective-permute-start(bf16[128,768]{1,0:T(8,128)(2,1)S(1)} %bitcast.34), channel_id=1, source_target_pairs={{0,256},{256,0},{1,257},{257,1},{2,258},{258,2},{3,259},{259,3},{4... | collective-permute-start | bytes 589832 | tf_op jit(solution)/shard_map/ppermute | solution.py:269
  28.6 44.5 %copy-start.1 = (bf16[128,2560]{1,0:T(8,128)(2,1)}, bf16[128,2560]{1,0:T(8,128)(2,1)S(1)}, u32[]{:S(2)}) copy-start(bf16[128,2560]{1,0:T(8,128)(2,1)S(1)} %pad_maximum_fusion.refs_5_) | copy-start | bytes 1966084
  28.6 39.8 %collective-permute-start.1 = (bf16[128,2560]{1,0:T(8,128)(2,1)S(1)}, bf16[128,2560]{1,0:T(8,128)(2,1)S(1)}, u32[]{:S(2)}, u32[]{:S(2)}) collective-permute-start(bf16[128,2560]{1,0:T(8,128)(2,1)S(1)} %pad_maximum_fusion.refs_5_), channel_id=1, source_target_pairs={{0,192},{64,0},{128,64},{192,128},{1,193},{65,1},{129,65},{193,129... | collective-permute-start | bytes 1966088 | tf_op jit(solution)/shard_map/ppermute | solution.py:274
  33.0 40.1 %collective-permute-start = (bf16[128,2560]{1,0:T(8,128)(2,1)S(1)}, bf16[128,2560]{1,0:T(8,128)(2,1)S(1)}, u32[]{:S(2)}, u32[]{:S(2)}) collective-permute-start(bf16[128,2560]{1,0:T(8,128)(2,1)S(1)} %pad_maximum_fusion.refs_5_), channel_id=1, source_target_pairs={{0,64},{64,128},{128,192},{192,0},{1,65},{65,129},{129,193},{193,1... | collective-permute-start | bytes 1966088 | tf_op jit(solution)/shard_map/ppermute | solution.py:274
  62.1 24.0 %copy-start.2 = (bf16[128,2560]{1,0:T(8,128)(2,1)}, bf16[128,2560]{1,0:T(8,128)(2,1)S(1)}, u32[]{:S(2)}) copy-start(bf16[128,2560]{1,0:T(8,128)(2,1)S(1)} %constant_dynamic-update-slice_fusion.refs_10_) | copy-start | bytes 1966084
  62.1 17.8 %collective-permute-start.7 = (bf16[128,2560]{1,0:T(8,128)(2,1)S(1)}, bf16[128,2560]{1,0:T(8,128)(2,1)S(1)}, u32[]{:S(2)}, u32[]{:S(2)}) collective-permute-start(bf16[128,2560]{1,0:T(8,128)(2,1)S(1)} %constant_dynamic-update-slice_fusion.refs_10_), channel_id=1, source_target_pairs={{0,192},{64,0},{128,64},{192,128},{1,193},{65,1},{129,65},{193,129... | collective-permute-start | bytes 1966088 | tf_op jit(solution)/shard_map/ppermute | solution.py:274
  66.5 18.7 %collective-permute-start.6 = (bf16[128,2560]{1,0:T(8,128)(2,1)S(1)}, bf16[128,2560]{1,0:T(8,128)(2,1)S(1)}, u32[]{:S(2)}, u32[]{:S(2)}) collective-permute-start(bf16[128,2560]{1,0:T(8,128)(2,1)S(1)} %constant_dynamic-update-slice_fusion.refs_10_), channel_id=1, source_target_pairs={{0,64},{64,128},{128,192},{192,0},{1,65},{65,129},{129,193},{193,1... | collective-permute-start | bytes 1966088 | tf_op jit(solution)/shard_map/ppermute | solution.py:274
  68.5 23.8 %collective-permute-start.3 = (bf16[64,2560]{1,0:T(8,128)(2,1)S(1)}, bf16[64,2560]{1,0:T(8,128)(2,1)}, u32[]{:S(2)}, u32[]{:S(2)}) collective-permute-start(bf16[64,2560]{1,0:T(8,128)(2,1)S(1)} %slice.26), channel_id=1, source_target_pairs={{0,192},{64,0},{128,64},{192,128},{1,193},{65,1},{129,65},{193,129... | collective-permute-start | bytes 983048 | tf_op jit(solution)/shard_map/ppermute | solution.py:274
  73.1 18.5 %copy-start.4 = (bf16[128,2560]{1,0:T(8,128)(2,1)}, bf16[128,2560]{1,0:T(8,128)(2,1)S(1)}, u32[]{:S(2)}) copy-start(bf16[128,2560]{1,0:T(8,128)(2,1)S(1)} %collective-permute-done.refs_6_) | copy-start | bytes 1966084
  73.1 19.1 %collective-permute-start.2 = (bf16[64,2560]{1,0:T(8,128)(2,1)S(1)}, bf16[64,2560]{1,0:T(8,128)(2,1)}, u32[]{:S(2)}, u32[]{:S(2)}) collective-permute-start(bf16[64,2560]{1,0:T(8,128)(2,1)S(1)} %slice.25), channel_id=1, source_target_pairs={{0,64},{64,128},{128,192},{192,0},{1,65},{65,129},{129,193},{193,1... | collective-permute-start | bytes 983048 | tf_op jit(solution)/shard_map/ppermute | solution.py:274
  79.9 14.0 %collective-permute-start.9 = (bf16[64,2560]{1,0:T(8,128)(2,1)S(1)}, bf16[64,2560]{1,0:T(8,128)(2,1)}, u32[]{:S(2)}, u32[]{:S(2)}) collective-permute-start(bf16[64,2560]{1,0:T(8,128)(2,1)S(1)} %slice.28), channel_id=1, source_target_pairs={{0,192},{64,0},{128,64},{192,128},{1,193},{65,1},{129,65},{193,129... | collective-permute-start | bytes 983048 | tf_op jit(solution)/shard_map/ppermute | solution.py:274
  86.1 12.3 %collective-permute-start.8 = (bf16[64,2560]{1,0:T(8,128)(2,1)}, bf16[64,2560]{1,0:T(8,128)(2,1)}, u32[]{:S(2)}, u32[]{:S(2)}) collective-permute-start(bf16[64,2560]{1,0:T(8,128)(2,1)} %slice.27), channel_id=1, source_target_pairs={{0,64},{64,128},{128,192},{192,0},{1,65},{65,129},{129,193},{193,1... | collective-permute-start | bytes 983048 | tf_op jit(solution)/shard_map/ppermute | solution.py:274
  106.6 31.1 %copy-start.14 = (bf16[2,3,32,768]{3,2,1,0:T(8,128)(2,1)S(1)}, bf16[2,3,32,768]{3,2,1,0:T(8,128)(2,1)}, u32[]{:S(2)}) copy-start(bf16[2,3,32,768]{3,2,1,0:T(8,128)(2,1)} %get-tuple-element.19) | copy-start | bytes 884740
  106.6 33.0 %copy-start.13 = (bf16[2,3,32,768]{3,2,1,0:T(8,128)(2,1)S(1)}, bf16[2,3,32,768]{3,2,1,0:T(8,128)(2,1)}, u32[]{:S(2)}) copy-start(bf16[2,3,32,768]{3,2,1,0:T(8,128)(2,1)} %get-tuple-element.20) | copy-start | bytes 884740
  106.6 35.0 %copy-start.12 = (bf16[2,3,32,768]{3,2,1,0:T(8,128)(2,1)S(1)}, bf16[2,3,32,768]{3,2,1,0:T(8,128)(2,1)}, u32[]{:S(2)}) copy-start(bf16[2,3,32,768]{3,2,1,0:T(8,128)(2,1)} %get-tuple-element.21) | copy-start | bytes 884740
  106.6 49.7 %copy-start.9 = (bf16[2,3,32,768]{3,2,1,0:T(8,128)(2,1)S(1)}, bf16[2,3,32,768]{3,2,1,0:T(8,128)(2,1)}, u32[]{:S(2)}) copy-start(bf16[2,3,32,768]{3,2,1,0:T(8,128)(2,1)} %get-tuple-element.18) | copy-start | bytes 884740
  106.6 65.2 %all-to-all-start.1 = ((bf16[64,56,128]{2,1,0:T(8,128)(2,1)}), bf16[64,56,128]{2,1,0:T(8,128)(2,1)S(1)}, u32[]{:S(2)}, u32[]{:S(2)}) async-start(bf16[64,56,128]{2,1,0:T(8,128)(2,1)} %bitcast.27), calls=%async_computation.1 | async-start | bytes 1835008 | tf_op jit(solution)/shard_map/all_to_all | solution.py:279
  137.7 11.6 %collective-permute-start.10 = (bf16[2,3,32,768]{3,2,1,0:T(8,128)(2,1)S(1)}, bf16[2,3,32,768]{3,2,1,0:T(8,128)(2,1)S(1)}, u32[]{:S(2)}, u32[]{:S(2)}) collective-permute-start(bf16[2,3,32,768]{3,2,1,0:T(8,128)(2,1)S(1)} %copy-done.14), channel_id=1, source_target_pairs={{0,128},{64,192},{128,0},{192,64},{1,129},{65,193},{129,1},{193,65... | collective-permute-start | bytes 884744 | tf_op jit(solution)/shard_map/ppermute | solution.py:274
  139.6 16.7 %collective-permute-start.11 = (bf16[2,3,32,768]{3,2,1,0:T(8,128)(2,1)S(1)}, bf16[2,3,32,768]{3,2,1,0:T(8,128)(2,1)S(1)}, u32[]{:S(2)}, u32[]{:S(2)}) collective-permute-start(bf16[2,3,32,768]{3,2,1,0:T(8,128)(2,1)S(1)} %copy-done.13), channel_id=1, source_target_pairs={{0,64},{64,128},{128,192},{192,0},{1,65},{65,129},{129,193},{193,1... | collective-permute-start | bytes 884744 | tf_op jit(solution)/shard_map/ppermute | solution.py:274
  141.5 14.8 %collective-permute-start.12 = (bf16[2,3,32,768]{3,2,1,0:T(8,128)(2,1)S(1)}, bf16[2,3,32,768]{3,2,1,0:T(8,128)(2,1)S(1)}, u32[]{:S(2)}, u32[]{:S(2)}) collective-permute-start(bf16[2,3,32,768]{3,2,1,0:T(8,128)(2,1)S(1)} %copy-done.12), channel_id=1, source_target_pairs={{0,192},{64,0},{128,64},{192,128},{1,193},{65,1},{129,65},{193,129... | collective-permute-start | bytes 884744 | tf_op jit(solution)/shard_map/ppermute | solution.py:274
  156.5 14.6 %collective-permute-start.13 = (bf16[3,32,768]{2,1,0:T(8,128)(2,1)S(1)}, bf16[3,32,768]{2,1,0:T(8,128)(2,1)S(1)}, u32[]{:S(2)}, u32[]{:S(2)}) collective-permute-start(bf16[3,32,768]{2,1,0:T(8,128)(2,1)S(1)} %fusion.2), channel_id=1, source_target_pairs={{0,256},{256,0},{1,257},{257,1},{2,258},{258,2},{3,259},{259,3},{4... | collective-permute-start | bytes 442376 | tf_op jit(solution)/shard_map/ppermute | solution.py:269
  (7 other events, 88.1 us)
